TPU v7x, 256 devices: a whole 4x4x8 slice. The times are simulated.
256 devices in a mesh: dp: 32 (over z, y), chan: 8 (over x, core).
Axes of the slice: x: 4, y: 4, z: 8, core: 2. Of those that a mesh axis runs over, the one named last changes fastest.
Arguments:
- activations: bfloat16 [32, 16, 64, 1024], P('dp', None, None, 'chan'), may hold values from -60 to 60
- cotangent: bfloat16 [32, 16, 64, 1024], P('dp', None, None, 'chan'), may hold values from -6 to 6
- dw_kernel: float32 [49, 1024], P(None, 'chan'), may hold values from -0.875 to 0.875
- norm_gain: float32 [4, 1024], P(None, 'chan'), may hold values from 0.1 to 1.9
- norm_bias: float32 [4, 1024], P(None, 'chan'), may hold values from -3 to 3
- w_in: bfloat16 [1024, 4096], P(None, 'chan'), may hold values from -0.1875 to 0.1875
- b_in: float32 [4096], P('chan'), may hold values from -3 to 3
- w_out: bfloat16 [4096, 1024], P('chan'), may hold values from -0.09375 to 0.09375
- layer_scale: float32 [1024], P('chan'), may hold values from 0.3 to 1.5
- group_sizes: int32 [4], replicated, may hold values from 1 to 16, 32 in all
Outputs:
- result: bfloat16 [32, 16, 64, 1024], P('dp', None, None, 'chan')
- d_input: bfloat16 [32, 16, 64, 1024], P('dp', None, None, 'chan')
- d_kernel: float32 [49, 1024], P(None, 'chan')
- d_gain: float32 [4, 1024], P(None, 'chan')
- d_bias: float32 [4, 1024], P(None, 'chan')
- d_w_in: float32 [1024, 4096], P('dp', 'chan')
- d_b_in: float32 [4096], P('chan')
- d_w_out: float32 [4096, 1024], P('chan', 'dp')
- d_scale: float32 [1024], P('chan')
Inputs may be any that keep to these rules, and one draw needn't show every extreme that they name: `group_sizes`: the sizes sum to 32, each is at least one, and the largest is exactly 16.
All inputs are finite; a program needn't handle non-finite values.
Results may differ from a plain program's by a relative error of at most 0.015.
Values may be sent and summed in bfloat16 or wider, within the bound.
No kernel may reach another device: no remote copies, remote signals or barrier semaphores. Data moves between devices by JAX's collectives and lax.ppermute only.
A program may use at most 128 MiB of HBM per device.

v0:
```python
import jax
import jax.numpy as jnp
from jax import lax
from jax.sharding import Mesh
from jax.sharding import PartitionSpec as P

KS = 7
DP = ("dp_0", "dp_1")


EPS = 1e-05


def sent_to_all(array, axis):
    size = lax.axis_size(axis)
    return lax.all_to_all(
        jnp.broadcast_to(array[None], (size, *array.shape)), axis, 0, 0, tiled=True
    )


def in_order(pieces, dim):
    pieces = jnp.moveaxis(pieces, 0, dim)
    shape = pieces.shape
    return pieces.reshape(*shape[:dim], shape[dim] * shape[dim + 1], *shape[dim + 2 :])


def gather_directly(array, axis, dim):
    pieces = sent_to_all(array, axis)
    return in_order(pieces, dim)


def cut_along(array, dim, size):
    shape = array.shape
    pieces = array.reshape(*shape[:dim], size, shape[dim] // size, *shape[dim + 1 :])
    return jnp.moveaxis(pieces, dim, 0)


def summed_on_arrival(array, axis, dim):
    size = lax.axis_size(axis)
    pieces = lax.all_to_all(cut_along(array, dim, size), axis, 0, 0, tiled=True)
    return jnp.sum(pieces.astype(jnp.float32), axis=0)


def summed_rows(array, axes, dim):
    if not axes:
        return array
    nearer = lax.psum_scatter(array, axes[0], scatter_dimension=dim, tiled=True)
    return summed_rows(nearer, axes[1:], dim)


def over_copies(array, axis):
    everything = sent_to_all(array, axis)
    return jnp.sum(everything, axis=0)


def packed_total(arrays, axis):
    ends = [0]
    for a in arrays:
        ends.append(ends[-1] + a.size)
    total = over_copies(jnp.concatenate([a.ravel() for a in arrays]), axis)
    return tuple((total[b:e].reshape(a.shape) for a, b, e in zip(arrays, ends, ends[1:])))


def depthwise(field, kernel):
    reach = KS // 2
    height, width = (field.shape[1], field.shape[2])
    padded = jnp.pad(field, ((0, 0), (reach, reach), (reach, reach), (0, 0)))
    running = jnp.zeros(field.shape, jnp.float32)
    for shift_row in range(KS):
        for shift_col in range(KS):
            window = padded[:, shift_row : shift_row + height, shift_col : shift_col + width, :]
            running = running + window * kernel[shift_row * KS + shift_col]
    return running


def kernel_grad(field, upstream):
    reach = KS // 2
    height, width = (field.shape[1], field.shape[2])
    padded = jnp.pad(field, ((0, 0), (reach, reach), (reach, reach), (0, 0)))
    collected = []
    for shift_row in range(KS):
        for shift_col in range(KS):
            window = padded[:, shift_row : shift_row + height, shift_col : shift_col + width, :]
            collected.append(jnp.sum(window * upstream, axis=(0, 1, 2)))
    return jnp.stack(collected)


def group_owners(group_sizes, number):
    group_ends = jnp.cumsum(group_sizes)
    positions = jnp.arange(number, dtype=jnp.int32)
    labels = jnp.sum((group_ends[None, :] <= positions[:, None]).astype(jnp.int32), axis=1)
    return (jnp.arange(group_sizes.shape[0], dtype=jnp.int32)[:, None] == labels[None, :]).astype(
        jnp.float32
    )


def body(
    activations,
    cotangent,
    dw_kernel,
    norm_gain,
    norm_bias,
    w_in,
    b_in,
    w_out,
    layer_scale,
    group_sizes,
):
    height, width, channels = (activations.shape[1], activations.shape[2], activations.shape[3])
    row_count = height * width
    devices = lax.axis_size(DP)
    position = lax.axis_index(DP)
    group_ends = jnp.cumsum(group_sizes)
    own_group = jnp.sum((group_ends <= position).astype(jnp.int32))
    member = (jnp.arange(group_sizes.shape[0], dtype=jnp.int32) == own_group).astype(jnp.float32)
    counts = group_sizes.astype(jnp.float32) * row_count
    own_count = jnp.sum(member * counts)
    source = activations.astype(jnp.float32)
    filtered = depthwise(source, dw_kernel).reshape(row_count, channels)
    moments = jnp.stack([jnp.sum(filtered, axis=0), jnp.sum(filtered * filtered, axis=0)])
    per_device = gather_directly(moments[None], DP, 0)
    owners = group_owners(group_sizes, devices)
    totals = jnp.sum(owners[:, :, None, None] * per_device[None], axis=1)
    group_mean = totals[:, 0] / counts[:, None]
    group_var = totals[:, 1] / counts[:, None] - group_mean * group_mean
    group_rstd = lax.rsqrt(group_var + EPS)
    own_mean = jnp.sum(member[:, None] * group_mean, axis=0)
    own_rstd = jnp.sum(member[:, None] * group_rstd, axis=0)
    own_gain = jnp.sum(member[:, None] * norm_gain, axis=0)
    own_bias = jnp.sum(member[:, None] * norm_bias, axis=0)
    centered = (filtered - own_mean) * own_rstd
    normed = (centered * own_gain + own_bias).astype(jnp.bfloat16)
    gathered = gather_directly(normed, "chan", 1)
    hidden = jnp.dot(gathered, w_in, preferred_element_type=jnp.float32) + b_in
    activated = jax.nn.gelu(hidden).astype(jnp.bfloat16)
    partial_branch = jnp.dot(activated, w_out, preferred_element_type=jnp.float32)
    branch = summed_on_arrival(partial_branch.astype(jnp.bfloat16), "chan", 1)
    initial = source.reshape(row_count, channels)
    result = (initial + layer_scale * branch).astype(jnp.bfloat16).reshape(activations.shape)
    incoming = cotangent.reshape(row_count, channels).astype(jnp.float32)
    scale_local = jnp.sum(incoming * branch, axis=0)
    d_branch = (incoming * layer_scale).astype(jnp.bfloat16)
    branch_full = gather_directly(d_branch, "chan", 1)
    contract_rows = (((0,), (0,)), ((), ()))
    contract_cols = (((1,), (1,)), ((), ()))
    out_local_t = lax.dot_general(
        branch_full, activated, contract_rows, preferred_element_type=jnp.float32
    )
    d_activated = lax.dot_general(
        branch_full, w_out, contract_cols, preferred_element_type=jnp.float32
    )
    _, pullback = jax.vjp(jax.nn.gelu, hidden)
    d_hidden = pullback(d_activated)[0]
    bias_local = jnp.sum(d_hidden, axis=0)
    hidden_b = d_hidden.astype(jnp.bfloat16)
    in_local = lax.dot_general(
        gathered, hidden_b, contract_rows, preferred_element_type=jnp.float32
    )
    hidden_cols = in_local.shape[1]
    both_local = jnp.concatenate([in_local, out_local_t], axis=1)
    both_sums = summed_rows(both_local.astype(jnp.bfloat16), DP, 0).astype(jnp.float32)
    d_w_in = both_sums[:, :hidden_cols]
    d_w_out = both_sums[:, hidden_cols:].T
    partial_normed = lax.dot_general(
        hidden_b, w_in, contract_cols, preferred_element_type=jnp.float32
    )
    d_normed = summed_on_arrival(partial_normed.astype(jnp.bfloat16), "chan", 1)
    grad_moments = jnp.stack([jnp.sum(d_normed * centered, axis=0), jnp.sum(d_normed, axis=0)])
    grad_rows = gather_directly(grad_moments[None], DP, 0)
    grad_owners = group_owners(group_sizes, devices)
    grad_totals = jnp.sum(grad_owners[:, :, None, None] * grad_rows[None], axis=1)
    d_gain = grad_totals[:, 0]
    d_bias = grad_totals[:, 1]
    own_dgain = jnp.sum(member[:, None] * d_gain, axis=0)
    own_dbias = jnp.sum(member[:, None] * d_bias, axis=0)
    d_filtered = (
        own_gain * own_rstd * (d_normed - own_dbias / own_count - centered * own_dgain / own_count)
    )
    d_filtered = d_filtered.reshape(activations.shape)
    kernel_local = kernel_grad(source, d_filtered)
    d_kernel, d_b_in, d_scale = packed_total((kernel_local, bias_local, scale_local), DP)
    d_input = (cotangent.astype(jnp.float32) + depthwise(d_filtered, dw_kernel[::-1])).astype(
        jnp.bfloat16
    )
    return (result, d_input, d_kernel, d_gain, d_bias, d_w_in, d_b_in, d_w_out, d_scale)


def solution(mesh):
    split = Mesh(mesh.devices.reshape(8, 4, mesh.shape["chan"]), ("dp_0", "dp_1", "chan"))
    in_specs = (
        P(DP, None, None, "chan"),
        P(DP, None, None, "chan"),
        P(None, "chan"),
        P(None, "chan"),
        P(None, "chan"),
        P(None, "chan"),
        P("chan"),
        P("chan", None),
        P("chan"),
        P(),
    )
    out_specs = (
        P(DP, None, None, "chan"),
        P(DP, None, None, "chan"),
        P(None, "chan"),
        P(None, "chan"),
        P(None, "chan"),
        P(DP, "chan"),
        P("chan"),
        P("chan", DP),
        P("chan"),
    )
    return jax.shard_map(body, mesh=split, in_specs=in_specs, out_specs=out_specs, check_vma=False)
```

profile of v0, /device:TPU:4, one launch (start us, length us, event | category | flops | bytes accessed | tf_op | source)
XLA Modules:
  0.0 238.3 jit_solution(1071786961160653208)
XLA Ops:
  11.4 4.4 %fusion.110 = (f32[128]{0:T(128)S(1)}, f32[128]{0:T(128)S(1)}, f32[1,16,64,128]{3,2,1,0:T(8,128)S(1)}) fusion(f32[128]{0:T(128)S(1)} %get-tuple-element.174, f32[128]{0:T(128)S(1)} %get-tuple-element.175, f32[128]{0:T(128)S(1)} %get-tuple-element.128, f32[128]{0:T(128)S(1)} %get-tuple-element.129, f32[128]{0:T(128)S(1)} %get-tuple-element.130, ...), kind=kLoop, calls=%fused_computation.347 | loop fusion | flops 13106944 | bytes 1074688 | tf_op jit(solution)/shard_map/reduce_sum | solution.py:120
  16.5 11.5 %all-to-all-start = ((f32[32,1,2,128]{3,2,1,0:T(2,128)}), f32[32,1,2,128]{3,2,1,0:T(2,128)S(1)}, u32[]{:S(2)}, u32[]{:S(2)}) async-start(f32[32,1,2,128]{3,2,1,0:T(2,128)} %broadcast_in_dim.10), calls=%async_computation | async-start | bytes 65536 | tf_op jit(solution)/shard_map/all_to_all | solution.py:16
  31.2 6.6 %all-to-all-done = f32[32,1,2,128]{3,2,1,0:T(2,128)S(1)} async-done(((f32[32,1,2,128]{3,2,1,0:T(2,128)}), f32[32,1,2,128]{3,2,1,0:T(2,128)S(1)}, u32[]{:S(2)}, u32[]{:S(2)}) %all-to-all-start) | async-done | bytes 32800 | tf_op jit(solution)/shard_map/all_to_all | solution.py:16
  39.8 4.9 %all-to-all-start.1 = ((bf16[8,1024,128]{1,2,0:T(8,128)(2,1)}), bf16[8,1024,128]{1,2,0:T(8,128)(2,1)}, u32[]{:S(2)}, u32[]{:S(2)}) async-start(bf16[8,1024,128]{1,2,0:T(8,128)(2,1)} %broadcast_in_dim.11), calls=%async_computation.1 | async-start | bytes 4194304 | tf_op jit(solution)/shard_map/all_to_all | solution.py:16
  45.0 23.9 %all-to-all-done.1 = bf16[8,1024,128]{1,2,0:T(8,128)(2,1)} async-done(((bf16[8,1024,128]{1,2,0:T(8,128)(2,1)}), bf16[8,1024,128]{1,2,0:T(8,128)(2,1)}, u32[]{:S(2)}, u32[]{:S(2)}) %all-to-all-start.1) | async-done | bytes 2097184 | tf_op jit(solution)/shard_map/all_to_all | solution.py:16
  70.4 7.4 %all-to-all-start.3 = ((bf16[8,1024,128]{1,2,0:T(8,128)(2,1)}), bf16[8,1024,128]{1,2,0:T(8,128)(2,1)}, u32[]{:S(2)}, u32[]{:S(2)}) async-start(bf16[8,1024,128]{1,2,0:T(8,128)(2,1)} %broadcast_in_dim.12), calls=%async_computation.3 | async-start | bytes 4194304 | tf_op jit(solution)/shard_map/all_to_all | solution.py:16
  77.8 3.2 %fusion.115 = f32[1024,512]{1,0:T(8,128)S(1)} fusion(bf16[1024,1024]{0,1:T(8,128)(2,1)} %bitcast.58, bf16[1024,512]{1,0:T(8,128)(2,1)} %param.15), kind=kOutput, calls=%fused_computation.351 | convolution fusion | flops 1073741824 | bytes 5242880 | tf_op jit(solution)/shard_map/dot_general | solution.py:134
  85.1 16.9 %all-to-all-done.3 = bf16[8,1024,128]{1,2,0:T(8,128)(2,1)} async-done(((bf16[8,1024,128]{1,2,0:T(8,128)(2,1)}), bf16[8,1024,128]{1,2,0:T(8,128)(2,1)}, u32[]{:S(2)}, u32[]{:S(2)}) %all-to-all-start.3) | async-done | bytes 2097184 | tf_op jit(solution)/shard_map/all_to_all | solution.py:16
  101.9 7.4 %all-to-all-start.2 = ((bf16[8,1024,128]{1,2,0:T(8,128)(2,1)}), bf16[8,1024,128]{1,2,0:T(8,128)(2,1)}, u32[]{:S(2)}, u32[]{:S(2)}) async-start(bf16[8,1024,128]{1,2,0:T(8,128)(2,1)} %bitcast.209), calls=%async_computation.2 | async-start | bytes 4194304 | tf_op jit(solution)/shard_map/all_to_all | solution.py:40
  109.4 5.5 %fusion.111 = (f32[512]{0:T(512)}, bf16[1024,512]{1,0:T(8,128)(2,1)S(1)}) fusion(f32[1024,512]{1,0:T(8,128)} %copy-done.76, f32[512]{0:T(512)S(1)} %copy-done.75, bf16[1024,1024]{0,1:T(8,128)(2,1)} %bitcast.64, bf16[512,1024]{1,0:T(8,128)(2,1)S(1)} %copy-done), kind=kOutput, calls=%fused_computation.348 | convolution fusion | flops 1085275648 | bytes 6295552 | tf_op jit(solution)/shard_map/dot_general | solution.py:149
  118.6 14.9 %all-to-all-done.2 = bf16[8,1024,128]{1,2,0:T(8,128)(2,1)} async-done(((bf16[8,1024,128]{1,2,0:T(8,128)(2,1)}), bf16[8,1024,128]{1,2,0:T(8,128)(2,1)}, u32[]{:S(2)}, u32[]{:S(2)}) %all-to-all-start.2) | async-done | bytes 2097184 | tf_op jit(solution)/shard_map/all_to_all | solution.py:40
  133.5 7.4 %all-to-all-start.4 = ((bf16[8,1024,128]{1,2,0:T(8,128)(2,1)}), bf16[8,1024,128]{1,2,0:T(8,128)(2,1)}, u32[]{:S(2)}, u32[]{:S(2)}) async-start(bf16[8,1024,128]{1,2,0:T(8,128)(2,1)} %bitcast.208), calls=%async_computation.4 | async-start | bytes 4194304 | tf_op jit(solution)/shard_map/all_to_all | solution.py:40
  140.9 3.3 %convolution_convert_fusion.3 = bf16[1024,512]{0,1:T(8,128)(2,1)S(1)} fusion(bf16[1024,1024]{0,1:T(8,128)(2,1)} %bitcast.58, bf16[1024,512]{1,0:T(8,128)(2,1)} %copy-done.78), kind=kOutput, calls=%fused_computation.112 | convolution fusion | flops 1074266112 | bytes 4194304 | tf_op jit(solution)/shard_map/dot_general | solution.py:156
  144.2 3.0 %convolution_convert_fusion.2 = bf16[1024,512]{0,1:T(8,128)(2,1)S(1)} fusion(bf16[1024,1024]{0,1:T(8,128)(2,1)} %bitcast.64, f32[1024,512]{1,0:T(8,128)S(1)} %copy-done.77, f32[512]{0:T(512)S(1)} %copy-done.75), kind=kOutput, calls=%fused_computation.111 | convolution fusion | flops 1079508992 | bytes 5244928 | tf_op jit(solution)/shard_map/dot_general | solution.py:146
  148.7 4.0 %copy.62 = bf16[1024,1024]{1,0:T(8,128)(2,1)} copy(bf16[1024,1024]{0,1:T(8,128)(2,1)} %pad_maximum_fusion) | data formatting | bytes 4194304
  155.4 9.6 %all-to-all-done.4 = bf16[8,1024,128]{1,2,0:T(8,128)(2,1)} async-done(((bf16[8,1024,128]{1,2,0:T(8,128)(2,1)}), bf16[8,1024,128]{1,2,0:T(8,128)(2,1)}, u32[]{:S(2)}, u32[]{:S(2)}) %all-to-all-start.4) | async-done | bytes 2097184 | tf_op jit(solution)/shard_map/all_to_all | solution.py:40
  165.0 2.9 %convert_reduce_fusion.1 = (f32[1024,128]{0,1:T(8,128)}, f32[128]{0:T(128)S(1)}) fusion(bf16[8,1024,128]{1,2,0:T(8,128)(2,1)} %all-to-all-done.4), kind=kLoop, calls=%fused_computation.97 | loop fusion | flops 3014528 | bytes 2621952 | tf_op jit(solution)/shard_map/reduce_sum | solution.py:41
  170.0 3.9 %all-to-all-start.5 = ((f32[32,1,2,128]{3,2,1,0:T(2,128)}), f32[32,1,2,128]{3,2,1,0:T(2,128)S(1)}, u32[]{:S(2)}, u32[]{:S(2)}) async-start(f32[32,1,2,128]{3,2,1,0:T(2,128)} %broadcast_in_dim.13), calls=%async_computation.5 | async-start | bytes 65536 | tf_op jit(solution)/shard_map/all_to_all | solution.py:16
  174.6 9.2 %all-to-all-done.5 = f32[32,1,2,128]{3,2,1,0:T(2,128)S(1)} async-done(((f32[32,1,2,128]{3,2,1,0:T(2,128)}), f32[32,1,2,128]{3,2,1,0:T(2,128)S(1)}, u32[]{:S(2)}, u32[]{:S(2)}) %all-to-all-start.5) | async-done | bytes 32800 | tf_op jit(solution)/shard_map/all_to_all | solution.py:16
  185.3 3.3 %multiply_reduce_fusion.1 = (f32[128]{0:T(128)}, f32[128]{0:T(128)}, f32[128]{0:T(128)}, f32[128]{0:T(128)}, f32[128]{0:T(128)}, /*index=5*/f32[128]{0:T(128)}, ...) fusion(f32[1,16,64,128]{3,2,1,0:T(8,128)S(1)} %convert_element_, ...), kind=kLoop, calls=%fused_computation.214 | loop fusion | flops 5633792 | bytes 2108932 | tf_op jit(solution)/shard_map/reduce_sum | solution.py:84
  195.6 3.9 %all-to-all-start.6 = ((f32[32,1,6912]{2,1,0:T(1,128)}), f32[32,1,6912]{2,1,0:T(1,128)S(1)}, u32[]{:S(2)}, u32[]{:S(2)}) async-start(f32[32,1,6912]{2,1,0:T(1,128)} %broadcast_in_dim.14), calls=%async_computation.6 | async-start | bytes 1769472 | tf_op jit(solution)/shard_map/all_to_all | solution.py:16
  200.5 5.1 %fusion.100 = bf16[1,16,64,128]{3,2,1,0:T(8,128)(2,1)} fusion(f32[1,16,64,128]{3,2,1,0:T(8,128)S(1)} %get-tuple-element.122, bf16[1,16,64,128]{3,2,1,0:T(8,128)(2,1)S(1)} %copy-done.2, f32[128]{0:T(128)S(1)} %get-tuple-element.174, f32[128]{0:T(128)S(1)} %get-tuple-element.175, f32[128]{0:T(128)S(1)} %get-tuple-element.128, f32[128]{0:T(128)S(1)} %get-tuple-element.129, ...), kind=kLoop, calls=%fused_computation.207 | loop fusion | flops 13107200 | bytes 1073664 | tf_op jit(solution)/shard_map/convert_element_type | solution.py:182
  205.6 18.2 %all-to-all-done.6 = f32[32,1,6912]{2,1,0:T(1,128)S(1)} async-done(((f32[32,1,6912]{2,1,0:T(1,128)}), f32[32,1,6912]{2,1,0:T(1,128)S(1)}, u32[]{:S(2)}, u32[]{:S(2)}) %all-to-all-start.6) | async-done | bytes 884768 | tf_op jit(solution)/shard_map/all_to_all | solution.py:16
  226.0 2.9 %reduce-scatter.9.cloned.1.call-done = bf16[32,1024]{1,0:T(8,128)(2,1)} async-done(((bf16[128,1024]{1,0:T(8,128)(2,1)}), bf16[32,1024]{1,0:T(8,128)(2,1)}) %reduce-scatter.9.cloned.1.call-update) | async-done | bytes 65552
  (216 shorter events, 39.8 us)
Async XLA Ops:
  7.2 75.1 %copy-start = (bf16[512,1024]{1,0:T(8,128)(2,1)S(1)}, bf16[512,1024]{1,0:T(8,128)(2,1)}, u32[]{:S(2)}) copy-start(bf16[512,1024]{1,0:T(8,128)(2,1)} %param.17) | copy-start | bytes 3145732
  7.2 20.8 %copy-start.73 = (s32[4]{0:T(128)S(1)}, s32[4]{0:T(128)}, u32[]{:S(2)}) copy-start(s32[4]{0:T(128)} %param.19) | copy-start | bytes 52
  7.2 30.7 %copy-start.56 = (f32[4,128]{1,0:T(4,128)S(1)}, f32[4,128]{1,0:T(4,128)}, u32[]{:S(2)}) copy-start(f32[4,128]{1,0:T(4,128)} %param.14) | copy-start | bytes 6148
  7.2 30.7 %copy-start.55 = (f32[4,128]{1,0:T(4,128)S(1)}, f32[4,128]{1,0:T(4,128)}, u32[]{:S(2)}) copy-start(f32[4,128]{1,0:T(4,128)} %param.13) | copy-start | bytes 6148
  9.2 21.0 %copy-start.6 = (f32[128]{0:T(128)}, f32[128]{0:T(128)S(1)}, u32[]{:S(2)}) copy-start(f32[128]{0:T(128)S(1)} %get-tuple-element.141) | copy-start | bytes 1540
  9.2 21.0 %copy-start.8 = (f32[128]{0:T(128)}, f32[128]{0:T(128)S(1)}, u32[]{:S(2)}) copy-start(f32[128]{0:T(128)S(1)} %get-tuple-element.142) | copy-start | bytes 1540
  9.2 20.9 %copy-start.10 = (f32[128]{0:T(128)}, f32[128]{0:T(128)S(1)}, u32[]{:S(2)}) copy-start(f32[128]{0:T(128)S(1)} %get-tuple-element.143) | copy-start | bytes 1540
  9.2 20.9 %copy-start.12 = (f32[128]{0:T(128)}, f32[128]{0:T(128)S(1)}, u32[]{:S(2)}) copy-start(f32[128]{0:T(128)S(1)} %get-tuple-element.144) | copy-start | bytes 1540
  9.2 20.9 %copy-start.14 = (f32[128]{0:T(128)}, f32[128]{0:T(128)S(1)}, u32[]{:S(2)}) copy-start(f32[128]{0:T(128)S(1)} %get-tuple-element.145) | copy-start | bytes 1540
  10.2 19.9 %copy-start.16 = (f32[128]{0:T(128)}, f32[128]{0:T(128)S(1)}, u32[]{:S(2)}) copy-start(f32[128]{0:T(128)S(1)} %get-tuple-element.146) | copy-start | bytes 1540
  10.2 19.9 %copy-start.18 = (f32[128]{0:T(128)}, f32[128]{0:T(128)S(1)}, u32[]{:S(2)}) copy-start(f32[128]{0:T(128)S(1)} %get-tuple-element.147) | copy-start | bytes 1540
  10.2 19.9 %copy-start.20 = (f32[128]{0:T(128)}, f32[128]{0:T(128)S(1)}, u32[]{:S(2)}) copy-start(f32[128]{0:T(128)S(1)} %get-tuple-element.148) | copy-start | bytes 1540
  10.2 19.9 %copy-start.22 = (f32[128]{0:T(128)}, f32[128]{0:T(128)S(1)}, u32[]{:S(2)}) copy-start(f32[128]{0:T(128)S(1)} %get-tuple-element.149) | copy-start | bytes 1540
  10.3 19.9 %copy-start.24 = (f32[128]{0:T(128)}, f32[128]{0:T(128)S(1)}, u32[]{:S(2)}) copy-start(f32[128]{0:T(128)S(1)} %get-tuple-element.150) | copy-start | bytes 1540
  10.3 19.9 %copy-start.26 = (f32[128]{0:T(128)}, f32[128]{0:T(128)S(1)}, u32[]{:S(2)}) copy-start(f32[128]{0:T(128)S(1)} %get-tuple-element.151) | copy-start | bytes 1540
  16.5 21.3 %all-to-all-start = ((f32[32,1,2,128]{3,2,1,0:T(2,128)}), f32[32,1,2,128]{3,2,1,0:T(2,128)S(1)}, u32[]{:S(2)}, u32[]{:S(2)}) async-start(f32[32,1,2,128]{3,2,1,0:T(2,128)} %broadcast_in_dim.10), calls=%async_computation | async-start | bytes 65536 | tf_op jit(solution)/shard_map/all_to_all | solution.py:16
  39.8 29.1 %all-to-all-start.1 = ((bf16[8,1024,128]{1,2,0:T(8,128)(2,1)}), bf16[8,1024,128]{1,2,0:T(8,128)(2,1)}, u32[]{:S(2)}, u32[]{:S(2)}) async-start(bf16[8,1024,128]{1,2,0:T(8,128)(2,1)} %broadcast_in_dim.11), calls=%async_computation.1 | async-start | bytes 4194304 | tf_op jit(solution)/shard_map/all_to_all | solution.py:16
  70.4 31.5 %all-to-all-start.3 = ((bf16[8,1024,128]{1,2,0:T(8,128)(2,1)}), bf16[8,1024,128]{1,2,0:T(8,128)(2,1)}, u32[]{:S(2)}, u32[]{:S(2)}) async-start(bf16[8,1024,128]{1,2,0:T(8,128)(2,1)} %broadcast_in_dim.12), calls=%async_computation.3 | async-start | bytes 4194304 | tf_op jit(solution)/shard_map/all_to_all | solution.py:16
  101.9 31.6 %all-to-all-start.2 = ((bf16[8,1024,128]{1,2,0:T(8,128)(2,1)}), bf16[8,1024,128]{1,2,0:T(8,128)(2,1)}, u32[]{:S(2)}, u32[]{:S(2)}) async-start(bf16[8,1024,128]{1,2,0:T(8,128)(2,1)} %bitcast.209), calls=%async_computation.2 | async-start | bytes 4194304 | tf_op jit(solution)/shard_map/all_to_all | solution.py:40
  133.5 31.5 %all-to-all-start.4 = ((bf16[8,1024,128]{1,2,0:T(8,128)(2,1)}), bf16[8,1024,128]{1,2,0:T(8,128)(2,1)}, u32[]{:S(2)}, u32[]{:S(2)}) async-start(bf16[8,1024,128]{1,2,0:T(8,128)(2,1)} %bitcast.208), calls=%async_computation.4 | async-start | bytes 4194304 | tf_op jit(solution)/shard_map/all_to_all | solution.py:40
  140.9 58.9 %reduce-scatter.7.cloned.1.call-start = ((), (), s32[]{:S(2)}) async-start(), calls=%async_computation.9 | async-start | bytes 2359296
  170.0 13.8 %all-to-all-start.5 = ((f32[32,1,2,128]{3,2,1,0:T(2,128)}), f32[32,1,2,128]{3,2,1,0:T(2,128)S(1)}, u32[]{:S(2)}, u32[]{:S(2)}) async-start(f32[32,1,2,128]{3,2,1,0:T(2,128)} %broadcast_in_dim.13), calls=%async_computation.5 | async-start | bytes 65536 | tf_op jit(solution)/shard_map/all_to_all | solution.py:16
  195.6 28.2 %all-to-all-start.6 = ((f32[32,1,6912]{2,1,0:T(1,128)}), f32[32,1,6912]{2,1,0:T(1,128)S(1)}, u32[]{:S(2)}, u32[]{:S(2)}) async-start(f32[32,1,6912]{2,1,0:T(1,128)} %broadcast_in_dim.14), calls=%async_computation.6 | async-start | bytes 1769472 | tf_op jit(solution)/shard_map/all_to_all | solution.py:16
  199.5 29.4 %reduce-scatter.9.cloned.1.call-start = ((), (), s32[]{:S(2)}) async-start(), calls=%async_computation.10 | async-start | bytes 327680
  (64 other events, 620.1 us)
Sparse Core Ops, SparseCore 0:
  152.8 37.5 reduce-scatter.6
  202.8 26.0 reduce-scatter.8
where the time goes:
time: 239 us; the launch traced here: 238 us
  waiting for transfers between devices  103 us (43%)
  starting transfers between devices  46.7 us (20%)
  other arithmetic  30.5 us (13%)
  local copies, waits for them, and re-layouts  22.7 us (9%)
  matrix products  20.4 us (9%)
  between operations  15.4 us (6%)
    all_to_all x5, waiting for transfers between devices, sent_to_all(): lax.all_to_all(jnp.broadcast_to(array[None], (size, *array.shape)), axis,...  74.7 us
    all_to_all x5, starting transfers between devices, sent_to_all(): lax.all_to_all(jnp.broadcast_to(array[None], (size, *array.shape)), axis,...  31.6 us
    all_to_all x2, waiting for transfers between devices, summed_on_arrival(): pieces = lax.all_to_all(cut_along(array, dim, size), axis, 0, 0, tiled=True)  24.5 us
    all_to_all x2, starting transfers between devices, summed_on_arrival(): pieces = lax.all_to_all(cut_along(array, dim, size), axis, 0, 0, tiled=True)  14.8 us
    unnamed x162, local copies, waits for them, and re-layouts  9.11 us
    reduce_sum x3, other arithmetic, kernel_grad(): collected.append(jnp.sum(window * upstream, axis=(0, 1, 2)))  6.92 us
    broadcast_in_dim x5, local copies, waits for them, and re-layouts, sent_to_all(): jnp.broadcast_to(array[None], (size, *array.shape))  5.77 us
    dot_general x1, matrix products, body(): lax.dot_general(branch_full, w_out, contract_cols, preferred_element_type...  5.49 us
  transfers between devices with their start and end apart: 9, of which 8 were waited for; matrix products, arithmetic and copies ran while one was open for 23% of the time, Pallas kernels for 0%

commit v1 on v0

v1 whole, which is shorter than its diff:
```python
import jax
import jax.numpy as jnp
from jax import lax
from jax.sharding import Mesh
from jax.sharding import PartitionSpec as P

KS = 7
DP = ("z", "y")
CH = ("x", "c")
SWAP = [(0, 1), (1, 0)]
EPS = 1e-05


def sent_to_all(array, axis):
    size = lax.axis_size(axis)
    return lax.all_to_all(
        jnp.broadcast_to(array[None], (size, *array.shape)), axis, 0, 0, tiled=True
    )


def packed_total(arrays, axis):
    ends = [0]
    for a in arrays:
        ends.append(ends[-1] + a.size)
    everything = sent_to_all(jnp.concatenate([a.ravel() for a in arrays]), axis)
    total = jnp.sum(everything, axis=0)
    return tuple((total[b:e].reshape(a.shape) for a, b, e in zip(arrays, ends, ends[1:])))


def depthwise(field, kernel):
    reach = KS // 2
    height, width = (field.shape[1], field.shape[2])
    padded = jnp.pad(field, ((0, 0), (reach, reach), (reach, reach), (0, 0)))
    running = jnp.zeros(field.shape, jnp.float32)
    for shift_row in range(KS):
        for shift_col in range(KS):
            window = padded[:, shift_row : shift_row + height, shift_col : shift_col + width, :]
            running = running + window * kernel[shift_row * KS + shift_col]
    return running


def kernel_grad(field, upstream):
    reach = KS // 2
    height, width = (field.shape[1], field.shape[2])
    padded = jnp.pad(field, ((0, 0), (reach, reach), (reach, reach), (0, 0)))
    collected = []
    for shift_row in range(KS):
        for shift_col in range(KS):
            window = padded[:, shift_row : shift_row + height, shift_col : shift_col + width, :]
            collected.append(jnp.sum(window * upstream, axis=(0, 1, 2)))
    return jnp.stack(collected)


def rows_of_all(array):
    rows, own = array.shape
    halves = jnp.broadcast_to(array.reshape(1, 2, rows // 2, own), (4, 2, rows // 2, own))
    pieces = lax.all_to_all(halves.reshape(8, rows // 2, own), CH, 0, 0, tiled=True)
    return jnp.moveaxis(pieces, 0, 1).reshape(rows // 2, 8 * own)


def summed_to_owner(array):
    rows, width = array.shape
    own = width // 8
    pieces = jnp.moveaxis(array.reshape(rows, 8, own), 1, 0)
    pieces = lax.all_to_all(pieces, CH, 0, 0, tiled=True).reshape(4, 2 * rows, own)
    return jnp.sum(pieces.astype(jnp.float32), axis=0)


def body(
    activations,
    cotangent,
    dw_kernel,
    norm_gain,
    norm_bias,
    w_in,
    b_in,
    w_out,
    layer_scale,
    group_sizes,
):
    height, width, channels = (activations.shape[1], activations.shape[2], activations.shape[3])
    row_count = height * width
    half = row_count // 2
    core = lax.axis_index("c")
    devices = lax.axis_size(DP)
    position = lax.axis_index(DP)
    groups = group_sizes.shape[0]
    group_ends = jnp.cumsum(group_sizes)
    positions = jnp.arange(devices, dtype=jnp.int32)
    labels = jnp.sum((group_ends[None, :] <= positions[:, None]).astype(jnp.int32), axis=1)
    own_group = jnp.sum((group_ends <= position).astype(jnp.int32))
    owners = (jnp.arange(groups, dtype=jnp.int32)[:, None] == labels[None, :]).astype(jnp.float32)
    mates = (labels == own_group).astype(jnp.float32)
    member = (jnp.arange(groups, dtype=jnp.int32) == own_group).astype(jnp.float32)
    own_count = jnp.sum(member * group_sizes.astype(jnp.float32)) * row_count
    own_gain = jnp.sum(member[:, None] * norm_gain, axis=0)
    own_bias = jnp.sum(member[:, None] * norm_bias, axis=0)

    incoming = cotangent.reshape(row_count, channels).astype(jnp.float32)
    d_branch = (incoming * layer_scale).astype(jnp.bfloat16)
    everyone = lax.all_gather(d_branch, CH, axis=0, tiled=False)
    mine = lax.dynamic_slice_in_dim(everyone, core * half, half, axis=1)
    branch_full = jnp.moveaxis(mine, 0, 1).reshape(half, 8 * channels)
    w_in_pair = lax.ppermute(w_in, "c", SWAP)
    w_out_pair = lax.ppermute(w_out, "c", SWAP)
    b_in_pair = lax.ppermute(b_in, "c", SWAP)

    source = activations.astype(jnp.float32)
    filtered = depthwise(source, dw_kernel).reshape(row_count, channels)
    moments = jnp.stack([jnp.sum(filtered, axis=0), jnp.sum(filtered * filtered, axis=0)])
    per_device = sent_to_all(moments, DP)
    totals = jnp.sum(mates[:, None, None] * per_device, axis=0)
    own_mean = totals[0] / own_count
    own_var = totals[1] / own_count - own_mean * own_mean
    own_rstd = lax.rsqrt(own_var + EPS)
    centered = (filtered - own_mean) * own_rstd
    normed = (centered * own_gain + own_bias).astype(jnp.bfloat16)
    gathered = rows_of_all(normed)

    contract_rows = (((0,), (0,)), ((), ()))
    contract_cols = (((1,), (1,)), ((), ()))

    def dot(a, b, dims):
        return lax.dot_general(a, b, dims, preferred_element_type=jnp.float32)

    def forward(weights, bias):
        hidden = jnp.dot(gathered, weights, preferred_element_type=jnp.float32) + bias
        return hidden, jax.nn.gelu(hidden).astype(jnp.bfloat16)

    hidden_own, active_own = forward(w_in, b_in)
    hidden_pair, active_pair = forward(w_in_pair, b_in_pair)

    def upstream(hidden, weights):
        _, pullback = jax.vjp(jax.nn.gelu, hidden)
        grad = pullback(dot(branch_full, weights, contract_cols))[0]
        return jnp.sum(grad, axis=0), grad.astype(jnp.bfloat16)

    bias_own, back_own = upstream(hidden_own, w_out)
    bias_pair, back_pair = upstream(hidden_pair, w_out_pair)
    partial_normed = dot(back_own, w_in, contract_cols) + dot(back_pair, w_in_pair, contract_cols)
    d_normed = summed_to_owner(partial_normed.astype(jnp.bfloat16))

    def weight_grads(active, back):
        out_t = dot(branch_full, active, contract_rows)
        inner = dot(gathered, back, contract_rows)
        return jnp.concatenate([inner, out_t], axis=1)

    for_pair = weight_grads(active_pair, back_pair).astype(jnp.bfloat16)
    from_pair = lax.ppermute(for_pair, "c", SWAP)
    both_local = weight_grads(active_own, back_own) + from_pair.astype(jnp.float32)
    both_sums = lax.psum_scatter(
        both_local.astype(jnp.bfloat16), "z", scatter_dimension=0, tiled=True
    )
    both_sums = lax.psum_scatter(both_sums, "y", scatter_dimension=0, tiled=True)
    both_sums = both_sums.astype(jnp.float32)
    hidden_cols = w_in.shape[1]
    d_w_in = both_sums[:, :hidden_cols]
    d_w_out = both_sums[:, hidden_cols:].T
    bias_local = bias_own + lax.ppermute(bias_pair, "c", SWAP)

    partial_branch = jnp.dot(active_own, w_out, preferred_element_type=jnp.float32) + jnp.dot(
        active_pair, w_out_pair, preferred_element_type=jnp.float32
    )
    branch = summed_to_owner(partial_branch.astype(jnp.bfloat16))
    initial = source.reshape(row_count, channels)
    result = (initial + layer_scale * branch).astype(jnp.bfloat16).reshape(activations.shape)
    scale_local = jnp.sum(incoming * branch, axis=0)

    grad_moments = jnp.stack([jnp.sum(d_normed * centered, axis=0), jnp.sum(d_normed, axis=0)])
    grad_rows = sent_to_all(grad_moments, DP)
    grad_totals = jnp.sum(owners[:, :, None, None] * grad_rows[None], axis=1)
    d_gain = grad_totals[:, 0]
    d_bias = grad_totals[:, 1]
    own_dgain = jnp.sum(member[:, None] * d_gain, axis=0)
    own_dbias = jnp.sum(member[:, None] * d_bias, axis=0)
    d_filtered = (
        own_gain * own_rstd * (d_normed - own_dbias / own_count - centered * own_dgain / own_count)
    )
    d_filtered = d_filtered.reshape(activations.shape)
    kernel_local = kernel_grad(source, d_filtered)
    d_kernel, d_b_in, d_scale = packed_total((kernel_local, bias_local, scale_local), DP)
    d_input = (cotangent.astype(jnp.float32) + depthwise(d_filtered, dw_kernel[::-1])).astype(
        jnp.bfloat16
    )
    return (result, d_input, d_kernel, d_gain, d_bias, d_w_in, d_b_in, d_w_out, d_scale)


def solution(mesh):
    split = Mesh(mesh.devices.reshape(8, 4, 4, 2), ("z", "y", "x", "c"))
    in_specs = (
        P(DP, None, None, CH),
        P(DP, None, None, CH),
        P(None, CH),
        P(None, CH),
        P(None, CH),
        P(None, CH),
        P(CH),
        P(CH, None),
        P(CH),
        P(),
    )
    out_specs = (
        P(DP, None, None, CH),
        P(DP, None, None, CH),
        P(None, CH),
        P(None, CH),
        P(None, CH),
        P(DP, CH),
        P(CH),
        P(CH, DP),
        P(CH),
    )
    return jax.shard_map(body, mesh=split, in_specs=in_specs, out_specs=out_specs, check_vma=False)
```

time: 239 us -> 202 us (0.85)
  waiting for transfers between devices: 103 us -> 70.5 us
  starting transfers between devices: 46.7 us -> 40.3 us
    all_to_all x5 -> x3, waiting for transfers between devices: 74.7 us -> 16.1 us  [sent_to_all(): lax.all_to_all(jnp.broadcast_to(array[None], (size, *array.shape)), axis,...]
    unnamed x4 -> x5, waiting for transfers between devices: 3.37 us -> 36.8 us
    all_to_all x5 -> x3, starting transfers between devices: 31.6 us -> 20 us  [sent_to_all(): lax.all_to_all(jnp.broadcast_to(array[None], (size, *array.shape)), axis,...]
    all_to_all x2 -> x3, waiting for transfers between devices: 24.5 us -> 15.9 us  [the longest x1 11.6 us: rows_of_all(): lax.all_to_all(halves.reshape(8, rows // 2, own), CH, 0, 0, tiled=True)]
    convert_element_type x3 -> x6, other arithmetic: 0.69 us -> 6.99 us  [the longest x1 4.29 us: body(): both_local.astype(jnp.bfloat16)]
    all_to_all x2 -> x3, starting transfers between devices: 14.8 us -> 19.4 us  [the longest x2 14.6 us: summed_to_owner(): lax.all_to_all(pieces, CH, 0, 0, tiled=True).reshape(4, 2 * rows, own)]
    broadcast_in_dim x5 -> x3, local copies, waits for them, and re-layouts: 5.77 us -> 2.63 us  [sent_to_all(): jnp.broadcast_to(array[None], (size, *array.shape))]
    reduce_sum x3, other arithmetic: 6.92 us -> 3.93 us  [kernel_grad(): collected.append(jnp.sum(window * upstream, axis=(0, 1, 2)))]
  transfers between devices with their start and end apart: 9 -> 14, of which waited for: 8 -> 9; matrix products, arithmetic and copies ran while one was open for 23% -> 33% of each run, Pallas kernels for 0% -> 0%
where the time goes in v1:
time: 202 us; the launch traced here: 200 us
  waiting for transfers between devices  70.5 us (35%)
  starting transfers between devices  40.3 us (20%)
  other arithmetic  31.5 us (16%)
  matrix products  21.9 us (11%)
  local copies, waits for them, and re-layouts  21.4 us (11%)
  between operations  14.9 us (7%)
    unnamed x5, waiting for transfers between devices  36.8 us
    all_to_all x3, starting transfers between devices, sent_to_all(): lax.all_to_all(jnp.broadcast_to(array[None], (size, *array.shape)), axis,...  20 us
    all_to_all x3, waiting for transfers between devices, sent_to_all(): lax.all_to_all(jnp.broadcast_to(array[None], (size, *array.shape)), axis,...  16.1 us
    all_to_all x2, starting transfers between devices, summed_to_owner(): lax.all_to_all(pieces, CH, 0, 0, tiled=True).reshape(4, 2 * rows, own)  14.6 us
    dot_general x8, matrix products, dot(): return lax.dot_general(a, b, dims, preferred_element_type=jnp.float32)  12.1 us
    all_to_all x1, waiting for transfers between devices, rows_of_all(): lax.all_to_all(halves.reshape(8, rows // 2, own), CH, 0, 0, tiled=True)  11.6 us
    unnamed x37, local copies, waits for them, and re-layouts  8.03 us
    dot_general x2, matrix products, forward(): jnp.dot(gathered, weights, preferred_element_type=jnp.float32) + bias  5.29 us
  transfers between devices with their start and end apart: 14, of which 9 were waited for; matrix products, arithmetic and copies ran while one was open for 33% of the time, Pallas kernels for 0%

profile of v1, /device:TPU:4, one launch (start us, length us, event | category | flops | bytes accessed | tf_op | source)
XLA Modules:
  0.0 200.5 jit_solution(1733299772697832537)
XLA Ops:
  13.0 4.4 %fusion.127 = (f32[128]{0:T(128)S(1)}, f32[128]{0:T(128)S(1)}, f32[1,16,64,128]{3,2,1,0:T(8,128)S(1)}) fusion(f32[128]{0:T(128)S(1)} %get-tuple-element.184, f32[128]{0:T(128)S(1)} %get-tuple-element.185, f32[128]{0:T(128)S(1)} %get-tuple-element.138, f32[128]{0:T(128)S(1)} %get-tuple-element.139, f32[128]{0:T(128)S(1)} %get-tuple-element.140, ...), kind=kLoop, calls=%fused_computation.373 | loop fusion | flops 13106944 | bytes 1074688 | tf_op jit(solution)/shard_map/reduce_sum | solution.py:110
  18.1 11.5 %all-to-all-start = ((f32[32,2,128]{2,1,0:T(2,128)}), f32[32,2,128]{2,1,0:T(2,128)S(1)}, u32[]{:S(2)}, u32[]{:S(2)}) async-start(f32[32,2,128]{2,1,0:T(2,128)} %broadcast_in_dim.8), calls=%async_computation | async-start | bytes 65536 | tf_op jit(solution)/shard_map/all_to_all | solution.py:16
  33.9 5.5 %all-to-all-done = f32[32,2,128]{2,1,0:T(2,128)S(1)} async-done(((f32[32,2,128]{2,1,0:T(2,128)}), f32[32,2,128]{2,1,0:T(2,128)S(1)}, u32[]{:S(2)}, u32[]{:S(2)}) %all-to-all-start) | async-done | bytes 32800 | tf_op jit(solution)/shard_map/all_to_all | solution.py:16
  40.9 4.8 %all-to-all-start.1 = ((bf16[8,512,128]{1,2,0:T(8,128)(2,1)}), bf16[8,512,128]{1,2,0:T(8,128)(2,1)S(1)}, u32[]{:S(2)}, u32[]{:S(2)}) async-start(bf16[8,512,128]{1,2,0:T(8,128)(2,1)} %bitcast.56), calls=%async_computation.1 | async-start | bytes 2097152 | tf_op jit(solution)/shard_map/all_to_all | solution.py:57
  46.9 11.6 %all-to-all-done.1 = bf16[8,512,128]{1,2,0:T(8,128)(2,1)S(1)} async-done(((bf16[8,512,128]{1,2,0:T(8,128)(2,1)}), bf16[8,512,128]{1,2,0:T(8,128)(2,1)S(1)}, u32[]{:S(2)}, u32[]{:S(2)}) %all-to-all-start.1) | async-done | bytes 1048608 | tf_op jit(solution)/shard_map/all_to_all | solution.py:57
  58.5 2.9 %convolution_add_fusion = f32[512,512]{1,0:T(8,128)} fusion(bf16[512,1024]{0,1:T(8,128)(2,1)S(1)} %bitcast.241, bf16[1024,512]{1,0:T(8,128)(2,1)} %collective-permute-done, f32[512]{0:T(512)S(1)} %collective-permute-done.1), kind=kOutput, calls=%fused_computation.111 | convolution fusion | flops 537133056 | bytes 3147776 | tf_op jit(solution)/shard_map/dot_general | solution.py:127
  61.4 2.3 %constant_dynamic-slice_fusion = bf16[8,512,128]{2,1,0:T(8,128)(2,1)} fusion(bf16[8,1024,128]{2,1,0:T(8,128)(2,1)} %all-gather.2.cloned.1.call-done, s32[]{:T(128)S(6)} %select_n.3), kind=kLoop, calls=%fused_computation.370 | loop fusion | bytes 2097156 | tf_op jit(solution)/shard_map/dynamic_slice | solution.py:102
  65.2 2.4 %fusion.133 = f32[512,512]{1,0:T(8,128)S(1)} fusion(bf16[512,1024]{0,1:T(8,128)(2,1)S(1)} %bitcast.237, bf16[512,1024]{1,0:T(8,128)(2,1)} %param.17), kind=kOutput, calls=%fused_computation.377 | convolution fusion | flops 536870912 | bytes 3145728 | tf_op jit(solution)/shard_map/dot_general | solution.py:124
  68.5 2.6 %fusion.128 = (f32[512]{0:T(512)S(1)}, bf16[512,512]{1,0:T(8,128)(2,1)S(1)}) fusion(f32[512,512]{1,0:T(8,128)S(1)} %copy-done.5, bf16[512,1024]{0,1:T(8,128)(2,1)S(1)} %bitcast.239, bf16[512,1024]{1,0:T(8,128)(2,1)} %collective-permute-done.2), kind=kOutput, calls=%fused_computation.374 | convolution fusion | flops 542375424 | bytes 3672064 | tf_op jit(solution)/shard_map/dot_general | solution.py:124
  73.3 2.4 %fusion.130 = (f32[512]{0:T(512)S(1)}, bf16[512,512]{1,0:T(8,128)(2,1)S(1)}, f32[512,512]{1,0:T(8,128)}) fusion(f32[512,512]{1,0:T(8,128)S(1)} %fusion.133, f32[512]{0:T(512)S(1)} %copy-done.14, bf16[512,1024]{0,1:T(8,128)(2,1)S(1)} %bitcast.243, bf16[1024,512]{1,0:T(8,128)(2,1)S(1)} %copy-done.4), kind=kOutput, calls=%fused_computation.375 | convolution fusion | flops 542637568 | bytes 4722688 | tf_op jit(solution)/shard_map/dot_general | solution.py:127
  79.6 7.3 %all-to-all-start.3 = ((bf16[8,512,128]{2,1,0:T(8,128)(2,1)}), bf16[8,512,128]{2,1,0:T(8,128)(2,1)}, u32[]{:S(2)}, u32[]{:S(2)}) async-start(bf16[8,512,128]{2,1,0:T(8,128)(2,1)} %bitcast.230), calls=%async_computation.3 | async-start | bytes 2097152 | tf_op jit(solution)/shard_map/all_to_all | solution.py:65
  86.9 2.4 %fusion.126 = f32[512,1024]{1,0:T(8,128)S(1)} fusion(bf16[512,1024]{1,0:T(8,128)(2,1)} %param.17, f32[512,512]{1,0:T(8,128)} %get-tuple-element.188), kind=kOutput, calls=%fused_computation.372 | convolution fusion | flops 539230208 | bytes 4194304 | tf_op jit(solution)/shard_map/dot_general | solution.py:161
  92.6 2.1 %fusion.116 = f32[1024,512]{0,1:T(8,128)} fusion(bf16[512,1024]{0,1:T(8,128)(2,1)S(1)} %bitcast.244, bf16[512,512]{1,0:T(8,128)(2,1)S(1)} %get-tuple-element.131), kind=kOutput, calls=%fused_computation.290 | convolution fusion | flops 536870912 | bytes 3670016 | tf_op jit(solution)/shard_map/dot_general | solution.py:124
  95.5 4.3 %all-to-all-done.3 = bf16[8,512,128]{2,1,0:T(8,128)(2,1)} async-done(((bf16[8,512,128]{2,1,0:T(8,128)(2,1)}), bf16[8,512,128]{2,1,0:T(8,128)(2,1)}, u32[]{:S(2)}, u32[]{:S(2)}) %all-to-all-start.3) | async-done | bytes 1048608 | tf_op jit(solution)/shard_map/all_to_all | solution.py:65
  99.7 7.3 %all-to-all-start.2 = ((bf16[8,512,128]{2,1,0:T(8,128)(2,1)}), bf16[8,512,128]{2,1,0:T(8,128)(2,1)}, u32[]{:S(2)}, u32[]{:S(2)}) async-start(bf16[8,512,128]{2,1,0:T(8,128)(2,1)} %bitcast.245), calls=%async_computation.2 | async-start | bytes 2097152 | tf_op jit(solution)/shard_map/all_to_all | solution.py:65
  107.1 4.3 %fusion = bf16[1024,1024]{0,1:T(8,128)(2,1)} fusion(f32[1024,512]{0,1:T(8,128)S(1)} %fusion.125, f32[1024,512]{0,1:T(8,128)} %fusion.116, bf16[1024,1024]{0,1:T(8,128)(2,1)} %collective-permute-done.4), kind=kLoop, calls=%fused_computation.97 | loop fusion | flops 4194304 | bytes 8388608 | tf_op jit(solution)/shard_map/convert_element_type | solution.py:152
  111.3 4.0 %copy.66 = bf16[1024,1024]{1,0:T(8,128)(2,1)} copy(bf16[1024,1024]{0,1:T(8,128)(2,1)} %fusion) | data formatting | bytes 4194304
  120.6 4.6 %all-to-all-start.4 = ((f32[32,2,128]{2,1,0:T(2,128)}), f32[32,2,128]{2,1,0:T(2,128)S(1)}, u32[]{:S(2)}, u32[]{:S(2)}) async-start(f32[32,2,128]{2,1,0:T(2,128)} %broadcast_in_dim.10), calls=%async_computation.4 | async-start | bytes 65536 | tf_op jit(solution)/shard_map/all_to_all | solution.py:16
  126.9 8.1 %all-to-all-done.4 = f32[32,2,128]{2,1,0:T(2,128)S(1)} async-done(((f32[32,2,128]{2,1,0:T(2,128)}), f32[32,2,128]{2,1,0:T(2,128)S(1)}, u32[]{:S(2)}, u32[]{:S(2)}) %all-to-all-start.4) | async-done | bytes 32800 | tf_op jit(solution)/shard_map/all_to_all | solution.py:16
  140.7 3.9 %all-to-all-start.5 = ((f32[32,1,6912]{2,1,0:T(1,128)}), f32[32,1,6912]{2,1,0:T(1,128)S(1)}, u32[]{:S(2)}, u32[]{:S(2)}) async-start(f32[32,1,6912]{2,1,0:T(1,128)} %broadcast_in_dim.11), calls=%async_computation.5 | async-start | bytes 1769472 | tf_op jit(solution)/shard_map/all_to_all | solution.py:16
  144.7 17.7 %reduce-scatter.7.cloned.1.call-done = bf16[128,1024]{1,0:T(8,128)(2,1)} async-done(((bf16[1024,1024]{1,0:T(8,128)(2,1)}), bf16[128,1024]{1,0:T(8,128)(2,1)}) %reduce-scatter.7.cloned.1.call-update) | async-done | bytes 262160
  162.4 5.1 %fusion.109 = bf16[1,16,64,128]{3,2,1,0:T(8,128)(2,1)} fusion(f32[1,16,64,128]{3,2,1,0:T(8,128)S(1)} %get-tuple-element.127, bf16[1,16,64,128]{3,2,1,0:T(8,128)(2,1)S(1)} %copy-done.2, f32[128]{0:T(128)S(1)} %get-tuple-element.184, f32[128]{0:T(128)S(1)} %get-tuple-element.185, f32[128]{0:T(128)S(1)} %get-tuple-element.138, f32[128]{0:T(128)S(1)} %get-tuple-element.139, ...), kind=kLoop, calls=%fused_computation.223 | loop fusion | flops 13107200 | bytes 1073664 | tf_op jit(solution)/shard_map/convert_element_type | solution.py:182
  167.5 2.5 %all-to-all-done.5 = f32[32,1,6912]{2,1,0:T(1,128)S(1)} async-done(((f32[32,1,6912]{2,1,0:T(1,128)}), f32[32,1,6912]{2,1,0:T(1,128)S(1)}, u32[]{:S(2)}, u32[]{:S(2)}) %all-to-all-start.5) | async-done | bytes 884768 | tf_op jit(solution)/shard_map/all_to_all | solution.py:16
  172.2 19.1 %reduce-scatter.9.cloned.1.call-done = bf16[32,1024]{1,0:T(8,128)(2,1)} async-done(((bf16[128,1024]{1,0:T(8,128)(2,1)}), bf16[32,1024]{1,0:T(8,128)(2,1)}) %reduce-scatter.9.cloned.1.call-update) | async-done | bytes 65552
  (110 shorter events, 42.7 us)
Async XLA Ops:
  7.2 22.4 %copy-start.3 = (bf16[1024,512]{1,0:T(8,128)(2,1)S(1)}, bf16[1024,512]{1,0:T(8,128)(2,1)}, u32[]{:S(2)}) copy-start(bf16[1024,512]{1,0:T(8,128)(2,1)} %param.15) | copy-start | bytes 3145732
  7.2 22.5 %copy-start.15 = (s32[4]{0:T(128)S(1)}, s32[4]{0:T(128)}, u32[]{:S(2)}) copy-start(s32[4]{0:T(128)} %param.19) | copy-start | bytes 52
  7.2 26.6 %copy-start.12 = (f32[4,128]{1,0:T(4,128)S(1)}, f32[4,128]{1,0:T(4,128)}, u32[]{:S(2)}) copy-start(f32[4,128]{1,0:T(4,128)} %param.13) | copy-start | bytes 6148
  7.2 26.6 %copy-start.13 = (f32[4,128]{1,0:T(4,128)S(1)}, f32[4,128]{1,0:T(4,128)}, u32[]{:S(2)}) copy-start(f32[4,128]{1,0:T(4,128)} %param.14) | copy-start | bytes 6148
  7.2 54.2 %all-gather.2.cloned.1.call-start = ((), (), s32[]{:S(2)}) async-start(), calls=%async_computation.8 | async-start | bytes 2359296 | tf_op jit(solution)/shard_map/all_gather | solution.py:101
  18.1 21.3 %all-to-all-start = ((f32[32,2,128]{2,1,0:T(2,128)}), f32[32,2,128]{2,1,0:T(2,128)S(1)}, u32[]{:S(2)}, u32[]{:S(2)}) async-start(f32[32,2,128]{2,1,0:T(2,128)} %broadcast_in_dim.8), calls=%async_computation | async-start | bytes 65536 | tf_op jit(solution)/shard_map/all_to_all | solution.py:16
  29.6 28.9 %collective-permute-start = (bf16[1024,512]{1,0:T(8,128)(2,1)S(1)}, bf16[1024,512]{1,0:T(8,128)(2,1)}, u32[]{:S(2)}, u32[]{:S(2)}) collective-permute-start(bf16[1024,512]{1,0:T(8,128)(2,1)S(1)} %copy-done.3), channel_id=1, source_target_pairs={{0,1},{1,0},{2,3},{3,2},{4,5},{5,4},{6,7},{7,6},{8,9},{9,8},{10,11... | collective-permute-start | bytes 3145736 | tf_op jit(solution)/shard_map/ppermute | solution.py:104
  39.6 6.0 %copy-start.14 = (f32[512]{0:T(512)S(1)}, f32[512]{0:T(512)}, u32[]{:S(2)}) copy-start(f32[512]{0:T(512)} %param.16) | copy-start | bytes 6148
  40.9 17.6 %all-to-all-start.1 = ((bf16[8,512,128]{1,2,0:T(8,128)(2,1)}), bf16[8,512,128]{1,2,0:T(8,128)(2,1)S(1)}, u32[]{:S(2)}, u32[]{:S(2)}) async-start(bf16[8,512,128]{1,2,0:T(8,128)(2,1)} %bitcast.56), calls=%async_computation.1 | async-start | bytes 2097152 | tf_op jit(solution)/shard_map/all_to_all | solution.py:57
  45.7 1.2 collective-permute-start.1
  45.8 22.6 %collective-permute-start.2 = (bf16[512,1024]{1,0:T(8,128)(2,1)}, bf16[512,1024]{1,0:T(8,128)(2,1)}, u32[]{:S(2)}, u32[]{:S(2)}) collective-permute-start(bf16[512,1024]{1,0:T(8,128)(2,1)} %param.17), channel_id=1, source_target_pairs={{0,1},{1,0},{2,3},{3,2},{4,5},{5,4},{6,7},{7,6},{8,9},{9,8},{10,11... | collective-permute-start | bytes 3145736 | tf_op jit(solution)/shard_map/ppermute | solution.py:105
  65.2 3.2 %copy-start = (bf16[8,512,128]{1,2,0:T(8,128)(2,1)}, bf16[8,512,128]{1,2,0:T(8,128)(2,1)S(1)}, u32[]{:S(2)}) copy-start(bf16[8,512,128]{1,2,0:T(8,128)(2,1)S(1)} %copy.71) | copy-start | bytes 3145732
  73.3 33.8 %collective-permute-start.4 = (bf16[1024,1024]{0,1:T(8,128)(2,1)}, bf16[1024,1024]{0,1:T(8,128)(2,1)}, u32[]{:S(2)}, u32[]{:S(2)}) collective-permute-start(bf16[1024,1024]{0,1:T(8,128)(2,1)} %pad_maximum_fusion), channel_id=1, source_target_pairs={{0,1},{1,0},{2,3},{3,2},{4,5},{5,4},{6,7},{7,6},{8,9},{9,8},{10,11... | collective-permute-start | bytes 6291464 | tf_op jit(solution)/shard_map/ppermute | solution.py:149
  79.6 20.2 %all-to-all-start.3 = ((bf16[8,512,128]{2,1,0:T(8,128)(2,1)}), bf16[8,512,128]{2,1,0:T(8,128)(2,1)}, u32[]{:S(2)}, u32[]{:S(2)}) async-start(bf16[8,512,128]{2,1,0:T(8,128)(2,1)} %bitcast.230), calls=%async_computation.3 | async-start | bytes 2097152 | tf_op jit(solution)/shard_map/all_to_all | solution.py:65
  99.7 20.3 %all-to-all-start.2 = ((bf16[8,512,128]{2,1,0:T(8,128)(2,1)}), bf16[8,512,128]{2,1,0:T(8,128)(2,1)}, u32[]{:S(2)}, u32[]{:S(2)}) async-start(bf16[8,512,128]{2,1,0:T(8,128)(2,1)} %bitcast.245), calls=%async_computation.2 | async-start | bytes 2097152 | tf_op jit(solution)/shard_map/all_to_all | solution.py:65
  107.1 55.3 %reduce-scatter.7.cloned.1.call-start = ((), (), s32[]{:S(2)}) async-start(), calls=%async_computation.9 | async-start | bytes 2359296
  115.3 1.3 collective-permute-start.3
  118.0 8.7 %copy-start.2 = (bf16[1,16,64,128]{3,2,1,0:T(8,128)(2,1)S(1)}, bf16[1,16,64,128]{3,2,1,0:T(8,128)(2,1)}, u32[]{:S(2)}) copy-start(bf16[1,16,64,128]{3,2,1,0:T(8,128)(2,1)} %param.11) | copy-start | bytes 786436
  120.6 14.3 %all-to-all-start.4 = ((f32[32,2,128]{2,1,0:T(2,128)}), f32[32,2,128]{2,1,0:T(2,128)S(1)}, u32[]{:S(2)}, u32[]{:S(2)}) async-start(f32[32,2,128]{2,1,0:T(2,128)} %broadcast_in_dim.10), calls=%async_computation.4 | async-start | bytes 65536 | tf_op jit(solution)/shard_map/all_to_all | solution.py:16
  125.2 10.9 %copy-start.8 = (bf16[1,16,64,128]{3,2,1,0:T(8,128)(2,1)S(1)}, bf16[1,16,64,128]{3,2,1,0:T(8,128)(2,1)}, u32[]{:S(2)}) copy-start(bf16[1,16,64,128]{3,2,1,0:T(8,128)(2,1)} %param.10) | copy-start | bytes 786436
  125.2 10.9 %copy-start.11 = (f32[128]{0:T(128)S(1)}, f32[128]{0:T(128)}, u32[]{:S(2)}) copy-start(f32[128]{0:T(128)} %param.18) | copy-start | bytes 1540
  135.1 2.5 %copy-start.9 = (f32[4,1,128]{2,1,0:T(1,128)}, f32[4,1,128]{2,1,0:T(1,128)S(1)}, u32[]{:S(2)}) copy-start(f32[4,1,128]{2,1,0:T(1,128)S(1)} %get-tuple-element.186) | copy-start | bytes 6148
  140.7 29.3 %all-to-all-start.5 = ((f32[32,1,6912]{2,1,0:T(1,128)}), f32[32,1,6912]{2,1,0:T(1,128)S(1)}, u32[]{:S(2)}, u32[]{:S(2)}) async-start(f32[32,1,6912]{2,1,0:T(1,128)} %broadcast_in_dim.11), calls=%async_computation.5 | async-start | bytes 1769472 | tf_op jit(solution)/shard_map/all_to_all | solution.py:16
  144.6 46.7 %reduce-scatter.9.cloned.1.call-start = ((), (), s32[]{:S(2)}) async-start(), calls=%async_computation.10 | async-start | bytes 327680
  (6 other events, 13.0 us)
Sparse Core Ops, SparseCore 0:
  10.5 29.8 all-gather.1
  115.4 46.8 reduce-scatter.6
  164.9 26.4 reduce-scatter.8

commit v2 on v1

--- a/solution.py
+++ b/solution.py
@@ -58,11 +58,14 @@
     return jnp.moveaxis(pieces, 0, 1).reshape(rows // 2, 8 * own)
 
 
-def summed_to_owner(array):
+def exchanged(array):
     rows, width = array.shape
     own = width // 8
     pieces = jnp.moveaxis(array.reshape(rows, 8, own), 1, 0)
-    pieces = lax.all_to_all(pieces, CH, 0, 0, tiled=True).reshape(4, 2 * rows, own)
+    return lax.all_to_all(pieces, CH, 0, 0, tiled=True).reshape(4, 2 * rows, own)
+
+
+def summed(pieces):
     return jnp.sum(pieces.astype(jnp.float32), axis=0)
 
 
@@ -130,6 +133,15 @@
     hidden_own, active_own = forward(w_in, b_in)
     hidden_pair, active_pair = forward(w_in_pair, b_in_pair)
 
+    partial_branch = jnp.dot(active_own, w_out, preferred_element_type=jnp.float32) + jnp.dot(
+        active_pair, w_out_pair, preferred_element_type=jnp.float32
+    )
+    branch_pieces = exchanged(partial_branch.astype(jnp.bfloat16))
+    branch = summed(branch_pieces)
+    initial = source.reshape(row_count, channels)
+    result = (initial + layer_scale * branch).astype(jnp.bfloat16).reshape(activations.shape)
+    scale_local = jnp.sum(incoming * branch, axis=0)
+
     def upstream(hidden, weights):
         _, pullback = jax.vjp(jax.nn.gelu, hidden)
         grad = pullback(dot(branch_full, weights, contract_cols))[0]
@@ -138,7 +150,10 @@
     bias_own, back_own = upstream(hidden_own, w_out)
     bias_pair, back_pair = upstream(hidden_pair, w_out_pair)
     partial_normed = dot(back_own, w_in, contract_cols) + dot(back_pair, w_in_pair, contract_cols)
-    d_normed = summed_to_owner(partial_normed.astype(jnp.bfloat16))
+    partial_normed, branch_pieces = lax.optimization_barrier(
+        (partial_normed.astype(jnp.bfloat16), branch_pieces)
+    )
+    normed_pieces = exchanged(partial_normed)
 
     def weight_grads(active, back):
         out_t = dot(branch_full, active, contract_rows)
@@ -148,23 +163,12 @@
     for_pair = weight_grads(active_pair, back_pair).astype(jnp.bfloat16)
     from_pair = lax.ppermute(for_pair, "c", SWAP)
     both_local = weight_grads(active_own, back_own) + from_pair.astype(jnp.float32)
-    both_sums = lax.psum_scatter(
-        both_local.astype(jnp.bfloat16), "z", scatter_dimension=0, tiled=True
-    )
-    both_sums = lax.psum_scatter(both_sums, "y", scatter_dimension=0, tiled=True)
-    both_sums = both_sums.astype(jnp.float32)
+    both_local = both_local.astype(jnp.bfloat16)
+    near = lax.psum_scatter(both_local, "z", scatter_dimension=0, tiled=True)
     hidden_cols = w_in.shape[1]
-    d_w_in = both_sums[:, :hidden_cols]
-    d_w_out = both_sums[:, hidden_cols:].T
     bias_local = bias_own + lax.ppermute(bias_pair, "c", SWAP)
-
-    partial_branch = jnp.dot(active_own, w_out, preferred_element_type=jnp.float32) + jnp.dot(
-        active_pair, w_out_pair, preferred_element_type=jnp.float32
-    )
-    branch = summed_to_owner(partial_branch.astype(jnp.bfloat16))
-    initial = source.reshape(row_count, channels)
-    result = (initial + layer_scale * branch).astype(jnp.bfloat16).reshape(activations.shape)
-    scale_local = jnp.sum(incoming * branch, axis=0)
+    normed_pieces, both_local = lax.optimization_barrier((normed_pieces, both_local))
+    d_normed = summed(normed_pieces)
 
     grad_moments = jnp.stack([jnp.sum(d_normed * centered, axis=0), jnp.sum(d_normed, axis=0)])
     grad_rows = sent_to_all(grad_moments, DP)
@@ -179,6 +183,11 @@
     d_filtered = d_filtered.reshape(activations.shape)
     kernel_local = kernel_grad(source, d_filtered)
     d_kernel, d_b_in, d_scale = packed_total((kernel_local, bias_local, scale_local), DP)
+    near, d_kernel = lax.optimization_barrier((near, d_kernel))
+    everything = lax.all_to_all(near.reshape(4, -1, near.shape[1]), "y", 0, 0, tiled=True)
+    both_sums = jnp.sum(everything.astype(jnp.float32), axis=0)
+    d_w_in = both_sums[:, :hidden_cols]
+    d_w_out = both_sums[:, hidden_cols:].T
     d_input = (cotangent.astype(jnp.float32) + depthwise(d_filtered, dw_kernel[::-1])).astype(
         jnp.bfloat16
     )

time: 202 us -> 203 us (level); the launches traced: 200 us -> 199 us
  blocking collectives: 0 us -> 33.8 us
  waiting for transfers between devices: 70.5 us -> 37.9 us
    unnamed x5 -> x3, waiting for transfers between devices: 36.8 us -> 0.03 us
    all_to_all x0 -> x1, blocking collectives: none -> 33.8 us  [sent_to_all(): lax.all_to_all(jnp.broadcast_to(array[None], (size, *array.shape)), axis,...]
    all_to_all x2 -> x3, waiting for transfers between devices: 4.27 us -> 10.1 us  [the longest x2 9.82 us: exchanged(): lax.all_to_all(pieces, CH, 0, 0, tiled=True).reshape(4, 2 * rows, own)]
    all_to_all x3 -> x2, starting transfers between devices: 20 us -> 15.9 us  [sent_to_all(): lax.all_to_all(jnp.broadcast_to(array[None], (size, *array.shape)), axis,...]
    all_to_all x2 -> x3, starting transfers between devices: 14.6 us -> 18.3 us  [the longest x2 14.5 us: exchanged(): lax.all_to_all(pieces, CH, 0, 0, tiled=True).reshape(4, 2 * rows, own)]
    convert_element_type x3 -> x1, other arithmetic: 5.69 us -> 2.47 us  [body(): both_local = both_local.astype(jnp.bfloat16)]
    unnamed x37 -> x116, local copies, waits for them, and re-layouts: 8.03 us -> 5.57 us
    all_to_all x3 -> x2, waiting for transfers between devices: 16.1 us -> 15.2 us  [sent_to_all(): lax.all_to_all(jnp.broadcast_to(array[None], (size, *array.shape)), axis,...]
  transfers between devices with their start and end apart: 14 -> 13, of which waited for: 9 -> 8; matrix products, arithmetic and copies ran while one was open for 33% -> 30% of each run, Pallas kernels for 0% -> 0%
where the time goes in v2:
time: 203 us; the launch traced here: 199 us
  starting transfers between devices  39.8 us (20%)
  waiting for transfers between devices  37.9 us (19%)
  blocking collectives  33.8 us (17%)
  other arithmetic  29.9 us (15%)
  matrix products  21.7 us (11%)
  local copies, waits for them, and re-layouts  20.5 us (10%)
  between operations  15.6 us (8%)
    all_to_all x1, blocking collectives, sent_to_all(): lax.all_to_all(jnp.broadcast_to(array[None], (size, *array.shape)), axis,...  33.8 us
    all_to_all x2, starting transfers between devices, sent_to_all(): lax.all_to_all(jnp.broadcast_to(array[None], (size, *array.shape)), axis,...  15.9 us
    all_to_all x2, waiting for transfers between devices, sent_to_all(): lax.all_to_all(jnp.broadcast_to(array[None], (size, *array.shape)), axis,...  15.2 us
    all_to_all x2, starting transfers between devices, exchanged(): lax.all_to_all(pieces, CH, 0, 0, tiled=True).reshape(4, 2 * rows, own)  14.5 us
    dot_general x8, matrix products, dot(): return lax.dot_general(a, b, dims, preferred_element_type=jnp.float32)  13.6 us
    all_to_all x1, waiting for transfers between devices, rows_of_all(): lax.all_to_all(halves.reshape(8, rows // 2, own), CH, 0, 0, tiled=True)  11.6 us
    all_to_all x2, waiting for transfers between devices, exchanged(): lax.all_to_all(pieces, CH, 0, 0, tiled=True).reshape(4, 2 * rows, own)  9.82 us
    unnamed x116, local copies, waits for them, and re-layouts  5.57 us
  transfers between devices with their start and end apart: 13, of which 8 were waited for; matrix products, arithmetic and copies ran while one was open for 30% of the time, Pallas kernels for 0%

profile of v2, /device:TPU:4, one launch (start us, length us, event | category | flops | bytes accessed | tf_op | source)
XLA Modules:
  0.0 199.1 jit_solution(1270470067304328371)
XLA Ops:
  13.2 4.4 %fusion.126 = (f32[128]{0:T(128)S(1)}, f32[128]{0:T(128)S(1)}, f32[1,16,64,128]{3,2,1,0:T(8,128)S(1)}) fusion(f32[128]{0:T(128)S(1)} %get-tuple-element.133, f32[128]{0:T(128)S(1)} %get-tuple-element.134, f32[128]{0:T(128)S(1)} %get-tuple-element.87, f32[128]{0:T(128)S(1)} %get-tuple-element.88, f32[128]{0:T(128)S(1)} %get-tuple-element.89, ...), kind=kLoop, calls=%fused_computation.373 | loop fusion | flops 13106944 | bytes 1074688 | tf_op jit(solution)/shard_map/reduce_sum | solution.py:113
  18.2 11.5 %all-to-all-start = ((f32[32,2,128]{2,1,0:T(2,128)}), f32[32,2,128]{2,1,0:T(2,128)S(1)}, u32[]{:S(2)}, u32[]{:S(2)}) async-start(f32[32,2,128]{2,1,0:T(2,128)} %broadcast_in_dim.8), calls=%async_computation | async-start | bytes 65536 | tf_op jit(solution)/shard_map/all_to_all | solution.py:16
  34.1 5.5 %all-to-all-done = f32[32,2,128]{2,1,0:T(2,128)S(1)} async-done(((f32[32,2,128]{2,1,0:T(2,128)}), f32[32,2,128]{2,1,0:T(2,128)S(1)}, u32[]{:S(2)}, u32[]{:S(2)}) %all-to-all-start) | async-done | bytes 32800 | tf_op jit(solution)/shard_map/all_to_all | solution.py:16
  41.7 4.8 %all-to-all-start.1 = ((bf16[8,512,128]{1,2,0:T(8,128)(2,1)}), bf16[8,512,128]{1,2,0:T(8,128)(2,1)S(1)}, u32[]{:S(2)}, u32[]{:S(2)}) async-start(bf16[8,512,128]{1,2,0:T(8,128)(2,1)} %bitcast.56), calls=%async_computation.1 | async-start | bytes 2097152 | tf_op jit(solution)/shard_map/all_to_all | solution.py:57
  47.7 11.6 %all-to-all-done.1 = bf16[8,512,128]{1,2,0:T(8,128)(2,1)S(1)} async-done(((bf16[8,512,128]{1,2,0:T(8,128)(2,1)}), bf16[8,512,128]{1,2,0:T(8,128)(2,1)S(1)}, u32[]{:S(2)}, u32[]{:S(2)}) %all-to-all-start.1) | async-done | bytes 1048608 | tf_op jit(solution)/shard_map/all_to_all | solution.py:57
  59.3 2.9 %convolution_add_fusion = f32[512,512]{1,0:T(8,128)} fusion(bf16[512,1024]{0,1:T(8,128)(2,1)S(1)} %bitcast.236, bf16[1024,512]{1,0:T(8,128)(2,1)} %collective-permute-done, f32[512]{0:T(512)S(1)} %collective-permute-done.1), kind=kOutput, calls=%fused_computation.111 | convolution fusion | flops 537133056 | bytes 3147776 | tf_op jit(solution)/shard_map/dot_general | solution.py:130
  62.2 2.3 %constant_dynamic-slice_fusion = bf16[8,512,128]{2,1,0:T(8,128)(2,1)} fusion(bf16[8,1024,128]{2,1,0:T(8,128)(2,1)} %all-gather.2.cloned.1.call-done, s32[]{:T(128)S(6)} %select_n.3), kind=kLoop, calls=%fused_computation.370 | loop fusion | bytes 2097156 | tf_op jit(solution)/shard_map/dynamic_slice | solution.py:105
  69.3 2.3 %fusion.129 = (f32[512]{0:T(512)S(1)}, bf16[512,512]{1,0:T(8,128)(2,1)}, f32[512,512]{1,0:T(8,128)S(1)}) fusion(f32[512,512]{1,0:T(8,128)S(1)} %fusion.132, f32[512]{0:T(512)S(1)} %copy-done.55, bf16[512,1024]{0,1:T(8,128)(2,1)S(1)} %bitcast.237, bf16[1024,512]{1,0:T(8,128)(2,1)S(1)} %copy-done.4), kind=kOutput, calls=%fused_computation.375 | convolution fusion | flops 542637568 | bytes 4722688 | tf_op jit(solution)/shard_map/dot_general | solution.py:130
  71.6 2.9 %fusion.127 = (f32[512]{0:T(512)S(1)}, bf16[512,512]{1,0:T(8,128)(2,1)S(1)}) fusion(f32[512,512]{1,0:T(8,128)S(1)} %copy-done.6, bf16[512,1024]{0,1:T(8,128)(2,1)S(1)} %bitcast.234, bf16[512,1024]{1,0:T(8,128)(2,1)} %collective-permute-done.2), kind=kOutput, calls=%fused_computation.374 | convolution fusion | flops 542375424 | bytes 3672064 | tf_op jit(solution)/shard_map/dot_general | solution.py:127
  78.5 2.1 %fusion.1 = bf16[64,8,8,128]{3,2,1,0:T(8,128)(2,1)S(1)} fusion(f32[512,1024]{1,0:T(8,128)S(1)} %fusion.125, bf16[512,1024]{1,0:T(8,128)(2,1)} %collective-permute-done.2, f32[512,512]{1,0:T(8,128)S(1)} %copy-done.6), kind=kOutput, calls=%fused_computation.110 | convolution fusion | flops 540278784 | bytes 5242880 | tf_op jit(solution)/shard_map/dot_general | solution.py:136
  81.8 7.3 %all-to-all-start.2 = ((bf16[8,512,128]{2,1,0:T(8,128)(2,1)}), bf16[8,512,128]{2,1,0:T(8,128)(2,1)}, u32[]{:S(2)}, u32[]{:S(2)}) async-start(bf16[8,512,128]{2,1,0:T(8,128)(2,1)} %bitcast.240), calls=%async_computation.2 | async-start | bytes 2097152 | tf_op jit(solution)/shard_map/all_to_all | solution.py:65
  89.1 2.2 %fusion.117 = f32[512,1024]{1,0:T(8,128)S(1)} fusion(bf16[1024,512]{1,0:T(8,128)(2,1)} %param.15, bf16[512,512]{1,0:T(8,128)(2,1)} %get-tuple-element.78), kind=kOutput, calls=%fused_computation.291 | convolution fusion | flops 536870912 | bytes 3670016 | tf_op jit(solution)/shard_map/dot_general | solution.py:127
  94.4 7.6 %all-to-all-done.2 = bf16[8,512,128]{2,1,0:T(8,128)(2,1)} async-done(((bf16[8,512,128]{2,1,0:T(8,128)(2,1)}), bf16[8,512,128]{2,1,0:T(8,128)(2,1)}, u32[]{:S(2)}, u32[]{:S(2)}) %all-to-all-start.2) | async-done | bytes 1048608 | tf_op jit(solution)/shard_map/all_to_all | solution.py:65
  102.0 7.3 %all-to-all-start.3 = ((bf16[8,512,128]{2,1,0:T(8,128)(2,1)}), bf16[8,512,128]{2,1,0:T(8,128)(2,1)}, u32[]{:S(2)}, u32[]{:S(2)}) async-start(bf16[8,512,128]{2,1,0:T(8,128)(2,1)} %bitcast_bitcast_fusion), calls=%async_computation.3 | async-start | bytes 2097152 | tf_op jit(solution)/shard_map/all_to_all | solution.py:65
  109.2 2.1 %fusion.124 = f32[1024,512]{0,1:T(8,128)S(1)} fusion(bf16[512,1024]{0,1:T(8,128)(2,1)S(1)} %bitcast.235, f32[512,512]{1,0:T(8,128)} %copy-done.5), kind=kOutput, calls=%fused_computation.371 | convolution fusion | flops 539230208 | bytes 4194304 | tf_op jit(solution)/shard_map/dot_general | solution.py:127
  112.6 2.2 %convert_reduce_fusion.2 = f32[1024,128]{1,0:T(8,128)} fusion(bf16[4,1024,128]{2,1,0:T(8,128)(2,1)} %bitcast.230), kind=kLoop, calls=%fused_computation.102 | loop fusion | flops 917504 | bytes 1572864 | tf_op jit(solution)/shard_map/reduce_sum | solution.py:69
  114.8 2.5 %fusion = bf16[1024,1024]{0,1:T(8,128)(2,1)S(1)} fusion(f32[1024,512]{0,1:T(8,128)S(1)} %fusion.124, f32[1024,512]{0,1:T(8,128)S(1)} %fusion.115, bf16[1024,1024]{0,1:T(8,128)(2,1)} %collective-permute-done.3), kind=kLoop, calls=%fused_computation.97 | loop fusion | flops 4194304 | bytes 8388608 | tf_op jit(solution)/shard_map/convert_element_type | solution.py:166
  117.3 2.6 %copy.58 = bf16[1024,1024]{1,0:T(8,128)(2,1)} copy(bf16[1024,1024]{0,1:T(8,128)(2,1)S(1)} %fusion) | data formatting | bytes 4194304
  119.9 2.3 %all-to-all-done.3 = bf16[8,512,128]{2,1,0:T(8,128)(2,1)} async-done(((bf16[8,512,128]{2,1,0:T(8,128)(2,1)}), bf16[8,512,128]{2,1,0:T(8,128)(2,1)}, u32[]{:S(2)}, u32[]{:S(2)}) %all-to-all-start.3) | async-done | bytes 1048608 | tf_op jit(solution)/shard_map/all_to_all | solution.py:65
  125.1 4.4 %all-to-all-start.4 = ((f32[32,2,128]{2,1,0:T(2,128)}), f32[32,2,128]{2,1,0:T(2,128)S(1)}, u32[]{:S(2)}, u32[]{:S(2)}) async-start(f32[32,2,128]{2,1,0:T(2,128)} %broadcast_in_dim.10), calls=%async_computation.4 | async-start | bytes 65536 | tf_op jit(solution)/shard_map/all_to_all | solution.py:16
  129.6 9.7 %all-to-all-done.4 = f32[32,2,128]{2,1,0:T(2,128)S(1)} async-done(((f32[32,2,128]{2,1,0:T(2,128)}), f32[32,2,128]{2,1,0:T(2,128)S(1)}, u32[]{:S(2)}, u32[]{:S(2)}) %all-to-all-start.4) | async-done | bytes 32800 | tf_op jit(solution)/shard_map/all_to_all | solution.py:16
  144.3 33.8 %all_to_all.36 = f32[32,1,6912]{2,1,0:T(1,128)S(1)} all-to-all(f32[32,1,6912]{2,1,0:T(1,128)S(1)} %broadcast_in_dim.11), channel_id=1, replica_groups=mesh['z'=8,'y'=4,'x'=4,'c'=2] {'z','y'}, dimensions={0} | all-to-all | bytes 1769472 | tf_op jit(solution)/shard_map/all_to_all | solution.py:16
  181.2 3.7 %all-to-all-start.6 = ((bf16[4,32,1024]{2,1,0:T(8,128)(2,1)}), bf16[4,32,1024]{2,1,0:T(8,128)(2,1)S(1)}, u32[]{:S(2)}, u32[]{:S(2)}) async-start(bf16[4,32,1024]{2,1,0:T(8,128)(2,1)} %bitcast.127), calls=%async_computation.6 | async-start | bytes 524288 | tf_op jit(solution)/shard_map/all_to_all | solution.py:187
  185.1 5.1 %fusion.108 = bf16[1,16,64,128]{3,2,1,0:T(8,128)(2,1)} fusion(f32[1,16,64,128]{3,2,1,0:T(8,128)S(1)} %get-tuple-element.74, bf16[1,16,64,128]{3,2,1,0:T(8,128)(2,1)S(1)} %copy-done.1, f32[128]{0:T(128)S(1)} %get-tuple-element.133, f32[128]{0:T(128)S(1)} %get-tuple-element.134, f32[128]{0:T(128)S(1)} %get-tuple-element.87, f32[128]{0:T(128)S(1)} %get-tuple-element.88, ...), kind=kLoop, calls=%fused_computation.223 | loop fusion | flops 13107200 | bytes 1073664 | tf_op jit(solution)/shard_map/convert_element_type | solution.py:191
  (186 shorter events, 40.6 us)
Async XLA Ops:
  7.2 55.0 %all-gather.2.cloned.1.call-start = ((), (), s32[]{:S(2)}) async-start(), calls=%async_computation.8 | async-start | bytes 2359296 | tf_op jit(solution)/shard_map/all_gather | solution.py:104
  18.2 21.3 %all-to-all-start = ((f32[32,2,128]{2,1,0:T(2,128)}), f32[32,2,128]{2,1,0:T(2,128)S(1)}, u32[]{:S(2)}, u32[]{:S(2)}) async-start(f32[32,2,128]{2,1,0:T(2,128)} %broadcast_in_dim.8), calls=%async_computation | async-start | bytes 65536 | tf_op jit(solution)/shard_map/all_to_all | solution.py:16
  29.7 29.6 %collective-permute-start = (bf16[1024,512]{1,0:T(8,128)(2,1)S(1)}, bf16[1024,512]{1,0:T(8,128)(2,1)}, u32[]{:S(2)}, u32[]{:S(2)}) collective-permute-start(bf16[1024,512]{1,0:T(8,128)(2,1)S(1)} %copy-done.3), channel_id=1, source_target_pairs={{0,1},{1,0},{2,3},{3,2},{4,5},{5,4},{6,7},{7,6},{8,9},{9,8},{10,11... | collective-permute-start | bytes 3145736 | tf_op jit(solution)/shard_map/ppermute | solution.py:107
  41.7 17.6 %all-to-all-start.1 = ((bf16[8,512,128]{1,2,0:T(8,128)(2,1)}), bf16[8,512,128]{1,2,0:T(8,128)(2,1)S(1)}, u32[]{:S(2)}, u32[]{:S(2)}) async-start(bf16[8,512,128]{1,2,0:T(8,128)(2,1)} %bitcast.56), calls=%async_computation.1 | async-start | bytes 2097152 | tf_op jit(solution)/shard_map/all_to_all | solution.py:57
  46.5 1.2 collective-permute-start.1
  46.6 25.0 %collective-permute-start.2 = (bf16[512,1024]{1,0:T(8,128)(2,1)}, bf16[512,1024]{1,0:T(8,128)(2,1)}, u32[]{:S(2)}, u32[]{:S(2)}) collective-permute-start(bf16[512,1024]{1,0:T(8,128)(2,1)} %param.17), channel_id=1, source_target_pairs={{0,1},{1,0},{2,3},{3,2},{4,5},{5,4},{6,7},{7,6},{8,9},{9,8},{10,11... | collective-permute-start | bytes 3145736 | tf_op jit(solution)/shard_map/ppermute | solution.py:108
  77.7 37.1 %collective-permute-start.3 = (bf16[1024,1024]{0,1:T(8,128)(2,1)}, bf16[1024,1024]{0,1:T(8,128)(2,1)}, u32[]{:S(2)}, u32[]{:S(2)}) collective-permute-start(bf16[1024,1024]{0,1:T(8,128)(2,1)} %pad_maximum_fusion), channel_id=1, source_target_pairs={{0,1},{1,0},{2,3},{3,2},{4,5},{5,4},{6,7},{7,6},{8,9},{9,8},{10,11... | collective-permute-start | bytes 6291464 | tf_op jit(solution)/shard_map/ppermute | solution.py:164
  81.8 20.2 %all-to-all-start.2 = ((bf16[8,512,128]{2,1,0:T(8,128)(2,1)}), bf16[8,512,128]{2,1,0:T(8,128)(2,1)}, u32[]{:S(2)}, u32[]{:S(2)}) async-start(bf16[8,512,128]{2,1,0:T(8,128)(2,1)} %bitcast.240), calls=%async_computation.2 | async-start | bytes 2097152 | tf_op jit(solution)/shard_map/all_to_all | solution.py:65
  102.0 20.2 %all-to-all-start.3 = ((bf16[8,512,128]{2,1,0:T(8,128)(2,1)}), bf16[8,512,128]{2,1,0:T(8,128)(2,1)}, u32[]{:S(2)}, u32[]{:S(2)}) async-start(bf16[8,512,128]{2,1,0:T(8,128)(2,1)} %bitcast_bitcast_fusion), calls=%async_computation.3 | async-start | bytes 2097152 | tf_op jit(solution)/shard_map/all_to_all | solution.py:65
  109.2 70.0 %reduce-scatter.4.cloned.1.call-start = ((), (), s32[]{:S(2)}) async-start(), calls=%async_computation.9 | async-start | bytes 2359296
  111.3 1.3 collective-permute-start.4
  125.1 14.3 %all-to-all-start.4 = ((f32[32,2,128]{2,1,0:T(2,128)}), f32[32,2,128]{2,1,0:T(2,128)S(1)}, u32[]{:S(2)}, u32[]{:S(2)}) async-start(f32[32,2,128]{2,1,0:T(2,128)} %broadcast_in_dim.10), calls=%async_computation.4 | async-start | bytes 65536 | tf_op jit(solution)/shard_map/all_to_all | solution.py:16
  144.1 40.8 %copy-start.13 = (f32[128]{0:T(128)S(1)}, f32[128]{0:T(128)}, u32[]{:S(2)}) copy-start(f32[128]{0:T(128)} %copy-done.12) | copy-start | bytes 1540
  144.2 40.8 %copy-start.15 = (f32[128]{0:T(128)S(1)}, f32[128]{0:T(128)}, u32[]{:S(2)}) copy-start(f32[128]{0:T(128)} %copy-done.14) | copy-start | bytes 1540
  144.2 40.8 %copy-start.17 = (f32[128]{0:T(128)S(1)}, f32[128]{0:T(128)}, u32[]{:S(2)}) copy-start(f32[128]{0:T(128)} %copy-done.16) | copy-start | bytes 1540
  144.2 40.8 %copy-start.19 = (f32[128]{0:T(128)S(1)}, f32[128]{0:T(128)}, u32[]{:S(2)}) copy-start(f32[128]{0:T(128)} %copy-done.18) | copy-start | bytes 1540
  144.2 40.8 %copy-start.21 = (f32[128]{0:T(128)S(1)}, f32[128]{0:T(128)}, u32[]{:S(2)}) copy-start(f32[128]{0:T(128)} %copy-done.20) | copy-start | bytes 1540
  144.2 40.8 %copy-start.23 = (f32[128]{0:T(128)S(1)}, f32[128]{0:T(128)}, u32[]{:S(2)}) copy-start(f32[128]{0:T(128)} %copy-done.22) | copy-start | bytes 1540
  144.2 40.8 %copy-start.25 = (f32[128]{0:T(128)S(1)}, f32[128]{0:T(128)}, u32[]{:S(2)}) copy-start(f32[128]{0:T(128)} %copy-done.24) | copy-start | bytes 1540
  144.2 40.8 %copy-start.27 = (f32[128]{0:T(128)S(1)}, f32[128]{0:T(128)}, u32[]{:S(2)}) copy-start(f32[128]{0:T(128)} %copy-done.26) | copy-start | bytes 1540
  144.2 40.8 %copy-start.29 = (f32[128]{0:T(128)S(1)}, f32[128]{0:T(128)}, u32[]{:S(2)}) copy-start(f32[128]{0:T(128)} %copy-done.28) | copy-start | bytes 1540
  144.2 40.8 %copy-start.31 = (f32[128]{0:T(128)S(1)}, f32[128]{0:T(128)}, u32[]{:S(2)}) copy-start(f32[128]{0:T(128)} %copy-done.30) | copy-start | bytes 1540
  144.2 40.8 %copy-start.33 = (f32[128]{0:T(128)S(1)}, f32[128]{0:T(128)}, u32[]{:S(2)}) copy-start(f32[128]{0:T(128)} %copy-done.32) | copy-start | bytes 1540
  181.2 10.4 %all-to-all-start.6 = ((bf16[4,32,1024]{2,1,0:T(8,128)(2,1)}), bf16[4,32,1024]{2,1,0:T(8,128)(2,1)S(1)}, u32[]{:S(2)}, u32[]{:S(2)}) async-start(bf16[4,32,1024]{2,1,0:T(8,128)(2,1)} %bitcast.127), calls=%async_computation.6 | async-start | bytes 524288 | tf_op jit(solution)/shard_map/all_to_all | solution.py:187
  (46 other events, 932.0 us)
Sparse Core Ops, SparseCore 0:
  10.5 29.8 all-gather.1
  124.3 54.0 reduce-scatter.3

commit v3 on v2

v3 whole, which is shorter than its diff:
```python
import jax
import jax.numpy as jnp
from jax import lax
from jax.experimental import pallas as pl
from jax.experimental.pallas import tpu as pltpu
from jax.sharding import Mesh
from jax.sharding import PartitionSpec as P


KS = 7
DP = ("z", "y")
CH = ("x", "c")
SWAP = [(0, 1), (1, 0)]
EPS = 1e-05


def sent_to_all(array, axis):
    size = lax.axis_size(axis)
    return lax.all_to_all(
        jnp.broadcast_to(array[None], (size, *array.shape)), axis, 0, 0, tiled=True
    )


def rows_of_all(array):
    rows, own = array.shape
    halves = jnp.broadcast_to(array.reshape(1, 2, rows // 2, own), (4, 2, rows // 2, own))
    return lax.all_to_all(halves.reshape(8, rows // 2, own), CH, 0, 0, tiled=True)


def exchanged(pieces):
    _, rows, own = pieces.shape
    return lax.all_to_all(pieces, CH, 0, 0, tiled=True).reshape(4, 2 * rows, own)


def summed(pieces):
    return jnp.sum(pieces.astype(jnp.float32), axis=0)


REACH = KS // 2
TAPS = KS * KS


def spread(field, pad, planes):
    height, width, lanes = field.shape
    pad[:, :8] = jnp.zeros((height, 8, lanes), jnp.float32)
    pad[:, width + 8 :] = jnp.zeros((height, 8, lanes), jnp.float32)
    edge = jnp.zeros((KS, REACH, width, lanes), jnp.float32)
    planes[:, :REACH] = edge
    planes[:, height + REACH :] = edge

    @pl.loop(0, height)
    def _(r):
        pad[r, 8 : width + 8] = field[r].astype(jnp.float32)
        for b in range(KS):
            planes[b, r + REACH] = pad[r, 8 - REACH + b : 8 - REACH + b + width]


def filtered_row(planes, kernel, r, reverse=False):
    total = None
    for a in range(KS):
        for b in range(KS):
            tap = a * KS + b
            tap = TAPS - 1 - tap if reverse else tap
            term = planes[b, r + a] * kernel[tap : tap + 1]
            total = term if total is None else total + term
    return total


def folded(value):
    return jnp.sum(value.reshape(-1, 8, value.shape[-1]), axis=0)


def tap_sums(planes, upstream, height, out, plain=None):
    out[...] = jnp.zeros_like(out)
    if plain is not None:
        plain[...] = jnp.zeros_like(plain)
    zero = jnp.zeros((8, out.shape[1]), jnp.float32)
    for b in range(KS):

        def step(r, sums):
            u = upstream(r)
            sums = list(sums)
            for a in range(KS):
                window = planes[b, r + a]
                sums[a] = sums[a] + folded(window * u)
                if plain is not None:
                    sums[KS + a] = sums[KS + a] + folded(window)
            return tuple(sums)

        sums = lax.fori_loop(0, height, step, (zero,) * (KS if plain is None else 2 * KS))
        for a in range(KS):
            tap = a * KS + b
            out[tap : tap + 1] = jnp.sum(sums[a], axis=0, keepdims=True)
            if plain is not None:
                plain[tap : tap + 1] = jnp.sum(sums[KS + a], axis=0, keepdims=True)


def filter_kernel(source, kernel, filtered, moments, pad, planes):
    spread(source, pad, planes)
    zero = jnp.zeros((8, kernel.shape[1]), jnp.float32)

    def step(r, sums):
        row = filtered_row(planes, kernel, r)
        filtered[r] = row
        return sums[0] + folded(row), sums[1] + folded(row * row)

    sums = lax.fori_loop(0, source.shape[0], step, (zero, zero))
    for i in range(2):
        moments[i : i + 1] = jnp.sum(sums[i], axis=0, keepdims=True)


def terms_kernel(source, filtered, mean, of_flat, of_rest, pad, planes):
    spread(source, pad, planes)
    tap_sums(planes, lambda r: filtered[r] - mean[...], source.shape[0], of_rest, of_flat)


def gather_kernel(pieces, source, filtered, mean, rstd, d_normed, of_normed, sums, pad, planes):
    height, width, lanes = source.shape
    spread(source, pad, planes)
    zero = jnp.zeros((8, lanes), jnp.float32)

    def step(r, carry):
        rows = pl.ds(pl.multiple_of(r * width, width), width)
        row = pieces[0, rows].astype(jnp.float32)
        for x in range(1, 4):
            row = row + pieces[x, rows].astype(jnp.float32)
        d_normed[r] = row
        centered = (filtered[r] - mean[...]) * rstd[...]
        return carry[0] + folded(row * centered), carry[1] + folded(row)

    carry = lax.fori_loop(0, height, step, (zero, zero))
    for i in range(2):
        sums[i : i + 1] = jnp.sum(carry[i], axis=0, keepdims=True)
    tap_sums(planes, lambda r: d_normed[r], height, of_normed)


def input_kernel(d_normed, filtered, cotangent, kernel, rows, d_input, field, pad, planes):
    height = d_normed.shape[0]
    mean, rstd, scaled, shift, slope = (rows[i : i + 1] for i in range(5))

    @pl.loop(0, height)
    def _(r):
        centered = (filtered[r] - mean) * rstd
        field[r] = scaled * (d_normed[r] - shift - centered * slope)

    spread(field, pad, planes)

    @pl.loop(0, height)
    def _(r):
        row = filtered_row(planes, kernel, r, reverse=True)
        d_input[r] = (cotangent[r].astype(jnp.float32) + row).astype(jnp.bfloat16)


def conv_scratch(shape):
    height, width, lanes = shape
    return (
        pltpu.VMEM((height, width + 16, lanes), jnp.float32),
        pltpu.VMEM((KS, height + 2 * REACH, width, lanes), jnp.float32),
    )


GELU_A = 0.7978845608028654
GELU_B = 0.044715
TILE = 256
DOT_ROWS = (((0,), (0,)), ((), ()))
DOT_PLAIN = (((1,), (0,)), ((), ()))
DOT_COLS = (((1,), (1,)), ((), ()))


def dot(a, b, dims):
    return lax.dot_general(a, b, dims, preferred_element_type=jnp.float32)


def kernel_call(kernel, outs, operands, flops, scalar=False, scratch=()):
    vmem = pl.BlockSpec(memory_space=pltpu.VMEM)
    specs = [vmem] * len(operands)
    if scalar:
        specs[0] = pl.BlockSpec(memory_space=pltpu.SMEM)
    return pl.pallas_call(
        kernel,
        out_shape=[jax.ShapeDtypeStruct(s, t) for s, t in outs],
        in_specs=specs,
        out_specs=[vmem] * len(outs),
        scratch_shapes=list(scratch),
        cost_estimate=pl.CostEstimate(flops=flops, bytes_accessed=8 << 20, transcendentals=0),
        compiler_params=pltpu.CompilerParams(vmem_limit_bytes=24 << 20),
    )(*operands)


def joined(pieces, start, size):
    return jnp.concatenate([pieces[k, pl.ds(start, size)] for k in range(8)], axis=1)


def up_kernel(z, w_own, w_pair, b_own, b_pair, v_own, v_pair, slope_o, slope_p, act_o, act_p, out):
    @pl.loop(0, z.shape[1] // TILE)
    def _(m):
        start = pl.multiple_of(m * TILE, TILE)
        rows = pl.ds(start, TILE)
        x = joined(z, start, TILE)
        for w, b, slope, act in ((w_own, b_own, slope_o, act_o), (w_pair, b_pair, slope_p, act_p)):
            hidden = dot(x, w[...], DOT_PLAIN) + b[...]
            square = hidden * hidden
            t = jnp.tanh(GELU_A * (hidden + GELU_B * (square * hidden)))
            half = 0.5 * (1.0 + t)
            act[rows] = (hidden * half).astype(jnp.bfloat16)
            slope[rows] = half + (0.5 * GELU_A) * hidden * (1.0 - t * t) * (
                1.0 + 3.0 * GELU_B * square
            )
        total = dot(act_o[rows], v_own[...], DOT_PLAIN) + dot(act_p[rows], v_pair[...], DOT_PLAIN)
        for k in range(8):
            out[k, rows] = total[:, k * 128 : (k + 1) * 128].astype(jnp.bfloat16)


def down_kernel(
    core, y, slope_o, slope_p, w_own, w_pair, v_own, v_pair, back_o, back_p, bias_o, bias_p, out
):
    half = slope_o.shape[0]
    bias_o[...] = jnp.zeros_like(bias_o)
    bias_p[...] = jnp.zeros_like(bias_p)

    @pl.loop(0, half // TILE)
    def _(m):
        start = pl.multiple_of(m * TILE, TILE)
        rows = pl.ds(start, TILE)
        up = joined(y, pl.multiple_of(core[0] * half + start, TILE), TILE)
        for v, slope, back, bias in (
            (v_own, slope_o, back_o, bias_o),
            (v_pair, slope_p, back_p, bias_p),
        ):
            grad = dot(up, v[...], DOT_COLS) * slope[rows]
            bias[...] += jnp.sum(grad, axis=0, keepdims=True)
            back[rows] = grad.astype(jnp.bfloat16)
        total = dot(back_o[rows], w_own[...], DOT_COLS) + dot(back_p[rows], w_pair[...], DOT_COLS)
        for k in range(8):
            out[k, rows] = total[:, k * 128 : (k + 1) * 128].astype(jnp.bfloat16)


def weight_kernel(core, z, y, back, act, out):
    half, width = back.shape
    rows = pl.ds(pl.multiple_of(core[0] * half, half), half)

    @pl.loop(0, 4)
    def _(k):
        here = pl.ds(pl.multiple_of(k * 256, 256), 256)
        x = jnp.concatenate([z[2 * k], z[2 * k + 1]], axis=1)
        up = jnp.concatenate([y[2 * k, rows], y[2 * k + 1, rows]], axis=1)
        for a, b, cols in ((x, back, pl.ds(0, width)), (up, act, pl.ds(width, width))):
            out[here, cols] = dot(a, b[...], DOT_ROWS).astype(out.dtype)


def up_pass(z, w_own, w_pair, b_own, b_pair, v_own, v_pair):
    rows, width = z.shape[1], w_own.shape[1]
    return kernel_call(
        up_kernel,
        [((rows, width), jnp.float32)] * 2
        + [((rows, width), jnp.bfloat16)] * 2
        + [(z.shape, jnp.bfloat16)],
        (z, w_own, w_pair, b_own[None], b_pair[None], v_own, v_pair),
        8 * rows * width * 1024,
    )


def down_pass(core, y, slope_o, slope_p, w_own, w_pair, v_own, v_pair):
    rows, width = slope_o.shape
    return kernel_call(
        down_kernel,
        [((rows, width), jnp.bfloat16)] * 2
        + [((1, width), jnp.float32)] * 2
        + [((8, rows, 128), jnp.bfloat16)],
        (core, y, slope_o, slope_p, w_own, w_pair, v_own, v_pair),
        8 * rows * width * 1024,
        scalar=True,
    )


def weight_pass(kind, *operands):
    rows, width = operands[3].shape
    return kernel_call(
        weight_kernel,
        [((1024, 2 * width), kind)],
        operands,
        4 * rows * width * 1024,
        scalar=True,
    )[0]


def body(
    activations,
    cotangent,
    dw_kernel,
    norm_gain,
    norm_bias,
    w_in,
    b_in,
    w_out,
    layer_scale,
    group_sizes,
):
    channels = activations.shape[3]
    row_count = activations.shape[1] * activations.shape[2]
    core = lax.axis_index("c")
    devices = lax.axis_size(DP)
    position = lax.axis_index(DP)
    groups = group_sizes.shape[0]
    group_ends = jnp.cumsum(group_sizes)
    positions = jnp.arange(devices, dtype=jnp.int32)
    labels = jnp.sum((group_ends[None, :] <= positions[:, None]).astype(jnp.int32), axis=1)
    own_group = jnp.sum((group_ends <= position).astype(jnp.int32))
    owners = (jnp.arange(groups, dtype=jnp.int32)[:, None] == labels[None, :]).astype(jnp.float32)
    member = (jnp.arange(groups, dtype=jnp.int32) == own_group).astype(jnp.float32)
    own_count = jnp.sum(member * group_sizes.astype(jnp.float32)) * row_count
    own_gain = jnp.sum(member[:, None] * norm_gain, axis=0)
    own_bias = jnp.sum(member[:, None] * norm_bias, axis=0)

    incoming = cotangent.reshape(row_count, channels).astype(jnp.float32)
    d_branch = (incoming * layer_scale).astype(jnp.bfloat16)
    everyone = lax.all_gather(d_branch, CH, axis=0, tiled=False)
    w_in_pair = lax.ppermute(w_in, "c", SWAP)
    w_out_pair = lax.ppermute(w_out, "c", SWAP)
    b_in_pair = lax.ppermute(b_in, "c", SWAP)

    image = activations.shape[1:]
    source = activations[0]
    scratch = conv_scratch(image)
    filtered, moments = kernel_call(
        filter_kernel,
        [(image, jnp.float32), ((2, channels), jnp.float32)],
        (source, dw_kernel),
        1 << 29,
        scratch=scratch,
    )
    per_device = sent_to_all(moments, DP)
    counts = group_sizes.astype(jnp.float32)[:, None] * row_count
    totals = jnp.sum(owners[:, :, None, None] * per_device[None], axis=1)
    group_mean = totals[:, 0] / counts
    group_rstd = lax.rsqrt(totals[:, 1] / counts - group_mean * group_mean + EPS)
    own_mean = jnp.sum(member[:, None] * group_mean, axis=0)
    own_rstd = jnp.sum(member[:, None] * group_rstd, axis=0)
    centered = (filtered.reshape(row_count, channels) - own_mean) * own_rstd
    normed = (centered * own_gain + own_bias).astype(jnp.bfloat16)
    gathered = rows_of_all(normed)

    slope_own, slope_pair, active_own, active_pair, partial_branch = up_pass(
        gathered, w_in, w_in_pair, b_in, b_in_pair, w_out, w_out_pair
    )
    branch_pieces = exchanged(partial_branch)
    branch = summed(branch_pieces)
    initial = activations.reshape(row_count, channels).astype(jnp.float32)
    result = (initial + layer_scale * branch).astype(jnp.bfloat16).reshape(activations.shape)
    scale_local = jnp.sum(incoming * branch, axis=0)

    where = core.astype(jnp.int32)[None]
    back_own, back_pair, bias_own, bias_pair, partial_normed = down_pass(
        where, everyone, slope_own, slope_pair, w_in, w_in_pair, w_out, w_out_pair
    )
    for_pair = weight_pass(jnp.bfloat16, where, gathered, everyone, back_pair, active_pair)
    from_pair = lax.ppermute(for_pair, "c", SWAP)
    own_grads = weight_pass(jnp.float32, where, gathered, everyone, back_own, active_own)
    both_local = (own_grads + from_pair.astype(jnp.float32)).astype(jnp.bfloat16)
    hidden_cols = w_in.shape[1]
    bias_local = bias_own + lax.ppermute(bias_pair, "c", SWAP)
    image_mean = moments[:1] / row_count
    of_flat, of_rest = kernel_call(
        terms_kernel,
        [((64, channels), jnp.float32)] * 2,
        (source, filtered, image_mean),
        1 << 29,
        scratch=scratch,
    )
    partial_normed, branch_pieces, both_local = lax.optimization_barrier(
        (partial_normed, branch_pieces, both_local)
    )
    near = lax.psum_scatter(both_local, "z", scatter_dimension=0, tiled=True)
    normed_pieces = exchanged(partial_normed)

    from_mean = per_device[:, 0] / row_count - jnp.sum(
        owners[:, :, None] * group_mean[:, None], axis=0
    )
    normed_pieces, of_flat, of_rest = lax.optimization_barrier((normed_pieces, of_flat, of_rest))
    d_normed, of_normed, grad_moments = kernel_call(
        gather_kernel,
        [(image, jnp.float32), ((64, channels), jnp.float32), ((2, channels), jnp.float32)],
        (normed_pieces, source, filtered, own_mean[None], own_rstd[None]),
        1 << 29,
        scratch=scratch,
    )
    own_scaled = own_gain * own_rstd
    others = jnp.concatenate(
        [bias_local.reshape(4, channels), scale_local[None], jnp.zeros((64 - TAPS - 5, channels))]
    )
    firsts = jnp.concatenate([own_scaled * of_normed[:TAPS], others])
    local = jnp.stack([a.reshape(devices, 2, channels) for a in (firsts, of_flat, of_rest)], axis=1)
    sent = jnp.concatenate(
        [
            local.reshape(devices, 6, channels),
            jnp.broadcast_to(grad_moments[None], (devices, 2, channels)),
        ],
        axis=1,
    )
    parts = lax.all_to_all(sent, DP, 0, 0, tiled=True)
    grad_totals = jnp.sum(owners[:, :, None, None] * parts[None, :, 6:], axis=1)
    d_gain = grad_totals[:, 0]
    d_bias = grad_totals[:, 1]
    from_mean = per_device[:, 0] / row_count - jnp.sum(
        owners[:, :, None] * group_mean[:, None], axis=0
    )
    rest_parts = parts[:, 4:6] + from_mean[:, None] * parts[:, 2:4]
    scaled_all = norm_gain * group_rstd / counts
    flat_weight = jnp.sum(owners[:, :, None] * (scaled_all * d_bias)[:, None], axis=0)
    rest_weight = jnp.sum(
        owners[:, :, None] * (scaled_all * group_rstd * d_gain)[:, None], axis=0
    )
    piece = jnp.sum(
        parts[:, :2]
        - flat_weight[:, None] * parts[:, 2:4]
        - rest_weight[:, None] * rest_parts,
        axis=0,
    )
    total = sent_to_all(piece, DP).reshape(64, channels)
    near, total = lax.optimization_barrier((near, total))
    d_kernel = total[:TAPS]
    d_b_in = total[TAPS : TAPS + 4].ravel()
    d_scale = total[TAPS + 4]
    own_dgain = jnp.sum(member[:, None] * d_gain, axis=0)
    own_dbias = jnp.sum(member[:, None] * d_bias, axis=0)
    rows = jnp.stack(
        [own_mean, own_rstd, own_scaled, own_dbias / own_count, own_dgain / own_count]
    )
    everything = lax.all_to_all(near.reshape(4, -1, near.shape[1]), "y", 0, 0, tiled=True)
    both_sums = jnp.sum(everything.astype(jnp.float32), axis=0)
    d_w_in = both_sums[:, :hidden_cols]
    d_w_out = both_sums[:, hidden_cols:].T
    (d_input,) = kernel_call(
        input_kernel,
        [(image, jnp.bfloat16)],
        (d_normed, filtered, cotangent[0], dw_kernel, rows),
        1 << 29,
        scratch=(pltpu.VMEM(image, jnp.float32), *scratch),
    )
    d_input = d_input[None]
    return (result, d_input, d_kernel, d_gain, d_bias, d_w_in, d_b_in, d_w_out, d_scale)


def solution(mesh):
    split = Mesh(mesh.devices.reshape(8, 4, 4, 2), ("z", "y", "x", "c"))
    in_specs = (
        P(DP, None, None, CH),
        P(DP, None, None, CH),
        P(None, CH),
        P(None, CH),
        P(None, CH),
        P(None, CH),
        P(CH),
        P(CH, None),
        P(CH),
        P(),
    )
    out_specs = (
        P(DP, None, None, CH),
        P(DP, None, None, CH),
        P(None, CH),
        P(None, CH),
        P(None, CH),
        P(DP, CH),
        P(CH),
        P(CH, DP),
        P(CH),
    )
    return jax.shard_map(body, mesh=split, in_specs=in_specs, out_specs=out_specs, check_vma=False)
```

time: 203 us -> 173 us (0.85)
  blocking collectives: 33.8 us -> 0 us
  Pallas kernels: 0 us -> 30.6 us
  matrix products: 21.7 us -> 0 us
  other arithmetic: 29.9 us -> 12.8 us
  waiting for transfers between devices: 37.9 us -> 51.1 us
  starting transfers between devices: 39.8 us -> 42.6 us
  local copies, waits for them, and re-layouts: 20.5 us -> 18.1 us
    all_to_all x1 -> x0, blocking collectives: 33.8 us -> none  [sent_to_all(): lax.all_to_all(jnp.broadcast_to(array[None], (size, *array.shape)), axis,...]
    pallas_call x0 -> x8, Pallas kernels: none -> 30.6 us  [kernel_call(): pl.pallas_call(kernel, out_shape=[jax.ShapeDtypeStruct(s, t) for s, t in...]
    dot_general x12 -> x0, matrix products: 21.7 us -> none  [the longest x8 13.6 us: dot(): return lax.dot_general(a, b, dims, preferred_element_type=jnp.float32)]
    reduce_sum x10 -> x5, other arithmetic: 9.35 us -> 0.45 us  [the longest x1 0.11 us: body(): own_mean = jnp.sum(member[:, None] * group_mean, axis=0)]
    all_to_all x0 -> x1, waiting for transfers between devices: none -> 8.88 us  [body(): parts = lax.all_to_all(sent, DP, 0, 0, tiled=True)]
    unnamed x116 -> x60, local copies, waits for them, and re-layouts: 5.57 us -> 12.5 us
    all_to_all x1, waiting for transfers between devices: 0.3 us -> 6.13 us  [body(): lax.all_to_all(near.reshape(4, -1, near.shape[1]), 'y', 0, 0, tiled=True)]
    all_to_all x0 -> x1, starting transfers between devices: none -> 3.86 us  [body(): parts = lax.all_to_all(sent, DP, 0, 0, tiled=True)]
  transfers between devices with their start and end apart: 13 -> 14, of which waited for: 8 -> 9; matrix products, arithmetic and copies ran while one was open for 30% -> 9% of each run, Pallas kernels for 0% -> 13%
where the time goes in v3:
time: 173 us; the launch traced here: 170 us
  waiting for transfers between devices  51.1 us (30%)
  starting transfers between devices  42.6 us (25%)
  Pallas kernels  30.6 us (18%)
  local copies, waits for them, and re-layouts  18.1 us (10%)
  between operations  15.1 us (9%)
  other arithmetic  12.8 us (7%)
    pallas_call x8, Pallas kernels, kernel_call(): pl.pallas_call(kernel, out_shape=[jax.ShapeDtypeStruct(s, t) for s, t in...  30.6 us
    all_to_all x2, starting transfers between devices, sent_to_all(): lax.all_to_all(jnp.broadcast_to(array[None], (size, *array.shape)), axis,...  15.5 us
    all_to_all x2, starting transfers between devices, exchanged(): lax.all_to_all(pieces, CH, 0, 0, tiled=True).reshape(4, 2 * rows, own)  14.1 us
    unnamed x60, local copies, waits for them, and re-layouts  12.5 us
    all_to_all x2, waiting for transfers between devices, sent_to_all(): lax.all_to_all(jnp.broadcast_to(array[None], (size, *array.shape)), axis,...  12.4 us
    all_to_all x1, waiting for transfers between devices, rows_of_all(): lax.all_to_all(halves.reshape(8, rows // 2, own), CH, 0, 0, tiled=True)  11.6 us
    all_to_all x2, waiting for transfers between devices, exchanged(): lax.all_to_all(pieces, CH, 0, 0, tiled=True).reshape(4, 2 * rows, own)  10.1 us
    all_to_all x1, waiting for transfers between devices, body(): parts = lax.all_to_all(sent, DP, 0, 0, tiled=True)  8.88 us
  transfers between devices with their start and end apart: 14, of which 9 were waited for; matrix products, arithmetic and copies ran while one was open for 9% of the time, Pallas kernels for 13%

profile of v3, /device:TPU:4, one launch (start us, length us, event | category | flops | bytes accessed | tf_op | source)
XLA Modules:
  0.0 170.4 jit_solution(6618261090777552102)
XLA Ops:
  7.2 1.9 %fusion = bf16[1,1024,128]{2,1,0:T(8,128)(2,1)} fusion(f32[128]{0:T(128)} %param.18, bf16[1,16,64,128]{3,2,1,0:T(8,128)(2,1)} %param.11), kind=kLoop, calls=%fused_computation.3 | loop fusion | flops 393216 | bytes 524800 | tf_op jit(solution)/shard_map/convert_element_type | solution.py:316
  10.8 3.4 %shard_map.169 = (f32[16,64,128]{2,1,0:T(8,128)S(1)}, f32[2,128]{1,0:T(2,128)S(1)}) custom-call(bf16[16,64,128]{2,1,0:T(8,128)(2,1)S(1)} %bitcast.73, f32[49,128]{1,0:T(8,128)S(1)} %copy-done.20), custom_call_target="tpu_custom_call" | custom-call | flops 536870912 | bytes 8388608 | tf_op jit(solution)/shard_map/pallas_call | solution.py:179
  14.9 11.5 %all-to-all-start = ((f32[32,2,128]{2,1,0:T(2,128)}), f32[32,2,128]{2,1,0:T(2,128)S(1)}, u32[]{:S(2)}, u32[]{:S(2)}) async-start(f32[32,2,128]{2,1,0:T(2,128)} %broadcast_in_dim.24), calls=%async_computation | async-start | bytes 65536 | tf_op jit(solution)/shard_map/all_to_all | solution.py:19
  29.8 6.4 %all-to-all-done = f32[32,2,128]{2,1,0:T(2,128)S(1)} async-done(((f32[32,2,128]{2,1,0:T(2,128)}), f32[32,2,128]{2,1,0:T(2,128)S(1)}, u32[]{:S(2)}, u32[]{:S(2)}) %all-to-all-start) | async-done | bytes 32800 | tf_op jit(solution)/shard_map/all_to_all | solution.py:19
  37.7 4.8 %all-to-all-start.1 = ((bf16[8,512,128]{2,1,0:T(8,128)(2,1)}), bf16[8,512,128]{2,1,0:T(8,128)(2,1)S(1)}, u32[]{:S(2)}, u32[]{:S(2)}) async-start(bf16[8,512,128]{2,1,0:T(8,128)(2,1)} %bitcast.85), calls=%async_computation.1 | async-start | bytes 2097152 | tf_op jit(solution)/shard_map/all_to_all | solution.py:27
  43.7 11.6 %all-to-all-done.1.z = bf16[8,512,128]{2,1,0:T(8,128)(2,1)S(1)} async-done(((bf16[8,512,128]{2,1,0:T(8,128)(2,1)}), bf16[8,512,128]{2,1,0:T(8,128)(2,1)S(1)}, u32[]{:S(2)}, u32[]{:S(2)}) %all-to-all-start.1) | async-done | bytes 1048608 | tf_op jit(solution)/shard_map/all_to_all | solution.py:27
  55.3 5.2 %shard_map.170 = (f32[512,512]{1,0:T(8,128)S(1)}, f32[512,512]{1,0:T(8,128)S(1)}, bf16[512,512]{1,0:T(8,128)(2,1)S(1)}, bf16[512,512]{1,0:T(8,128)(2,1)S(1)}, bf16[8,512,128]{2,1,0:T(8,128)(2,1)S(1)}) custom-call(bf16[8,512,128]{2,1,0:T(8,128)(2,1)S(1)} %all-to-all-done.1.z, bf16[1024,512]{1,0:T(8,128)(2,1)S(1)} %copy-done.2, ...), custom_call_target="tpu_custom_call" | custom-call | flops 2147483648 | bytes 8388608 | tf_op jit(solution)/shard_map/pallas_call | solution.py:179
  69.2 5.4 %shard_map.171 = (bf16[512,512]{1,0:T(8,128)(2,1)S(1)}, bf16[512,512]{1,0:T(8,128)(2,1)S(1)}, f32[1,512]{1,0:T(1,128)S(1)}, f32[1,512]{1,0:T(1,128)S(1)}, bf16[8,512,128]{2,1,0:T(8,128)(2,1)}) custom-call(s32[1]{0:T(128)} %bitcast.11.core, bf16[8,1024,128]{2,1,0:T(8,128)(2,1)S(1)} %copy-done, f32[512,512]{1,0:T(8,128)S(1)} %copy-done.5, ...), custom_call_target="tpu_custom_call" | custom-call | flops 2147483648 | bytes 8388608 | tf_op jit(solution)/shard_map/pallas_call | solution.py:179
  74.5 3.2 %shard_map.173 = bf16[1024,1024]{1,0:T(8,128)(2,1)} custom-call(s32[1]{0:T(128)} %bitcast.11.core, bf16[8,512,128]{2,1,0:T(8,128)(2,1)S(1)} %all-to-all-done.1.z, bf16[8,1024,128]{2,1,0:T(8,128)(2,1)S(1)} %copy-done, bf16[512,512]{1,0:T(8,128)(2,1)S(1)} %get-tuple-element.41.back, bf16[512,512]{1,0:T(8,128)(2,1)S(1)} %copy-done.15), custom_call_target="tpu_custom_call" | custom-call | flops 1073741824 | bytes 8388608 | tf_op jit(solution)/shard_map/pallas_call | solution.py:179
  77.8 7.4 %all-to-all-start.2 = ((bf16[8,512,128]{2,1,0:T(8,128)(2,1)}), bf16[8,512,128]{2,1,0:T(8,128)(2,1)}, u32[]{:S(2)}, u32[]{:S(2)}) async-start(bf16[8,512,128]{2,1,0:T(8,128)(2,1)} %copy-done.8), calls=%async_computation.2 | async-start | bytes 2097152 | tf_op jit(solution)/shard_map/all_to_all | solution.py:32
  87.3 1.9 %shard_map.172 = f32[1024,1024]{1,0:T(8,128)S(1)} custom-call(s32[1]{0:T(128)} %bitcast.11.core, bf16[8,512,128]{2,1,0:T(8,128)(2,1)S(1)} %all-to-all-done.1.z, bf16[8,1024,128]{2,1,0:T(8,128)(2,1)S(1)} %copy-done.1, bf16[512,512]{1,0:T(8,128)(2,1)S(1)} %copy-done.13, bf16[512,512]{1,0:T(8,128)(2,1)S(1)} %copy-done.11), custom_call_target="tpu_custom_call" | custom-call | flops 1073741824 | bytes 8388608 | tf_op jit(solution)/shard_map/pallas_call | solution.py:179
  89.3 3.8 %add_convert_fusion = bf16[1024,1024]{1,0:T(8,128)(2,1)} fusion(f32[1024,1024]{1,0:T(8,128)S(1)} %shard_map.172, bf16[1024,1024]{1,0:T(8,128)(2,1)} %collective-permute-done.3), kind=kLoop, calls=%fused_computation | loop fusion | flops 3145728 | bytes 8388608 | tf_op jit(solution)/shard_map/convert_element_type | solution.py:359
  93.1 5.0 %all-to-all-done.2 = bf16[8,512,128]{2,1,0:T(8,128)(2,1)} async-done(((bf16[8,512,128]{2,1,0:T(8,128)(2,1)}), bf16[8,512,128]{2,1,0:T(8,128)(2,1)}, u32[]{:S(2)}, u32[]{:S(2)}) %all-to-all-start.2) | async-done | bytes 1048608 | tf_op jit(solution)/shard_map/all_to_all | solution.py:32
  98.1 6.6 %all-to-all-start.3 = ((bf16[8,512,128]{2,1,0:T(8,128)(2,1)}), bf16[8,512,128]{2,1,0:T(8,128)(2,1)S(1)}, u32[]{:S(2)}, u32[]{:S(2)}) async-start(bf16[8,512,128]{2,1,0:T(8,128)(2,1)} %get-tuple-element.43), calls=%async_computation.3 | async-start | bytes 2097152 | tf_op jit(solution)/shard_map/all_to_all | solution.py:32
  105.5 4.1 %shard_map.174 = (f32[64,128]{1,0:T(8,128)S(1)}, f32[64,128]{1,0:T(8,128)S(1)}) custom-call(bf16[16,64,128]{2,1,0:T(8,128)(2,1)S(1)} %bitcast.74, f32[16,64,128]{2,1,0:T(8,128)S(1)} %copy-done.17, f32[1,128]{1,0:T(1,128)S(1)} %slice_multiply_fusion.2.mean), custom_call_target="tpu_custom_call" | custom-call | flops 536870912 | bytes 8388608 | tf_op jit(solution)/shard_map/pallas_call | solution.py:179
  112.4 5.1 %all-to-all-done.3 = bf16[8,512,128]{2,1,0:T(8,128)(2,1)S(1)} async-done(((bf16[8,512,128]{2,1,0:T(8,128)(2,1)}), bf16[8,512,128]{2,1,0:T(8,128)(2,1)S(1)}, u32[]{:S(2)}, u32[]{:S(2)}) %all-to-all-start.3) | async-done | bytes 1048608 | tf_op jit(solution)/shard_map/all_to_all | solution.py:32
  117.5 3.6 %shard_map.175 = (f32[16,64,128]{2,1,0:T(8,128)S(1)}, f32[64,128]{1,0:T(8,128)S(1)}, f32[2,128]{1,0:T(2,128)S(1)}) custom-call(bf16[4,1024,128]{2,1,0:T(8,128)(2,1)S(1)} %bitcast.70, bf16[16,64,128]{2,1,0:T(8,128)(2,1)S(1)} %bitcast.75, f32[16,64,128]{2,1,0:T(8,128)S(1)} %copy-done.17, f32[1,128]{1,0:T(1,128)S(1)} %bitcast.78, f32[1,128]{1,0:T(1,128)S(1)} %bitcast.80), custom_call_target="tpu_custom_call" | custom-call | flops 536870912 | bytes 8388608 | tf_op jit(solution)/shard_map/pallas_call | solution.py:179
  122.0 3.9 %all-to-all-start.4 = ((f32[32,8,128]{2,1,0:T(8,128)}), f32[32,8,128]{2,1,0:T(8,128)S(1)}, u32[]{:S(2)}, u32[]{:S(2)}) async-start(f32[32,8,128]{2,1,0:T(8,128)} %copy.33), calls=%async_computation.4 | async-start | bytes 262144 | tf_op jit(solution)/shard_map/all_to_all | solution.py:400
  127.7 8.9 %all-to-all-done.4 = f32[32,8,128]{2,1,0:T(8,128)S(1)} async-done(((f32[32,8,128]{2,1,0:T(8,128)}), f32[32,8,128]{2,1,0:T(8,128)S(1)}, u32[]{:S(2)}, u32[]{:S(2)}) %all-to-all-start.4) | async-done | bytes 131104 | tf_op jit(solution)/shard_map/all_to_all | solution.py:400
  137.7 4.1 %all-to-all-start.5 = ((f32[32,2,128]{2,1,0:T(2,128)}), f32[32,2,128]{2,1,0:T(2,128)S(1)}, u32[]{:S(2)}, u32[]{:S(2)}) async-start(f32[32,2,128]{2,1,0:T(2,128)} %broadcast_in_dim.35), calls=%async_computation.6 | async-start | bytes 65536 | tf_op jit(solution)/shard_map/all_to_all | solution.py:19
  141.8 3.9 %shard_map.176 = bf16[16,64,128]{2,1,0:T(8,128)(2,1)} custom-call(f32[16,64,128]{2,1,0:T(8,128)S(1)} %get-tuple-element.47.d_normed, f32[16,64,128]{2,1,0:T(8,128)S(1)} %copy-done.17, bf16[16,64,128]{2,1,0:T(8,128)(2,1)S(1)} %bitcast.71, f32[49,128]{1,0:T(8,128)S(1)} %copy-done.21, f32[5,128]{1,0:T(8,128)S(1)} %stack.5.rows), custom_call_target="tpu_custom_call" | custom-call | flops 536870912 | bytes 8388608 | tf_op jit(solution)/shard_map/pallas_call | solution.py:179
  145.6 5.9 %all-to-all-done.5 = f32[32,2,128]{2,1,0:T(2,128)S(1)} async-done(((f32[32,2,128]{2,1,0:T(2,128)}), f32[32,2,128]{2,1,0:T(2,128)S(1)}, u32[]{:S(2)}, u32[]{:S(2)}) %all-to-all-start.5) | async-done | bytes 32800 | tf_op jit(solution)/shard_map/all_to_all | solution.py:19
  152.8 3.4 %all-to-all-start.6 = ((bf16[4,32,1024]{2,1,0:T(8,128)(2,1)}), bf16[4,32,1024]{2,1,0:T(8,128)(2,1)S(1)}, u32[]{:S(2)}, u32[]{:S(2)}) async-start(bf16[4,32,1024]{2,1,0:T(8,128)(2,1)} %bitcast.87), calls=%async_computation.7 | async-start | bytes 524288 | tf_op jit(solution)/shard_map/all_to_all | solution.py:429
  156.7 6.1 %all-to-all-done.6 = bf16[4,32,1024]{2,1,0:T(8,128)(2,1)S(1)} async-done(((bf16[4,32,1024]{2,1,0:T(8,128)(2,1)}), bf16[4,32,1024]{2,1,0:T(8,128)(2,1)S(1)}, u32[]{:S(2)}, u32[]{:S(2)}) %all-to-all-start.6) | async-done | bytes 262176 | tf_op jit(solution)/shard_map/all_to_all | solution.py:429
  (124 shorter events, 28.2 us)
Async XLA Ops:
  7.2 19.2 %copy-start.2 = (bf16[1024,512]{1,0:T(8,128)(2,1)S(1)}, bf16[1024,512]{1,0:T(8,128)(2,1)}, u32[]{:S(2)}) copy-start(bf16[1024,512]{1,0:T(8,128)(2,1)} %w_own.3) | copy-start | bytes 3145732
  7.2 19.3 %copy-start.3 = (bf16[512,1024]{1,0:T(8,128)(2,1)S(1)}, bf16[512,1024]{1,0:T(8,128)(2,1)}, u32[]{:S(2)}) copy-start(bf16[512,1024]{1,0:T(8,128)(2,1)} %v_own.3) | copy-start | bytes 3145732
  7.2 57.9 %all-gather.2.cloned.1.call-start = ((), (), s32[]{:S(2)}) async-start(), calls=%async_computation.8 | async-start | bytes 2359296 | tf_op jit(solution)/shard_map/all_gather | solution.py:317
  10.8 16.2 %copy-start.29 = (s32[4]{0:T(128)S(1)}, s32[4]{0:T(128)}, u32[]{:S(2)}) copy-start(s32[4]{0:T(128)} %param.19) | copy-start | bytes 52
  10.8 25.6 %copy-start.24 = (f32[4,128]{1,0:T(4,128)S(1)}, f32[4,128]{1,0:T(4,128)}, u32[]{:S(2)}) copy-start(f32[4,128]{1,0:T(4,128)} %param.13) | copy-start | bytes 6148
  10.8 25.6 %copy-start.28 = (f32[4,128]{1,0:T(4,128)S(1)}, f32[4,128]{1,0:T(4,128)}, u32[]{:S(2)}) copy-start(f32[4,128]{1,0:T(4,128)} %param.14) | copy-start | bytes 6148
  14.2 23.5 %copy-start.16 = (f32[16,64,128]{2,1,0:T(8,128)}, f32[16,64,128]{2,1,0:T(8,128)S(1)}, u32[]{:S(2)}) copy-start(f32[16,64,128]{2,1,0:T(8,128)S(1)} %get-tuple-element.33.filtered) | copy-start | bytes 1572868
  14.9 21.3 %all-to-all-start = ((f32[32,2,128]{2,1,0:T(2,128)}), f32[32,2,128]{2,1,0:T(2,128)S(1)}, u32[]{:S(2)}, u32[]{:S(2)}) async-start(f32[32,2,128]{2,1,0:T(2,128)} %broadcast_in_dim.24), calls=%async_computation | async-start | bytes 65536 | tf_op jit(solution)/shard_map/all_to_all | solution.py:19
  26.4 28.9 %collective-permute-start = (bf16[1024,512]{1,0:T(8,128)(2,1)S(1)}, bf16[1024,512]{1,0:T(8,128)(2,1)}, u32[]{:S(2)}, u32[]{:S(2)}) collective-permute-start(bf16[1024,512]{1,0:T(8,128)(2,1)S(1)} %copy-done.2), channel_id=1, source_target_pairs={{0,1},{1,0},{2,3},{3,2},{4,5},{5,4},{6,7},{7,6},{8,9},{9,8},{10,11... | collective-permute-start | bytes 3145736 | tf_op jit(solution)/shard_map/ppermute | solution.py:318
  26.5 28.8 %collective-permute-start.2 = (bf16[512,1024]{1,0:T(8,128)(2,1)S(1)}, bf16[512,1024]{1,0:T(8,128)(2,1)}, u32[]{:S(2)}, u32[]{:S(2)}) collective-permute-start(bf16[512,1024]{1,0:T(8,128)(2,1)S(1)} %copy-done.3), channel_id=1, source_target_pairs={{0,1},{1,0},{2,3},{3,2},{4,5},{5,4},{6,7},{7,6},{8,9},{9,8},{10,11... | collective-permute-start | bytes 3145736 | tf_op jit(solution)/shard_map/ppermute | solution.py:319
  37.7 17.6 %all-to-all-start.1 = ((bf16[8,512,128]{2,1,0:T(8,128)(2,1)}), bf16[8,512,128]{2,1,0:T(8,128)(2,1)S(1)}, u32[]{:S(2)}, u32[]{:S(2)}) async-start(bf16[8,512,128]{2,1,0:T(8,128)(2,1)} %bitcast.85), calls=%async_computation.1 | async-start | bytes 2097152 | tf_op jit(solution)/shard_map/all_to_all | solution.py:27
  42.5 1.2 collective-permute-start.1
  77.8 11.5 %collective-permute-start.3 = (bf16[1024,1024]{1,0:T(8,128)(2,1)}, bf16[1024,1024]{1,0:T(8,128)(2,1)}, u32[]{:S(2)}, u32[]{:S(2)}) collective-permute-start(bf16[1024,1024]{1,0:T(8,128)(2,1)} %shard_map.173), channel_id=1, source_target_pairs={{0,1},{1,0},{2,3},{3,2},{4,5},{5,4},{6,7},{7,6},{8,9},{9,8},{10,11... | collective-permute-start | bytes 6291464 | tf_op jit(solution)/shard_map/ppermute | solution.py:357
  77.8 20.3 %all-to-all-start.2 = ((bf16[8,512,128]{2,1,0:T(8,128)(2,1)}), bf16[8,512,128]{2,1,0:T(8,128)(2,1)}, u32[]{:S(2)}, u32[]{:S(2)}) async-start(bf16[8,512,128]{2,1,0:T(8,128)(2,1)} %copy-done.8), calls=%async_computation.2 | async-start | bytes 2097152 | tf_op jit(solution)/shard_map/all_to_all | solution.py:32
  85.2 66.4 %reduce-scatter.2.cloned.1.call-start = ((), (), s32[]{:S(2)}) async-start(), calls=%async_computation.9 | async-start | bytes 2359296 | tf_op jit(solution)/shard_map/reduce_scatter | solution.py:373
  98.1 19.4 %all-to-all-start.3 = ((bf16[8,512,128]{2,1,0:T(8,128)(2,1)}), bf16[8,512,128]{2,1,0:T(8,128)(2,1)S(1)}, u32[]{:S(2)}, u32[]{:S(2)}) async-start(bf16[8,512,128]{2,1,0:T(8,128)(2,1)} %get-tuple-element.43), calls=%async_computation.3 | async-start | bytes 2097152 | tf_op jit(solution)/shard_map/all_to_all | solution.py:32
  111.2 14.7 %copy-start.27 = (f32[128]{0:T(128)S(1)}, f32[128]{0:T(128)}, u32[]{:S(2)}) copy-start(f32[128]{0:T(128)} %param.18) | copy-start | bytes 1540
  111.2 1.3 collective-permute-start.4
  117.5 24.2 %copy-start.21 = (f32[49,128]{1,0:T(8,128)S(1)}, f32[49,128]{1,0:T(8,128)}, u32[]{:S(2)}) copy-start(f32[49,128]{1,0:T(8,128)} %kernel.3) | copy-start | bytes 75268
  122.0 14.6 %all-to-all-start.4 = ((f32[32,8,128]{2,1,0:T(8,128)}), f32[32,8,128]{2,1,0:T(8,128)S(1)}, u32[]{:S(2)}, u32[]{:S(2)}) async-start(f32[32,8,128]{2,1,0:T(8,128)} %copy.33), calls=%async_computation.4 | async-start | bytes 262144 | tf_op jit(solution)/shard_map/all_to_all | solution.py:400
  136.8 26.8 %copy-start.25 = (f32[4,1,128]{2,1,0:T(1,128)}, f32[4,1,128]{2,1,0:T(1,128)S(1)}, u32[]{:S(2)}) copy-start(f32[4,1,128]{2,1,0:T(1,128)S(1)} %get-tuple-element.73) | copy-start | bytes 6148
  136.8 26.8 %copy-start.26 = (f32[4,1,128]{2,1,0:T(1,128)}, f32[4,1,128]{2,1,0:T(1,128)S(1)}, u32[]{:S(2)}) copy-start(f32[4,1,128]{2,1,0:T(1,128)S(1)} %get-tuple-element.74) | copy-start | bytes 6148
  137.7 13.9 %all-to-all-start.5 = ((f32[32,2,128]{2,1,0:T(2,128)}), f32[32,2,128]{2,1,0:T(2,128)S(1)}, u32[]{:S(2)}, u32[]{:S(2)}) async-start(f32[32,2,128]{2,1,0:T(2,128)} %broadcast_in_dim.35), calls=%async_computation.6 | async-start | bytes 65536 | tf_op jit(solution)/shard_map/all_to_all | solution.py:19
  152.8 10.1 %all-to-all-start.6 = ((bf16[4,32,1024]{2,1,0:T(8,128)(2,1)}), bf16[4,32,1024]{2,1,0:T(8,128)(2,1)S(1)}, u32[]{:S(2)}, u32[]{:S(2)}) async-start(bf16[4,32,1024]{2,1,0:T(8,128)(2,1)} %bitcast.87), calls=%async_computation.7 | async-start | bytes 524288 | tf_op jit(solution)/shard_map/all_to_all | solution.py:429
  (20 other events, 72.4 us)
Sparse Core Ops, SparseCore 0:
  10.4 29.8 all-gather.1
  93.2 37.2 reduce-scatter.1

commit v4 on v3

--- a/solution.py
+++ b/solution.py
@@ -27,13 +27,30 @@
     return lax.all_to_all(halves.reshape(8, rows // 2, own), CH, 0, 0, tiled=True)
 
 
-def exchanged(pieces):
-    _, rows, own = pieces.shape
-    return lax.all_to_all(pieces, CH, 0, 0, tiled=True).reshape(4, 2 * rows, own)
-
-
-def summed(pieces):
-    return jnp.sum(pieces.astype(jnp.float32), axis=0)
+def ring_scattered(array):
+    here = lax.axis_index("x")
+    up = [(i, (i + 1) % 4) for i in range(4)]
+    down = [(i, (i + 3) % 4) for i in range(4)]
+
+    def piece(k):
+        return lax.dynamic_index_in_dim(array, (here + k) % 4, 0, keepdims=False)
+
+    def added(a, b):
+        return (a.astype(jnp.float32) + b.astype(jnp.float32)).astype(array.dtype)
+
+    after, across, before = piece(1), piece(2), piece(3)
+    cut = across.shape[1] // 2
+    from_below = lax.ppermute(across[:, :cut], "x", up)
+    from_above = lax.ppermute(across[:, cut:], "x", down)
+    after = jnp.concatenate([added(after[:, :cut], from_below), after[:, cut:]], axis=1)
+    before = jnp.concatenate([before[:, :cut], added(before[:, cut:], from_above)], axis=1)
+    from_below = lax.ppermute(after, "x", up)
+    from_above = lax.ppermute(before, "x", down)
+    return (
+        piece(0).astype(jnp.float32)
+        + from_below.astype(jnp.float32)
+        + from_above.astype(jnp.float32)
+    )
 
 
 REACH = KS // 2
@@ -95,13 +112,23 @@
                 plain[tap : tap + 1] = jnp.sum(sums[KS + a], axis=0, keepdims=True)
 
 
-def filter_kernel(source, kernel, filtered, moments, pad, planes):
+def filter_kernel(*refs):
+    filtered, moments, d_branch, pad, planes = refs[4:9]
+    source, cotangent, scale, kernel = refs[9:13]
+    copies = [
+        pltpu.make_async_copy(refs[i], refs[9 + i], refs[13].at[i]) for i in range(4)
+    ]
+    for copy in copies:
+        copy.start()
+    for copy in copies:
+        copy.wait()
     spread(source, pad, planes)
     zero = jnp.zeros((8, kernel.shape[1]), jnp.float32)
 
     def step(r, sums):
         row = filtered_row(planes, kernel, r)
         filtered[r] = row
+        d_branch[r] = (cotangent[r].astype(jnp.float32) * scale[...]).astype(jnp.bfloat16)
         return sums[0] + folded(row), sums[1] + folded(row * row)
 
     sums = lax.fori_loop(0, source.shape[0], step, (zero, zero))
@@ -114,16 +141,19 @@
     tap_sums(planes, lambda r: filtered[r] - mean[...], source.shape[0], of_rest, of_flat)
 
 
-def gather_kernel(pieces, source, filtered, mean, rstd, d_normed, of_normed, sums, pad, planes):
+def gather_kernel(
+    pieces, source, filtered, mean, rstd, scale, d_normed, of_normed, sums, pad, planes
+):
     height, width, lanes = source.shape
     spread(source, pad, planes)
     zero = jnp.zeros((8, lanes), jnp.float32)
 
     def step(r, carry):
-        rows = pl.ds(pl.multiple_of(r * width, width), width)
-        row = pieces[0, rows].astype(jnp.float32)
+        side = r // (height // 2)
+        rows = pl.ds(pl.multiple_of((r - side * (height // 2)) * width, width), width)
+        row = pieces[side, rows].astype(jnp.float32)
         for x in range(1, 4):
-            row = row + pieces[x, rows].astype(jnp.float32)
+            row = row + pieces[2 * x + side, rows].astype(jnp.float32)
         d_normed[r] = row
         centered = (filtered[r] - mean[...]) * rstd[...]
         return carry[0] + folded(row * centered), carry[1] + folded(row)
@@ -131,6 +161,10 @@
     carry = lax.fori_loop(0, height, step, (zero, zero))
     for i in range(2):
         sums[i : i + 1] = jnp.sum(carry[i], axis=0, keepdims=True)
+    tail = pieces[0, pl.ds(height * width // 2, 16)].astype(jnp.float32)
+    for k in range(1, 8):
+        tail = tail + pieces[k, pl.ds(height * width // 2, 16)].astype(jnp.float32)
+    sums[2:3] = jnp.sum(tail, axis=0, keepdims=True) / scale[...]
     tap_sums(planes, lambda r: d_normed[r], height, of_normed)
 
 
@@ -171,9 +205,13 @@
     return lax.dot_general(a, b, dims, preferred_element_type=jnp.float32)
 
 
-def kernel_call(kernel, outs, operands, flops, scalar=False, scratch=()):
+def in_hbm(array):
+    return pltpu.with_memory_space_constraint(array, pltpu.HBM)
+
+
+def kernel_call(kernel, outs, operands, flops, scalar=False, scratch=(), space=pltpu.VMEM):
     vmem = pl.BlockSpec(memory_space=pltpu.VMEM)
-    specs = [vmem] * len(operands)
+    specs = [pl.BlockSpec(memory_space=space)] * len(operands)
     if scalar:
         specs[0] = pl.BlockSpec(memory_space=pltpu.SMEM)
     return pl.pallas_call(
@@ -191,48 +229,83 @@
     return jnp.concatenate([pieces[k, pl.ds(start, size)] for k in range(8)], axis=1)
 
 
-def up_kernel(z, w_own, w_pair, b_own, b_pair, v_own, v_pair, slope_o, slope_p, act_o, act_p, out):
-    @pl.loop(0, z.shape[1] // TILE)
+def pointwise_kernel(core, z, y_all, w_own, w_pair, b_own, b_pair, v_own, v_pair, *rest):
+    results, bias_o, bias_p, held, slopes, scale, sems = rest[:6], *rest[6:8], *rest[8:]
+    act_o, act_p, back_o, back_p, out, grad_out = held[:6]
+    y = held[7]
+    half = z.shape[1]
+    fetched = pltpu.make_async_copy(
+        y_all.at[:, pl.ds(pl.multiple_of(core[0] * half, half), half)], y, sems.at[half // TILE, 1]
+    )
+    fetched.start()
+    tiles = half // TILE
+    bias_o[...] = jnp.zeros_like(bias_o)
+    bias_p[...] = jnp.zeros_like(bias_p)
+    scale[...] = jnp.zeros_like(scale)
+
+    def copy(m, j):
+        rows = pl.ds(pl.multiple_of(m * TILE, TILE), TILE)
+        at = (slice(None), rows) if j >= 4 else (rows,)
+        return pltpu.make_async_copy(held[j].at[at], results[j].at[at], sems.at[m, j])
+
+    @pl.loop(0, tiles)
     def _(m):
         start = pl.multiple_of(m * TILE, TILE)
         rows = pl.ds(start, TILE)
         x = joined(z, start, TILE)
-        for w, b, slope, act in ((w_own, b_own, slope_o, act_o), (w_pair, b_pair, slope_p, act_p)):
+        for w, b, slope, act in (
+            (w_own, b_own, slopes[0], act_o),
+            (w_pair, b_pair, slopes[1], act_p),
+        ):
             hidden = dot(x, w[...], DOT_PLAIN) + b[...]
             square = hidden * hidden
             t = jnp.tanh(GELU_A * (hidden + GELU_B * (square * hidden)))
-            half = 0.5 * (1.0 + t)
-            act[rows] = (hidden * half).astype(jnp.bfloat16)
-            slope[rows] = half + (0.5 * GELU_A) * hidden * (1.0 - t * t) * (
+            part = 0.5 * (1.0 + t)
+            act[rows] = (hidden * part).astype(jnp.bfloat16)
+            slope[...] = part + (0.5 * GELU_A) * hidden * (1.0 - t * t) * (
                 1.0 + 3.0 * GELU_B * square
             )
+        copy(m, 0).start()
+        copy(m, 1).start()
+
+        @pl.when(m == 0)
+        def _():
+            fetched.wait()
+
+        up = joined(y, start, TILE)
+        for v, slope, back, bias in (
+            (v_own, slopes[0], back_o, bias_o),
+            (v_pair, slopes[1], back_p, bias_p),
+        ):
+            grad = dot(up, v[...], DOT_COLS) * slope[...]
+            bias[...] += jnp.sum(grad, axis=0, keepdims=True)
+            back[rows] = grad.astype(jnp.bfloat16)
+        copy(m, 2).start()
+        copy(m, 3).start()
+        total = dot(back_o[rows], w_own[...], DOT_COLS) + dot(back_p[rows], w_pair[...], DOT_COLS)
+        for k in range(8):
+            grad_out[k, rows] = total[:, k * 128 : (k + 1) * 128].astype(jnp.bfloat16)
+        copy(m, 5).start()
         total = dot(act_o[rows], v_own[...], DOT_PLAIN) + dot(act_p[rows], v_pair[...], DOT_PLAIN)
         for k in range(8):
             out[k, rows] = total[:, k * 128 : (k + 1) * 128].astype(jnp.bfloat16)
-
-
-def down_kernel(
-    core, y, slope_o, slope_p, w_own, w_pair, v_own, v_pair, back_o, back_p, bias_o, bias_p, out
-):
-    half = slope_o.shape[0]
-    bias_o[...] = jnp.zeros_like(bias_o)
-    bias_p[...] = jnp.zeros_like(bias_p)
-
-    @pl.loop(0, half // TILE)
-    def _(m):
-        start = pl.multiple_of(m * TILE, TILE)
-        rows = pl.ds(start, TILE)
-        up = joined(y, pl.multiple_of(core[0] * half + start, TILE), TILE)
-        for v, slope, back, bias in (
-            (v_own, slope_o, back_o, bias_o),
-            (v_pair, slope_p, back_p, bias_p),
-        ):
-            grad = dot(up, v[...], DOT_COLS) * slope[rows]
-            bias[...] += jnp.sum(grad, axis=0, keepdims=True)
-            back[rows] = grad.astype(jnp.bfloat16)
-        total = dot(back_o[rows], w_own[...], DOT_COLS) + dot(back_p[rows], w_pair[...], DOT_COLS)
-        for k in range(8):
-            out[k, rows] = total[:, k * 128 : (k + 1) * 128].astype(jnp.bfloat16)
+        copy(m, 4).start()
+        scale[...] += jnp.sum(up.astype(jnp.float32) * total, axis=0, keepdims=True)
+
+    for k in range(8):
+        value = scale[:, k * 128 : (k + 1) * 128]
+        high = value.astype(jnp.bfloat16).astype(jnp.float32)
+        row = lax.broadcasted_iota(jnp.int32, (16, 128), 0)
+        both = jnp.where(row == 0, high, jnp.where(row == 1, value - high, 0.0))
+        held[6][k] = both.astype(jnp.bfloat16)
+    last = pltpu.make_async_copy(
+        held[6], results[5].at[:, pl.ds(half, 16)], sems.at[tiles, 0]
+    )
+    last.start()
+    for m in range(tiles):
+        for j in range(6):
+            copy(m, j).wait()
+    last.wait()
 
 
 def weight_kernel(core, z, y, back, act, out):
@@ -248,29 +321,32 @@
             out[here, cols] = dot(a, b[...], DOT_ROWS).astype(out.dtype)
 
 
-def up_pass(z, w_own, w_pair, b_own, b_pair, v_own, v_pair):
+def pointwise_pass(core, z, y, w_own, w_pair, b_own, b_pair, v_own, v_pair):
     rows, width = z.shape[1], w_own.shape[1]
-    return kernel_call(
-        up_kernel,
-        [((rows, width), jnp.float32)] * 2
-        + [((rows, width), jnp.bfloat16)] * 2
-        + [(z.shape, jnp.bfloat16)],
-        (z, w_own, w_pair, b_own[None], b_pair[None], v_own, v_pair),
-        8 * rows * width * 1024,
-    )
-
-
-def down_pass(core, y, slope_o, slope_p, w_own, w_pair, v_own, v_pair):
-    rows, width = slope_o.shape
-    return kernel_call(
-        down_kernel,
-        [((rows, width), jnp.bfloat16)] * 2
-        + [((1, width), jnp.float32)] * 2
-        + [((8, rows, 128), jnp.bfloat16)],
-        (core, y, slope_o, slope_p, w_own, w_pair, v_own, v_pair),
-        8 * rows * width * 1024,
-        scalar=True,
-    )
+    vmem = pl.BlockSpec(memory_space=pltpu.VMEM)
+    flat, wide = (rows, width), (8, rows, 128)
+    outs = [flat] * 4 + [wide, (8, rows + 16, 128)]
+    held = tuple(pltpu.VMEM(s, jnp.bfloat16) for s in [flat] * 4 + [wide, wide, (8, 16, 128), wide])
+    return pl.pallas_call(
+        lambda *refs: pointwise_kernel(*refs[:17], refs[17:25], refs[25:27], *refs[27:]),
+        out_shape=[pltpu.HBM(s, jnp.bfloat16) for s in outs]
+        + [jax.ShapeDtypeStruct((1, width), jnp.float32)] * 2,
+        in_specs=[pl.BlockSpec(memory_space=pltpu.SMEM), vmem]
+        + [pl.BlockSpec(memory_space=pltpu.HBM)]
+        + [vmem] * 6,
+        out_specs=[pl.BlockSpec(memory_space=pltpu.HBM)] * 6 + [vmem] * 2,
+        scratch_shapes=[
+            *held,
+            pltpu.VMEM((TILE, width), jnp.float32),
+            pltpu.VMEM((TILE, width), jnp.float32),
+            pltpu.VMEM((1, 1024), jnp.float32),
+            pltpu.SemaphoreType.DMA((rows // TILE + 1, 6)),
+        ],
+        cost_estimate=pl.CostEstimate(
+            flops=16 * rows * width * 1024, bytes_accessed=8 << 20, transcendentals=0
+        ),
+        compiler_params=pltpu.CompilerParams(vmem_limit_bytes=36 << 20),
+    )(core, z, in_hbm(y), w_own, w_pair, b_own[None], b_pair[None], v_own, v_pair)
 
 
 def weight_pass(kind, *operands):
@@ -312,9 +388,6 @@
     own_gain = jnp.sum(member[:, None] * norm_gain, axis=0)
     own_bias = jnp.sum(member[:, None] * norm_bias, axis=0)
 
-    incoming = cotangent.reshape(row_count, channels).astype(jnp.float32)
-    d_branch = (incoming * layer_scale).astype(jnp.bfloat16)
-    everyone = lax.all_gather(d_branch, CH, axis=0, tiled=False)
     w_in_pair = lax.ppermute(w_in, "c", SWAP)
     w_out_pair = lax.ppermute(w_out, "c", SWAP)
     b_in_pair = lax.ppermute(b_in, "c", SWAP)
@@ -322,13 +395,20 @@
     image = activations.shape[1:]
     source = activations[0]
     scratch = conv_scratch(image)
-    filtered, moments = kernel_call(
+    operands = (source, cotangent[0], layer_scale[None], dw_kernel)
+    filtered, moments, d_branch = kernel_call(
         filter_kernel,
-        [(image, jnp.float32), ((2, channels), jnp.float32)],
-        (source, dw_kernel),
+        [(image, jnp.float32), ((2, channels), jnp.float32), (image, jnp.bfloat16)],
+        tuple(in_hbm(a) for a in operands),
         1 << 29,
-        scratch=scratch,
-    )
+        scratch=(
+            *scratch,
+            *(pltpu.VMEM(a.shape, a.dtype) for a in operands),
+            pltpu.SemaphoreType.DMA((4,)),
+        ),
+        space=pltpu.HBM,
+    )
+    everyone = lax.all_gather(d_branch.reshape(row_count, channels), CH)
     per_device = sent_to_all(moments, DP)
     counts = group_sizes.astype(jnp.float32)[:, None] * row_count
     totals = jnp.sum(owners[:, :, None, None] * per_device[None], axis=1)
@@ -338,27 +418,6 @@
     own_rstd = jnp.sum(member[:, None] * group_rstd, axis=0)
     centered = (filtered.reshape(row_count, channels) - own_mean) * own_rstd
     normed = (centered * own_gain + own_bias).astype(jnp.bfloat16)
-    gathered = rows_of_all(normed)
-
-    slope_own, slope_pair, active_own, active_pair, partial_branch = up_pass(
-        gathered, w_in, w_in_pair, b_in, b_in_pair, w_out, w_out_pair
-    )
-    branch_pieces = exchanged(partial_branch)
-    branch = summed(branch_pieces)
-    initial = activations.reshape(row_count, channels).astype(jnp.float32)
-    result = (initial + layer_scale * branch).astype(jnp.bfloat16).reshape(activations.shape)
-    scale_local = jnp.sum(incoming * branch, axis=0)
-
-    where = core.astype(jnp.int32)[None]
-    back_own, back_pair, bias_own, bias_pair, partial_normed = down_pass(
-        where, everyone, slope_own, slope_pair, w_in, w_in_pair, w_out, w_out_pair
-    )
-    for_pair = weight_pass(jnp.bfloat16, where, gathered, everyone, back_pair, active_pair)
-    from_pair = lax.ppermute(for_pair, "c", SWAP)
-    own_grads = weight_pass(jnp.float32, where, gathered, everyone, back_own, active_own)
-    both_local = (own_grads + from_pair.astype(jnp.float32)).astype(jnp.bfloat16)
-    hidden_cols = w_in.shape[1]
-    bias_local = bias_own + lax.ppermute(bias_pair, "c", SWAP)
     image_mean = moments[:1] / row_count
     of_flat, of_rest = kernel_call(
         terms_kernel,
@@ -367,37 +426,64 @@
         1 << 29,
         scratch=scratch,
     )
-    partial_normed, branch_pieces, both_local = lax.optimization_barrier(
-        (partial_normed, branch_pieces, both_local)
-    )
+    gathered = rows_of_all(normed)
+    gathered, of_flat, of_rest = lax.optimization_barrier((gathered, of_flat, of_rest))
+
+    where = core.astype(jnp.int32)[None]
+    (
+        active_own,
+        active_pair,
+        back_own,
+        back_pair,
+        partial_branch,
+        partial_normed,
+        bias_own,
+        bias_pair,
+    ) = pointwise_pass(where, gathered, everyone, w_in, w_in_pair, b_in, b_in_pair, w_out, w_out_pair)
+    normed_pieces = lax.all_to_all(partial_normed, CH, 0, 0, tiled=True)
+    for_pair = weight_pass(jnp.bfloat16, where, gathered, everyone, back_pair, active_pair)
+    from_pair = lax.ppermute(for_pair, "c", SWAP)
+    own_grads = weight_pass(jnp.float32, where, gathered, everyone, back_own, active_own)
+    both_local = (own_grads + from_pair.astype(jnp.float32)).astype(jnp.bfloat16)
+    hidden_cols = w_in.shape[1]
+    bias_local = bias_own + lax.ppermute(bias_pair, "c", SWAP)
     near = lax.psum_scatter(both_local, "z", scatter_dimension=0, tiled=True)
-    normed_pieces = exchanged(partial_normed)
 
     from_mean = per_device[:, 0] / row_count - jnp.sum(
         owners[:, :, None] * group_mean[:, None], axis=0
     )
-    normed_pieces, of_flat, of_rest = lax.optimization_barrier((normed_pieces, of_flat, of_rest))
     d_normed, of_normed, grad_moments = kernel_call(
         gather_kernel,
-        [(image, jnp.float32), ((64, channels), jnp.float32), ((2, channels), jnp.float32)],
-        (normed_pieces, source, filtered, own_mean[None], own_rstd[None]),
+        [(image, jnp.float32), ((64, channels), jnp.float32), ((3, channels), jnp.float32)],
+        (normed_pieces, source, filtered, own_mean[None], own_rstd[None], layer_scale[None]),
         1 << 29,
         scratch=scratch,
     )
     own_scaled = own_gain * own_rstd
     others = jnp.concatenate(
-        [bias_local.reshape(4, channels), scale_local[None], jnp.zeros((64 - TAPS - 5, channels))]
+        [bias_local.reshape(4, channels), grad_moments[2:], jnp.zeros((64 - TAPS - 5, channels))]
     )
     firsts = jnp.concatenate([own_scaled * of_normed[:TAPS], others])
     local = jnp.stack([a.reshape(devices, 2, channels) for a in (firsts, of_flat, of_rest)], axis=1)
     sent = jnp.concatenate(
         [
             local.reshape(devices, 6, channels),
-            jnp.broadcast_to(grad_moments[None], (devices, 2, channels)),
+            jnp.broadcast_to(grad_moments[None, :2], (devices, 2, channels)),
         ],
         axis=1,
     )
+    sent, partial_branch = lax.optimization_barrier((sent, partial_branch))
     parts = lax.all_to_all(sent, DP, 0, 0, tiled=True)
+    halves = (4, 2, row_count // 2, channels)
+    chip_branch = ring_scattered(partial_branch.reshape(halves)).astype(jnp.bfloat16)
+    kept = lax.dynamic_index_in_dim(chip_branch, core, 0, keepdims=False)
+    given = lax.dynamic_index_in_dim(chip_branch, 1 - core, 0, keepdims=False)
+    taken = lax.ppermute(given, "c", SWAP)
+    branch = jnp.concatenate(
+        [jnp.where(core == 0, kept, taken), jnp.where(core == 0, taken, kept)]
+    ).astype(jnp.float32)
+    initial = activations.reshape(row_count, channels).astype(jnp.float32)
+    result = (initial + layer_scale * branch).astype(jnp.bfloat16).reshape(activations.shape)
     grad_totals = jnp.sum(owners[:, :, None, None] * parts[None, :, 6:], axis=1)
     d_gain = grad_totals[:, 0]
     d_bias = grad_totals[:, 1]

time: 173 us -> 164 us (0.948); the launches traced: 170 us -> 163 us
  waiting for transfers between devices: 51.1 us -> 42.8 us
  Pallas kernels: 30.6 us -> 32.9 us
    pallas_call x0 -> x1, Pallas kernels: none -> 9.5 us  [pointwise_pass(): pl.pallas_call(lambda *refs: pointwise_kernel(*refs[:17], refs[17:25], re...]
    pallas_call x8 -> x6, Pallas kernels: 30.6 us -> 23.4 us  [kernel_call(): pl.pallas_call(kernel, out_shape=[jax.ShapeDtypeStruct(s, t) for s, t in...]
    all_to_all x2 -> x1, starting transfers between devices: 14.1 us -> 7.28 us  [body(): normed_pieces = lax.all_to_all(partial_normed, CH, 0, 0, tiled=True)]
    ppermute x0 -> x5, starting transfers between devices: none -> 5.64 us  [the longest x1 2.26 us: ring_scattered(): from_above = lax.ppermute(across[:, cut:], 'x', down)]
    all_to_all x2 -> x1, waiting for transfers between devices: 10.1 us -> 4.7 us  [body(): normed_pieces = lax.all_to_all(partial_normed, CH, 0, 0, tiled=True)]
    reduce_scatter x1, waiting for transfers between devices: 0.01 us -> 4.54 us  [body(): near = lax.psum_scatter(both_local, 'z', scatter_dimension=0, tiled=True)]
    all_to_all x1, waiting for transfers between devices: 8.88 us -> 5.56 us  [body(): parts = lax.all_to_all(sent, DP, 0, 0, tiled=True)]
    all_to_all x1, waiting for transfers between devices: 11.6 us -> 8.56 us  [rows_of_all(): lax.all_to_all(halves.reshape(8, rows // 2, own), CH, 0, 0, tiled=True)]
  transfers between devices with their start and end apart: 14 -> 18, of which waited for: 9 -> 8; matrix products, arithmetic and copies ran while one was open for 9% -> 7% of each run, Pallas kernels for 13% -> 9%
where the time goes in v4:
time: 164 us; the launch traced here: 163 us
  starting transfers between devices  43.8 us (27%)
  waiting for transfers between devices  42.8 us (26%)
  Pallas kernels  32.9 us (20%)
  local copies, waits for them, and re-layouts  17.4 us (11%)
  between operations  15.2 us (9%)
  other arithmetic  11.3 us (7%)
    pallas_call x6, Pallas kernels, kernel_call(): pl.pallas_call(kernel, out_shape=[jax.ShapeDtypeStruct(s, t) for s, t in...  23.4 us
    all_to_all x2, starting transfers between devices, sent_to_all(): lax.all_to_all(jnp.broadcast_to(array[None], (size, *array.shape)), axis,...  15.7 us
    all_to_all x2, waiting for transfers between devices, sent_to_all(): lax.all_to_all(jnp.broadcast_to(array[None], (size, *array.shape)), axis,...  10.2 us
    unnamed x54, local copies, waits for them, and re-layouts  9.59 us
    pallas_call x1, Pallas kernels, pointwise_pass(): pl.pallas_call(lambda *refs: pointwise_kernel(*refs[:17], refs[17:25], re...  9.5 us
    all_to_all x1, waiting for transfers between devices, rows_of_all(): lax.all_to_all(halves.reshape(8, rows // 2, own), CH, 0, 0, tiled=True)  8.56 us
    all_to_all x1, starting transfers between devices, body(): normed_pieces = lax.all_to_all(partial_normed, CH, 0, 0, tiled=True)  7.28 us
    all_to_all x1, waiting for transfers between devices, body(): lax.all_to_all(near.reshape(4, -1, near.shape[1]), 'y', 0, 0, tiled=True)  6.17 us
  transfers between devices with their start and end apart: 18, of which 8 were waited for; matrix products, arithmetic and copies ran while one was open for 7% of the time, Pallas kernels for 9%

profile of v4, /device:TPU:4, one launch (start us, length us, event | category | flops | bytes accessed | tf_op | source)
XLA Modules:
  0.0 163.5 jit_solution(1824270888228423420)
XLA Ops:
  7.3 5.4 %shard_map.169 = (f32[16,64,128]{2,1,0:T(8,128)S(1)}, f32[2,128]{1,0:T(2,128)S(1)}, bf16[16,64,128]{2,1,0:T(8,128)(2,1)}) custom-call(bf16[16,64,128]{2,1,0:T(8,128)(2,1)} %bitcast.78, bf16[16,64,128]{2,1,0:T(8,128)(2,1)} %bitcast.89, f32[1,128]{1,0:T(1,128)} %bitcast.87, f32[49,128]{1,0:T(8,128)} %kernel.1), custom_call_target="tpu_custom_call" | custom-call | flops 536870912 | bytes 8388608 | tf_op jit(solution)/shard_map/pallas_call | solution.py:217
  13.4 11.5 %all-to-all-start = ((f32[32,2,128]{2,1,0:T(2,128)}), f32[32,2,128]{2,1,0:T(2,128)S(1)}, u32[]{:S(2)}, u32[]{:S(2)}) async-start(f32[32,2,128]{2,1,0:T(2,128)} %broadcast_in_dim.23), calls=%async_computation | async-start | bytes 65536 | tf_op jit(solution)/shard_map/all_to_all | solution.py:19
  28.4 6.4 %all-to-all-done = f32[32,2,128]{2,1,0:T(2,128)S(1)} async-done(((f32[32,2,128]{2,1,0:T(2,128)}), f32[32,2,128]{2,1,0:T(2,128)S(1)}, u32[]{:S(2)}, u32[]{:S(2)}) %all-to-all-start) | async-done | bytes 32800 | tf_op jit(solution)/shard_map/all_to_all | solution.py:19
  36.4 4.8 %all-to-all-start.1 = ((bf16[8,512,128]{2,1,0:T(8,128)(2,1)}), bf16[8,512,128]{2,1,0:T(8,128)(2,1)S(1)}, u32[]{:S(2)}, u32[]{:S(2)}) async-start(bf16[8,512,128]{2,1,0:T(8,128)(2,1)} %bitcast.93), calls=%async_computation.1 | async-start | bytes 2097152 | tf_op jit(solution)/shard_map/all_to_all | solution.py:27
  41.3 4.1 %shard_map.170 = (f32[64,128]{1,0:T(8,128)S(1)}, f32[64,128]{1,0:T(8,128)S(1)}) custom-call(bf16[16,64,128]{2,1,0:T(8,128)(2,1)S(1)} %bitcast.79, f32[16,64,128]{2,1,0:T(8,128)S(1)} %get-tuple-element.33.filtered, f32[1,128]{1,0:T(1,128)S(1)} %slice_multiply_fusion.2.mean), custom_call_target="tpu_custom_call" | custom-call | flops 536870912 | bytes 8388608 | tf_op jit(solution)/shard_map/pallas_call | solution.py:217
  45.4 8.6 %all-to-all-done.1.refs_1_.z = bf16[8,512,128]{2,1,0:T(8,128)(2,1)S(1)} async-done(((bf16[8,512,128]{2,1,0:T(8,128)(2,1)}), bf16[8,512,128]{2,1,0:T(8,128)(2,1)S(1)}, u32[]{:S(2)}, u32[]{:S(2)}) %all-to-all-start.1) | async-done | bytes 1048608 | tf_op jit(solution)/shard_map/all_to_all | solution.py:27
  55.2 9.5 %shard_map.171 = (bf16[512,512]{1,0:T(8,128)(2,1)}, bf16[512,512]{1,0:T(8,128)(2,1)}, bf16[512,512]{1,0:T(8,128)(2,1)}, bf16[512,512]{1,0:T(8,128)(2,1)}, bf16[8...) custom-call(s32[1]{0:T(128)} %bitcast.7.refs_0_.core, ...), custom_call_target="tpu_custom_call" | custom-call | flops 4294967296 | bytes 8388608 | tf_op jit(solution)/shard_map/pallas_call | solution.py:330
  66.9 3.2 %shard_map.175 = bf16[1024,1024]{1,0:T(8,128)(2,1)} custom-call(s32[1]{0:T(128)} %bitcast.7.refs_0_.core, bf16[8,512,128]{2,1,0:T(8,128)(2,1)S(1)} %all-to-all-done.1.refs_1_.z, bf16[8,1024,128]{2,1,0:T(8,128)(2,1)S(1)} %copy-done.1, bf16[512,512]{1,0:T(8,128)(2,1)S(1)} %copy-done.5, bf16[512,512]{1,0:T(8,128)(2,1)S(1)} %copy-done.4), custom_call_target="tpu_custom_call" | custom-call | flops 1073741824 | bytes 8388608 | tf_op jit(solution)/shard_map/pallas_call | solution.py:217
  70.1 7.3 %all-to-all-start.2 = ((bf16[8,528,128]{2,1,0:T(8,128)(2,1)}), bf16[8,528,128]{2,1,0:T(8,128)(2,1)}, u32[]{:S(2)}, u32[]{:S(2)}) async-start(bf16[8,528,128]{2,1,0:T(8,128)(2,1)} %get-tuple-element.38), calls=%async_computation.2 | async-start | bytes 2162688 | tf_op jit(solution)/shard_map/all_to_all | solution.py:443
  84.0 2.0 %copy-done = f32[1024,1024]{1,0:T(8,128)} copy-done((f32[1024,1024]{1,0:T(8,128)}, f32[1024,1024]{1,0:T(8,128)S(1)}, u32[]{:S(2)}) %copy-start) | copy-done | bytes 4194328
  85.9 4.7 %all-to-all-done.2.pieces = bf16[8,528,128]{2,1,0:T(8,128)(2,1)} async-done(((bf16[8,528,128]{2,1,0:T(8,128)(2,1)}), bf16[8,528,128]{2,1,0:T(8,128)(2,1)}, u32[]{:S(2)}, u32[]{:S(2)}) %all-to-all-start.2) | async-done | bytes 1081376 | tf_op jit(solution)/shard_map/all_to_all | solution.py:443
  91.7 4.9 %shard_map.172 = (f32[16,64,128]{2,1,0:T(8,128)S(1)}, f32[64,128]{1,0:T(8,128)S(1)}, f32[3,128]{1,0:T(4,128)S(1)}) custom-call(bf16[8,528,128]{2,1,0:T(8,128)(2,1)} %all-to-all-done.2.pieces, bf16[16,64,128]{2,1,0:T(8,128)(2,1)S(1)} %bitcast.80, f32[16,64,128]{2,1,0:T(8,128)S(1)} %copy-done.7, f32[1,128]{1,0:T(1,128)S(1)} %bitcast.83, ...), custom_call_target="tpu_custom_call" | custom-call | flops 536870912 | bytes 8388608 | tf_op jit(solution)/shard_map/pallas_call | solution.py:217
  96.6 5.0 %add_convert_fusion = bf16[1024,1024]{1,0:T(8,128)(2,1)} fusion(f32[1024,1024]{1,0:T(8,128)} %copy-done, bf16[1024,1024]{1,0:T(8,128)(2,1)} %collective-permute-done.9), kind=kLoop, calls=%fused_computation | loop fusion | flops 3145728 | bytes 8388608 | tf_op jit(solution)/shard_map/convert_element_type | solution.py:447
  103.7 2.3 %collective-permute-start.6 = (bf16[2,256,128]{2,1,0:T(8,128)(2,1)}, bf16[2,256,128]{2,1,0:T(8,128)(2,1)S(1)}, u32[]{:S(2)}, u32[]{:S(2)}) collective-permute-start(bf16[2,256,128]{2,1,0:T(8,128)(2,1)} %get-tuple-element.71), channel_id=1, source_target_pairs={{0,6},{2,0},{4,2},{6,4},{1,7},{3,1},{5,3},{7,5},{8,14},{10,8},{12,... | collective-permute-start | bytes 393224 | tf_op jit(solution)/shard_map/ppermute | solution.py:44
  106.7 5.2 %all-to-all-start.3 = ((f32[32,8,128]{2,1,0:T(8,128)}), f32[32,8,128]{2,1,0:T(8,128)S(1)}, u32[]{:S(2)}, u32[]{:S(2)}) async-start(f32[32,8,128]{2,1,0:T(8,128)} %copy.33), calls=%async_computation.3 | async-start | bytes 262144 | tf_op jit(solution)/shard_map/all_to_all | solution.py:476
  112.3 2.1 %collective-permute-start.7 = (bf16[2,512,128]{2,1,0:T(8,128)(2,1)S(1)}, bf16[2,512,128]{2,1,0:T(8,128)(2,1)}, u32[]{:S(2)}, u32[]{:S(2)}) collective-permute-start(bf16[2,512,128]{2,1,0:T(8,128)(2,1)S(1)} %pad_maximum_fusion.1), channel_id=1, source_target_pairs={{0,6},{2,0},{4,2},{6,4},{1,7},{3,1},{5,3},{7,5},{8,14},{10,8},{12,... | collective-permute-start | bytes 786440 | tf_op jit(solution)/shard_map/ppermute | solution.py:48
  114.4 3.0 %collective-permute-done.4 = bf16[2,256,128]{2,1,0:T(8,128)(2,1)S(1)} collective-permute-done((bf16[2,256,128]{2,1,0:T(8,128)(2,1)}, bf16[2,256,128]{2,1,0:T(8,128)(2,1)S(1)}, u32[]{:S(2)}, u32[]{:S(2)}) %collective-permute-start.4) | collective-permute-done | bytes 131104 | tf_op jit(solution)/shard_map/ppermute | solution.py:43
  118.4 5.6 %all-to-all-done.3 = f32[32,8,128]{2,1,0:T(8,128)S(1)} async-done(((f32[32,8,128]{2,1,0:T(8,128)}), f32[32,8,128]{2,1,0:T(8,128)S(1)}, u32[]{:S(2)}, u32[]{:S(2)}) %all-to-all-start.3) | async-done | bytes 131104 | tf_op jit(solution)/shard_map/all_to_all | solution.py:476
  125.0 4.2 %all-to-all-start.4 = ((f32[32,2,128]{2,1,0:T(2,128)}), f32[32,2,128]{2,1,0:T(2,128)S(1)}, u32[]{:S(2)}, u32[]{:S(2)}) async-start(f32[32,2,128]{2,1,0:T(2,128)} %broadcast_in_dim.32), calls=%async_computation.5 | async-start | bytes 65536 | tf_op jit(solution)/shard_map/all_to_all | solution.py:19
  130.6 3.9 %shard_map.173 = bf16[16,64,128]{2,1,0:T(8,128)(2,1)} custom-call(f32[16,64,128]{2,1,0:T(8,128)S(1)} %get-tuple-element.47.d_normed, f32[16,64,128]{2,1,0:T(8,128)S(1)} %copy-done.8, bf16[16,64,128]{2,1,0:T(8,128)(2,1)S(1)} %bitcast.90, f32[49,128]{1,0:T(8,128)S(1)} %copy-done.14, f32[5,128]{1,0:T(8,128)S(1)} %stack.5.rows), custom_call_target="tpu_custom_call" | custom-call | flops 536870912 | bytes 8388608 | tf_op jit(solution)/shard_map/pallas_call | solution.py:217
  135.4 3.8 %all-to-all-done.4 = f32[32,2,128]{2,1,0:T(2,128)S(1)} async-done(((f32[32,2,128]{2,1,0:T(2,128)}), f32[32,2,128]{2,1,0:T(2,128)S(1)}, u32[]{:S(2)}, u32[]{:S(2)}) %all-to-all-start.4) | async-done | bytes 32800 | tf_op jit(solution)/shard_map/all_to_all | solution.py:19
  139.2 4.5 %reduce-scatter.2.cloned.1.call-done = bf16[128,1024]{1,0:T(8,128)(2,1)} async-done(((bf16[1024,1024]{1,0:T(8,128)(2,1)}), bf16[128,1024]{1,0:T(8,128)(2,1)}) %reduce-scatter.2.cloned.1.call-update) | async-done | bytes 262160 | tf_op jit(solution)/shard_map/reduce_scatter | solution.py:450
  144.9 4.3 %all-to-all-start.5 = ((bf16[4,32,1024]{2,1,0:T(8,128)(2,1)}), bf16[4,32,1024]{2,1,0:T(8,128)(2,1)S(1)}, u32[]{:S(2)}, u32[]{:S(2)}) async-start(bf16[4,32,1024]{2,1,0:T(8,128)(2,1)} %bitcast.98), calls=%async_computation.6 | async-start | bytes 524288 | tf_op jit(solution)/shard_map/all_to_all | solution.py:515
  149.7 6.2 %all-to-all-done.5 = bf16[4,32,1024]{2,1,0:T(8,128)(2,1)S(1)} async-done(((bf16[4,32,1024]{2,1,0:T(8,128)(2,1)}), bf16[4,32,1024]{2,1,0:T(8,128)(2,1)S(1)}, u32[]{:S(2)}, u32[]{:S(2)}) %all-to-all-start.5) | async-done | bytes 262176 | tf_op jit(solution)/shard_map/all_to_all | solution.py:515
  (135 shorter events, 25.8 us)
Async XLA Ops:
  7.2 27.8 %copy-start.19 = (f32[4,128]{1,0:T(4,128)S(1)}, f32[4,128]{1,0:T(4,128)}, u32[]{:S(2)}) copy-start(f32[4,128]{1,0:T(4,128)} %param.13) | copy-start | bytes 6148
  7.2 27.8 %copy-start.22 = (f32[4,128]{1,0:T(4,128)S(1)}, f32[4,128]{1,0:T(4,128)}, u32[]{:S(2)}) copy-start(f32[4,128]{1,0:T(4,128)} %param.14) | copy-start | bytes 6148
  7.2 46.8 %all-gather.2.cloned.1.call-start = ((), (), s32[]{:S(2)}) async-start(), calls=%async_computation.7 | async-start | bytes 2359296 | tf_op jit(solution)/shard_map/all_gather | solution.py:411
  12.7 28.6 %copy-start.6 = (f32[16,64,128]{2,1,0:T(8,128)}, f32[16,64,128]{2,1,0:T(8,128)S(1)}, u32[]{:S(2)}) copy-start(f32[16,64,128]{2,1,0:T(8,128)S(1)} %get-tuple-element.33.filtered) | copy-start | bytes 1572868
  13.4 21.3 %all-to-all-start = ((f32[32,2,128]{2,1,0:T(2,128)}), f32[32,2,128]{2,1,0:T(2,128)S(1)}, u32[]{:S(2)}, u32[]{:S(2)}) async-start(f32[32,2,128]{2,1,0:T(2,128)} %broadcast_in_dim.23), calls=%async_computation | async-start | bytes 65536 | tf_op jit(solution)/shard_map/all_to_all | solution.py:19
  25.0 29.0 %collective-permute-start = (bf16[1024,512]{1,0:T(8,128)(2,1)S(1)}, bf16[1024,512]{1,0:T(8,128)(2,1)}, u32[]{:S(2)}, u32[]{:S(2)}) collective-permute-start(bf16[1024,512]{1,0:T(8,128)(2,1)S(1)} %copy-done.11), channel_id=1, source_target_pairs={{0,1},{1,0},{2,3},{3,2},{4,5},{5,4},{6,7},{7,6},{8,9},{9,8},{10,11... | collective-permute-start | bytes 3145736 | tf_op jit(solution)/shard_map/ppermute | solution.py:391
  25.1 28.9 %collective-permute-start.2 = (bf16[512,1024]{1,0:T(8,128)(2,1)}, bf16[512,1024]{1,0:T(8,128)(2,1)}, u32[]{:S(2)}, u32[]{:S(2)}) collective-permute-start(bf16[512,1024]{1,0:T(8,128)(2,1)} %refs_7_.1), channel_id=1, source_target_pairs={{0,1},{1,0},{2,3},{3,2},{4,5},{5,4},{6,7},{7,6},{8,9},{9,8},{10,11... | collective-permute-start | bytes 3145736 | tf_op jit(solution)/shard_map/ppermute | solution.py:392
  36.4 17.6 %all-to-all-start.1 = ((bf16[8,512,128]{2,1,0:T(8,128)(2,1)}), bf16[8,512,128]{2,1,0:T(8,128)(2,1)S(1)}, u32[]{:S(2)}, u32[]{:S(2)}) async-start(bf16[8,512,128]{2,1,0:T(8,128)(2,1)} %bitcast.93), calls=%async_computation.1 | async-start | bytes 2097152 | tf_op jit(solution)/shard_map/all_to_all | solution.py:27
  41.2 12.8 %collective-permute-start.1 = (f32[512]{0:T(512)S(1)}, f32[512]{0:T(512)S(1)}, u32[]{:S(2)}, u32[]{:S(2)}) collective-permute-start(f32[512]{0:T(512)S(1)} %copy-done.15), channel_id=1, source_target_pairs={{0,1},{1,0},{2,3},{3,2},{4,5},{5,4},{6,7},{7,6},{8,9},{9,8},{10,11... | collective-permute-start | bytes 6152 | tf_op jit(solution)/shard_map/ppermute | solution.py:393
  70.1 26.5 %collective-permute-start.9 = (bf16[1024,1024]{1,0:T(8,128)(2,1)}, bf16[1024,1024]{1,0:T(8,128)(2,1)}, u32[]{:S(2)}, u32[]{:S(2)}) collective-permute-start(bf16[1024,1024]{1,0:T(8,128)(2,1)} %shard_map.175), channel_id=1, source_target_pairs={{0,1},{1,0},{2,3},{3,2},{4,5},{5,4},{6,7},{7,6},{8,9},{9,8},{10,11... | collective-permute-start | bytes 6291464 | tf_op jit(solution)/shard_map/ppermute | solution.py:445
  70.1 20.5 %all-to-all-start.2 = ((bf16[8,528,128]{2,1,0:T(8,128)(2,1)}), bf16[8,528,128]{2,1,0:T(8,128)(2,1)}, u32[]{:S(2)}, u32[]{:S(2)}) async-start(bf16[8,528,128]{2,1,0:T(8,128)(2,1)} %get-tuple-element.38), calls=%async_computation.2 | async-start | bytes 2162688 | tf_op jit(solution)/shard_map/all_to_all | solution.py:443
  77.4 66.3 %reduce-scatter.2.cloned.1.call-start = ((), (), s32[]{:S(2)}) async-start(), calls=%async_computation.8 | async-start | bytes 2359296 | tf_op jit(solution)/shard_map/reduce_scatter | solution.py:450
  79.9 6.1 %collective-permute-start.3 = (f32[1,512]{1,0:T(1,128)S(1)}, f32[1,512]{1,0:T(1,128)S(1)}, u32[]{:S(2)}, u32[]{:S(2)}) collective-permute-start(f32[1,512]{1,0:T(1,128)S(1)} %get-tuple-element.41), channel_id=1, source_target_pairs={{0,1},{1,0},{2,3},{3,2},{4,5},{5,4},{6,7},{7,6},{8,9},{9,8},{10,11... | collective-permute-start | bytes 6152 | tf_op jit(solution)/shard_map/ppermute | solution.py:449
  103.0 21.2 %copy-start.24 = (f32[4]{0:T(128)S(1)}, f32[4]{0:T(128)}, u32[]{:S(2)}) copy-start(f32[4]{0:T(128)} %copy-done.23) | copy-start | bytes 52
  103.7 8.5 %collective-permute-start.6 = (bf16[2,256,128]{2,1,0:T(8,128)(2,1)}, bf16[2,256,128]{2,1,0:T(8,128)(2,1)S(1)}, u32[]{:S(2)}, u32[]{:S(2)}) collective-permute-start(bf16[2,256,128]{2,1,0:T(8,128)(2,1)} %get-tuple-element.71), channel_id=1, source_target_pairs={{0,6},{2,0},{4,2},{6,4},{1,7},{3,1},{5,3},{7,5},{8,14},{10,8},{12,... | collective-permute-start | bytes 393224 | tf_op jit(solution)/shard_map/ppermute | solution.py:44
  106.7 17.3 %all-to-all-start.3 = ((f32[32,8,128]{2,1,0:T(8,128)}), f32[32,8,128]{2,1,0:T(8,128)S(1)}, u32[]{:S(2)}, u32[]{:S(2)}) async-start(f32[32,8,128]{2,1,0:T(8,128)} %copy.33), calls=%async_computation.3 | async-start | bytes 262144 | tf_op jit(solution)/shard_map/all_to_all | solution.py:476
  111.9 18.7 %copy-start.8 = (f32[16,64,128]{2,1,0:T(8,128)S(1)}, f32[16,64,128]{2,1,0:T(8,128)}, u32[]{:S(2)}) copy-start(f32[16,64,128]{2,1,0:T(8,128)} %copy-done.6) | copy-start | bytes 1572868
  111.9 18.7 %copy-start.13 = (bf16[1,16,64,128]{3,2,1,0:T(8,128)(2,1)S(1)}, bf16[1,16,64,128]{3,2,1,0:T(8,128)(2,1)}, u32[]{:S(2)}) copy-start(bf16[1,16,64,128]{3,2,1,0:T(8,128)(2,1)} %param.11) | copy-start | bytes 786436
  111.9 5.4 %collective-permute-start.4 = (bf16[2,256,128]{2,1,0:T(8,128)(2,1)}, bf16[2,256,128]{2,1,0:T(8,128)(2,1)S(1)}, u32[]{:S(2)}, u32[]{:S(2)}) collective-permute-start(bf16[2,256,128]{2,1,0:T(8,128)(2,1)} %get-tuple-element.70), channel_id=1, source_target_pairs={{0,2},{2,4},{4,6},{6,0},{1,3},{3,5},{5,7},{7,1},{8,10},{10,12},{12... | collective-permute-start | bytes 393224 | tf_op jit(solution)/shard_map/ppermute | solution.py:43
  112.3 17.0 %collective-permute-start.7 = (bf16[2,512,128]{2,1,0:T(8,128)(2,1)S(1)}, bf16[2,512,128]{2,1,0:T(8,128)(2,1)}, u32[]{:S(2)}, u32[]{:S(2)}) collective-permute-start(bf16[2,512,128]{2,1,0:T(8,128)(2,1)S(1)} %pad_maximum_fusion.1), channel_id=1, source_target_pairs={{0,6},{2,0},{4,2},{6,4},{1,7},{3,1},{5,3},{7,5},{8,14},{10,8},{12,... | collective-permute-start | bytes 786440 | tf_op jit(solution)/shard_map/ppermute | solution.py:48
  117.4 11.8 %collective-permute-start.5 = (bf16[2,512,128]{2,1,0:T(8,128)(2,1)S(1)}, bf16[2,512,128]{2,1,0:T(8,128)(2,1)}, u32[]{:S(2)}, u32[]{:S(2)}) collective-permute-start(bf16[2,512,128]{2,1,0:T(8,128)(2,1)S(1)} %pad_maximum_fusion), channel_id=1, source_target_pairs={{0,2},{2,4},{4,6},{6,0},{1,3},{3,5},{5,7},{7,1},{8,10},{10,12},{12... | collective-permute-start | bytes 786440 | tf_op jit(solution)/shard_map/ppermute | solution.py:47
  125.0 14.1 %all-to-all-start.4 = ((f32[32,2,128]{2,1,0:T(2,128)}), f32[32,2,128]{2,1,0:T(2,128)S(1)}, u32[]{:S(2)}, u32[]{:S(2)}) async-start(f32[32,2,128]{2,1,0:T(2,128)} %broadcast_in_dim.32), calls=%async_computation.5 | async-start | bytes 65536 | tf_op jit(solution)/shard_map/all_to_all | solution.py:19
  130.4 4.0 %collective-permute-start.8 = (bf16[512,128]{1,0:T(8,128)(2,1)S(1)}, bf16[512,128]{1,0:T(8,128)(2,1)S(1)}, u32[]{:S(2)}, u32[]{:S(2)}) collective-permute-start(bf16[512,128]{1,0:T(8,128)(2,1)S(1)} %dynamic-slice_bitcast_fusion.3), channel_id=1, source_target_pairs={{0,1},{1,0},{2,3},{3,2},{4,5},{5,4},{6,7},{7,6},{8,9},{9,8},{10,11... | collective-permute-start | bytes 393224 | tf_op jit(solution)/shard_map/ppermute | solution.py:481
  144.9 11.0 %all-to-all-start.5 = ((bf16[4,32,1024]{2,1,0:T(8,128)(2,1)}), bf16[4,32,1024]{2,1,0:T(8,128)(2,1)S(1)}, u32[]{:S(2)}, u32[]{:S(2)}) async-start(bf16[4,32,1024]{2,1,0:T(8,128)(2,1)} %bitcast.98), calls=%async_computation.6 | async-start | bytes 524288 | tf_op jit(solution)/shard_map/all_to_all | solution.py:515
  (21 other events, 125.9 us)
Sparse Core Ops, SparseCore 0:
  12.9 29.8 all-gather.1
  101.8 41.8 reduce-scatter.1

commit v5 on v4

v5 whole, which is shorter than its diff:
```python
import jax
import jax.numpy as jnp
from jax import lax
from jax.experimental import pallas as pl
from jax.experimental.pallas import tpu as pltpu
from jax.sharding import Mesh
from jax.sharding import PartitionSpec as P


KS = 7
DP = ("z", "y")
CH = ("x", "c")
SWAP = [(0, 1), (1, 0)]
EPS = 1e-05


def sent_to_all(array, axis):
    size = lax.axis_size(axis)
    return lax.all_to_all(
        jnp.broadcast_to(array[None], (size, *array.shape)), axis, 0, 0, tiled=True
    )


def rows_of_all(array):
    rows, own = array.shape
    halves = jnp.broadcast_to(array.reshape(1, 2, rows // 2, own), (4, 2, rows // 2, own))
    return lax.all_to_all(halves.reshape(8, rows // 2, own), CH, 0, 0, tiled=True)


def ring_scattered(array, axis):
    here = lax.axis_index(axis)

    def piece(k):
        return lax.dynamic_index_in_dim(array, (here + k) % 4, 0, keepdims=False)

    terms = [piece(0)] + [
        lax.ppermute(piece(k), axis, [(i, (i + k) % 4) for i in range(4)]) for k in (2, 1, 3)
    ]
    return sum(term.astype(jnp.float32) for term in terms)


REACH = KS // 2
TAPS = KS * KS


def spread(field, pad, planes):
    height, width, lanes = field.shape
    pad[:, :8] = jnp.zeros((height, 8, lanes), jnp.float32)
    pad[:, width + 8 :] = jnp.zeros((height, 8, lanes), jnp.float32)
    edge = jnp.zeros((KS, REACH, width, lanes), jnp.float32)
    planes[:, :REACH] = edge
    planes[:, height + REACH :] = edge

    @pl.loop(0, height)
    def _(r):
        pad[r, 8 : width + 8] = field[r].astype(jnp.float32)
        for b in range(KS):
            planes[b, r + REACH] = pad[r, 8 - REACH + b : 8 - REACH + b + width]


BLOCK = 4


def filtered_rows(planes, kernel, start, reverse=False):
    totals = [None] * BLOCK
    for b in range(KS):
        for t in range(BLOCK + KS - 1):
            window = planes[b, start + t]
            for i in range(BLOCK):
                if 0 <= t - i < KS:
                    tap = (t - i) * KS + b
                    tap = TAPS - 1 - tap if reverse else tap
                    term = window * kernel[tap : tap + 1]
                    totals[i] = term if totals[i] is None else totals[i] + term
    return totals


def folded(value):
    return jnp.sum(value.reshape(-1, 8, value.shape[-1]), axis=0)


def tap_sums(planes, upstream, height, width, store, plain=None):
    zero = jnp.zeros((8, planes.shape[-1]), jnp.float32)
    for b in range(KS):

        def step(block, sums):
            start = block * BLOCK
            sums = list(sums)
            for j in range(width // 8):
                cols = pl.ds(8 * j, 8)
                ups = [upstream(start + i, cols) for i in range(BLOCK)]
                for t in range(BLOCK + KS - 1):
                    window = planes[b, start + t, cols]
                    for i in range(BLOCK):
                        if 0 <= t - i < KS:
                            sums[t - i] = sums[t - i] + window * ups[i]
                            if plain is not None:
                                sums[KS + t - i] = sums[KS + t - i] + window
            return tuple(sums)

        count = KS if plain is None else 2 * KS
        sums = lax.fori_loop(0, height // BLOCK, step, (zero,) * count)
        for a in range(KS):
            store(a * KS + b, jnp.sum(sums[a], axis=0, keepdims=True))
            if plain is not None:
                plain(a * KS + b, jnp.sum(sums[KS + a], axis=0, keepdims=True))


def row_store(ref, first):
    def store(tap, row):
        ref[tap // 2, pl.ds(first + tap % 2, 1)] = row

    return store


def filter_kernel(*refs):
    filtered, moments, d_branch, pad, planes = refs[4:9]
    source, cotangent, scale, kernel = refs[9:13]
    copies = [
        pltpu.make_async_copy(refs[i], refs[9 + i], refs[13].at[i]) for i in range(4)
    ]
    for copy in copies:
        copy.start()
    for copy in copies:
        copy.wait()
    spread(source, pad, planes)
    zero = jnp.zeros((8, kernel.shape[1]), jnp.float32)

    def step(block, sums):
        start = block * BLOCK
        first, second = sums
        for i, row in enumerate(filtered_rows(planes, kernel, start)):
            r = start + i
            filtered[r] = row
            d_branch[r] = (cotangent[r].astype(jnp.float32) * scale[...]).astype(jnp.bfloat16)
            first, second = first + folded(row), second + folded(row * row)
        return first, second

    sums = lax.fori_loop(0, source.shape[0] // BLOCK, step, (zero, zero))
    for i in range(2):
        row = jnp.sum(sums[i], axis=0, keepdims=True)
        moments[:, i : i + 1] = jnp.broadcast_to(row[None], (moments.shape[0], *row.shape))


def terms_kernel(source, filtered, mean, sent, pad, planes):
    height, width, _ = source.shape
    sent[...] = jnp.zeros_like(sent)
    spread(source, pad, planes)
    tap_sums(
        planes,
        lambda r, cols: filtered[r, cols] - mean[...],
        height,
        width,
        row_store(sent, 4),
        row_store(sent, 2),
    )


def gather_kernel(
    pieces, source, filtered, rows, bias, base, d_normed, sent, pad, planes
):
    height, width, lanes = source.shape
    mean, rstd, scale, scaled = (rows[i : i + 1] for i in range(4))
    sent[...] = base[...]
    spread(source, pad, planes)
    zero = jnp.zeros((8, lanes), jnp.float32)

    def step(r, carry):
        side = r // (height // 2)
        here = pl.ds(pl.multiple_of((r - side * (height // 2)) * width, width), width)
        row = pieces[side, here].astype(jnp.float32)
        for x in range(1, 4):
            row = row + pieces[2 * x + side, here].astype(jnp.float32)
        d_normed[r] = row
        centered = (filtered[r] - mean) * rstd
        return carry[0] + folded(row * centered), carry[1] + folded(row)

    carry = lax.fori_loop(0, height, step, (zero, zero))
    for i in range(2):
        row = jnp.sum(carry[i], axis=0, keepdims=True)
        sent[:, 6 + i : 7 + i] = jnp.broadcast_to(row[None], (sent.shape[0], 1, lanes))
    tail = pieces[0, pl.ds(height * width // 2, 16)].astype(jnp.float32)
    for k in range(1, 8):
        tail = tail + pieces[k, pl.ds(height * width // 2, 16)].astype(jnp.float32)
    store = row_store(sent, 0)
    for q in range(4):
        store(TAPS + q, bias[:, q * lanes : (q + 1) * lanes])
    store(TAPS + 4, jnp.sum(tail, axis=0, keepdims=True) / scale)
    tap_sums(
        planes,
        lambda r, cols: d_normed[r, cols],
        height,
        width,
        lambda tap, row: store(tap, scaled * row),
    )


def input_kernel(d_normed, filtered, cotangent, kernel, rows, d_input, field, pad, planes):
    height = d_normed.shape[0]
    mean, rstd, scaled, shift, slope = (rows[i : i + 1] for i in range(5))

    @pl.loop(0, height)
    def _(r):
        centered = (filtered[r] - mean) * rstd
        field[r] = scaled * (d_normed[r] - shift - centered * slope)

    spread(field, pad, planes)

    @pl.loop(0, height // BLOCK)
    def _(block):
        start = block * BLOCK
        for i, row in enumerate(filtered_rows(planes, kernel, start, reverse=True)):
            r = start + i
            d_input[r] = (cotangent[r].astype(jnp.float32) + row).astype(jnp.bfloat16)


def conv_scratch(shape):
    height, width, lanes = shape
    return (
        pltpu.VMEM((height, width + 16, lanes), jnp.float32),
        pltpu.VMEM((KS, height + 2 * REACH, width, lanes), jnp.float32),
    )


GELU_A = 0.7978845608028654
GELU_B = 0.044715
TILE = 256
DOT_ROWS = (((0,), (0,)), ((), ()))
DOT_PLAIN = (((1,), (0,)), ((), ()))
DOT_COLS = (((1,), (1,)), ((), ()))


def dot(a, b, dims):
    return lax.dot_general(a, b, dims, preferred_element_type=jnp.float32)


def in_hbm(array):
    return pltpu.with_memory_space_constraint(array, pltpu.HBM)


def kernel_call(kernel, outs, operands, flops, scalar=False, scratch=(), space=pltpu.VMEM):
    vmem = pl.BlockSpec(memory_space=pltpu.VMEM)
    specs = [pl.BlockSpec(memory_space=space)] * len(operands)
    if scalar:
        specs[0] = pl.BlockSpec(memory_space=pltpu.SMEM)
    return pl.pallas_call(
        kernel,
        out_shape=[jax.ShapeDtypeStruct(s, t) for s, t in outs],
        in_specs=specs,
        out_specs=[vmem] * len(outs),
        scratch_shapes=list(scratch),
        cost_estimate=pl.CostEstimate(flops=flops, bytes_accessed=8 << 20, transcendentals=0),
        compiler_params=pltpu.CompilerParams(vmem_limit_bytes=24 << 20),
    )(*operands)


def joined(pieces, start, size):
    return jnp.concatenate([pieces[k, pl.ds(start, size)] for k in range(8)], axis=1)


def pointwise_kernel(core, z, y_all, w_own, w_pair, b_own, b_pair, v_own_far, v_pair_far, *rest):
    results, rest = rest[:4], rest[4:]
    bias_o, bias_p, held, slopes, scale, v_own, v_pair, pair, own, sems = rest
    act_o, act_p, back_o, back_p, out, grad_out = held[:6]
    y = held[7]
    half = z.shape[1]
    fetched = pltpu.make_async_copy(
        y_all.at[:, pl.ds(pl.multiple_of(core[0] * half, half), half)], y, sems.at[half // TILE, 1]
    )
    fetched = [
        fetched,
        pltpu.make_async_copy(v_own_far, v_own, sems.at[half // TILE, 2]),
        pltpu.make_async_copy(v_pair_far, v_pair, sems.at[half // TILE, 3]),
    ]
    for copy_in in fetched:
        copy_in.start()
    tiles = half // TILE
    bias_o[...] = jnp.zeros_like(bias_o)
    bias_p[...] = jnp.zeros_like(bias_p)
    scale[...] = jnp.zeros_like(scale)

    def copy(m, j):
        rows = pl.ds(pl.multiple_of(m * TILE, TILE), TILE)
        at = (slice(None), rows)
        return pltpu.make_async_copy(held[j].at[at], results[j - 4].at[at], sems.at[m, j])

    @pl.loop(0, tiles)
    def _(m):
        start = pl.multiple_of(m * TILE, TILE)
        rows = pl.ds(start, TILE)
        x = joined(z, start, TILE)
        for w, b, slope, act in (
            (w_own, b_own, slopes[0], act_o),
            (w_pair, b_pair, slopes[1], act_p),
        ):
            hidden = dot(x, w[...], DOT_PLAIN) + b[...]
            square = hidden * hidden
            t = jnp.tanh(GELU_A * (hidden + GELU_B * (square * hidden)))
            part = 0.5 * (1.0 + t)
            act[rows] = (hidden * part).astype(jnp.bfloat16)
            slope[...] = part + (0.5 * GELU_A) * hidden * (1.0 - t * t) * (
                1.0 + 3.0 * GELU_B * square
            )

        @pl.when(m == 0)
        def _():
            for copy_in in fetched:
                copy_in.wait()

        up = joined(y, start, TILE)
        for v, slope, back, bias in (
            (v_own, slopes[0], back_o, bias_o),
            (v_pair, slopes[1], back_p, bias_p),
        ):
            grad = dot(up, v[...], DOT_COLS) * slope[...]
            bias[...] += jnp.sum(grad, axis=0, keepdims=True)
            back[rows] = grad.astype(jnp.bfloat16)
        total = dot(back_o[rows], w_own[...], DOT_COLS) + dot(back_p[rows], w_pair[...], DOT_COLS)
        for k in range(8):
            grad_out[k, rows] = total[:, k * 128 : (k + 1) * 128].astype(jnp.bfloat16)
        copy(m, 5).start()
        total = dot(act_o[rows], v_own[...], DOT_PLAIN) + dot(act_p[rows], v_pair[...], DOT_PLAIN)
        for k in range(8):
            out[k, rows] = total[:, k * 128 : (k + 1) * 128].astype(jnp.bfloat16)
        copy(m, 4).start()
        scale[...] += jnp.sum(up.astype(jnp.float32) * total, axis=0, keepdims=True)

    for k in range(8):
        value = scale[:, k * 128 : (k + 1) * 128]
        high = value.astype(jnp.bfloat16).astype(jnp.float32)
        row = lax.broadcasted_iota(jnp.int32, (16, 128), 0)
        both = jnp.where(row == 0, high, jnp.where(row == 1, value - high, 0.0))
        held[6][k] = both.astype(jnp.bfloat16)
    last = pltpu.make_async_copy(
        held[6], results[1].at[:, pl.ds(half, 16)], sems.at[tiles, 0]
    )
    last.start()

    def grad_copy(k, i):
        here = pl.ds(pl.multiple_of(k * 256, 256), 256)
        grads = (pair, own)[i]
        return pltpu.make_async_copy(
            grads.at[here], results[2 + i].at[here], sems.at[tiles + 1 + i, k]
        )

    width = back_p.shape[1]
    for i, (grads, back, act) in enumerate(((pair, back_p, act_p), (own, back_o, act_o))):

        @pl.loop(0, 4)
        def _(k):
            here = pl.ds(pl.multiple_of(k * 256, 256), 256)
            x = jnp.concatenate([z[2 * k], z[2 * k + 1]], axis=1)
            up = jnp.concatenate([y[2 * k], y[2 * k + 1]], axis=1)
            grads[here, :width] = dot(x, back[...], DOT_ROWS).astype(jnp.bfloat16)
            grads[here, width:] = dot(up, act[...], DOT_ROWS).astype(jnp.bfloat16)
            grad_copy(k, i).start()

    for m in range(tiles):
        for j in (4, 5):
            copy(m, j).wait()
    last.wait()
    for i in range(2):
        for k in range(4):
            grad_copy(k, i).wait()


def pointwise_pass(core, z, y, w_own, w_pair, b_own, b_pair, v_own, v_pair):
    rows, width = z.shape[1], w_own.shape[1]
    vmem = pl.BlockSpec(memory_space=pltpu.VMEM)
    flat, wide = (rows, width), (8, rows, 128)
    outs = [wide, (8, rows + 16, 128)] + [(1024, 2 * width)] * 2
    held = tuple(pltpu.VMEM(s, jnp.bfloat16) for s in [flat] * 4 + [wide, wide, (8, 16, 128), wide])
    return pl.pallas_call(
        lambda *refs: pointwise_kernel(*refs[:15], refs[15:23], refs[23:25], *refs[25:]),
        out_shape=[pltpu.HBM(s, jnp.bfloat16) for s in outs]
        + [jax.ShapeDtypeStruct((1, width), jnp.float32)] * 2,
        in_specs=[pl.BlockSpec(memory_space=pltpu.SMEM), vmem]
        + [pl.BlockSpec(memory_space=pltpu.HBM)]
        + [vmem] * 4
        + [pl.BlockSpec(memory_space=pltpu.HBM)] * 2,
        out_specs=[pl.BlockSpec(memory_space=pltpu.HBM)] * 4 + [vmem] * 2,
        scratch_shapes=[
            *held,
            pltpu.VMEM((TILE, width), jnp.float32),
            pltpu.VMEM((TILE, width), jnp.float32),
            pltpu.VMEM((1, 1024), jnp.float32),
            pltpu.VMEM(v_own.shape, jnp.bfloat16),
            pltpu.VMEM(v_own.shape, jnp.bfloat16),
            pltpu.VMEM((1024, 2 * width), jnp.bfloat16),
            pltpu.VMEM((1024, 2 * width), jnp.bfloat16),
            pltpu.SemaphoreType.DMA((rows // TILE + 3, 6)),
        ],
        cost_estimate=pl.CostEstimate(
            flops=16 * rows * width * 1024, bytes_accessed=8 << 20, transcendentals=0
        ),
        compiler_params=pltpu.CompilerParams(vmem_limit_bytes=36 << 20),
    )(
        core,
        z,
        in_hbm(y),
        w_own,
        w_pair,
        b_own[None],
        b_pair[None],
        in_hbm(v_own),
        in_hbm(v_pair),
    )


def body(
    activations,
    cotangent,
    dw_kernel,
    norm_gain,
    norm_bias,
    w_in,
    b_in,
    w_out,
    layer_scale,
    group_sizes,
):
    channels = activations.shape[3]
    row_count = activations.shape[1] * activations.shape[2]
    core = lax.axis_index("c")
    devices = lax.axis_size(DP)
    position = lax.axis_index(DP)
    groups = group_sizes.shape[0]
    group_ends = jnp.cumsum(group_sizes)
    positions = jnp.arange(devices, dtype=jnp.int32)
    labels = jnp.sum((group_ends[None, :] <= positions[:, None]).astype(jnp.int32), axis=1)
    own_group = jnp.sum((group_ends <= position).astype(jnp.int32))
    owners = (jnp.arange(groups, dtype=jnp.int32)[:, None] == labels[None, :]).astype(jnp.float32)
    member = (jnp.arange(groups, dtype=jnp.int32) == own_group).astype(jnp.float32)
    own_count = jnp.sum(member * group_sizes.astype(jnp.float32)) * row_count
    own_gain = jnp.sum(member[:, None] * norm_gain, axis=0)
    own_bias = jnp.sum(member[:, None] * norm_bias, axis=0)

    w_in_pair = lax.ppermute(w_in, "c", SWAP)
    w_out_pair = lax.ppermute(w_out, "c", SWAP)
    b_in_pair = lax.ppermute(b_in, "c", SWAP)

    image = activations.shape[1:]
    source = activations[0]
    scratch = conv_scratch(image)
    operands = (source, cotangent[0], layer_scale[None], dw_kernel)
    filtered, moments, d_branch = kernel_call(
        filter_kernel,
        [(image, jnp.float32), ((devices, 2, channels), jnp.float32), (image, jnp.bfloat16)],
        tuple(in_hbm(a) for a in operands),
        1 << 29,
        scratch=(
            *scratch,
            *(pltpu.VMEM(a.shape, a.dtype) for a in operands),
            pltpu.SemaphoreType.DMA((4,)),
        ),
        space=pltpu.HBM,
    )
    everyone = lax.all_gather(d_branch.reshape(row_count, channels), CH)
    per_device = lax.all_to_all(moments, DP, 0, 0, tiled=True)
    counts = group_sizes.astype(jnp.float32)[:, None] * row_count
    totals = jnp.sum(owners[:, :, None, None] * per_device[None], axis=1)
    group_mean = totals[:, 0] / counts
    group_rstd = lax.rsqrt(totals[:, 1] / counts - group_mean * group_mean + EPS)
    own_mean = jnp.sum(member[:, None] * group_mean, axis=0)
    own_rstd = jnp.sum(member[:, None] * group_rstd, axis=0)
    centered = (filtered.reshape(row_count, channels) - own_mean) * own_rstd
    normed = (centered * own_gain + own_bias).astype(jnp.bfloat16)
    (base,) = kernel_call(
        terms_kernel,
        [((devices, 8, channels), jnp.float32)],
        (source, filtered, moments[0, :1] / row_count),
        1 << 29,
        scratch=scratch,
    )
    gathered = rows_of_all(normed)
    gathered, base = lax.optimization_barrier((gathered, base))

    where = core.astype(jnp.int32)[None]
    (
        partial_branch,
        partial_normed,
        for_pair,
        own_grads,
        bias_own,
        bias_pair,
    ) = pointwise_pass(where, gathered, everyone, w_in, w_in_pair, b_in, b_in_pair, w_out, w_out_pair)
    normed_pieces = lax.all_to_all(partial_normed, CH, 0, 0, tiled=True)
    from_pair = lax.ppermute(for_pair, "c", SWAP)
    both_local = own_grads.astype(jnp.float32) + from_pair.astype(jnp.float32)
    both_local = both_local.astype(jnp.bfloat16)
    hidden_cols = w_in.shape[1]
    bias_local = bias_own + lax.ppermute(bias_pair, "c", SWAP)
    near = lax.psum_scatter(both_local, "z", scatter_dimension=0, tiled=True)

    from_mean = per_device[:, 0] / row_count - jnp.sum(
        owners[:, :, None] * group_mean[:, None], axis=0
    )
    own_scaled = own_gain * own_rstd
    d_normed, sent = kernel_call(
        gather_kernel,
        [(image, jnp.float32), (base.shape, jnp.float32)],
        (
            normed_pieces,
            source,
            filtered,
            jnp.stack([own_mean, own_rstd, layer_scale, own_scaled]),
            bias_local,
            base,
        ),
        1 << 29,
        scratch=scratch,
    )
    sent, partial_branch = lax.optimization_barrier((sent, partial_branch))
    parts = lax.all_to_all(sent, DP, 0, 0, tiled=True)
    halves = (4, 2, row_count // 2, channels)
    chip_branch = ring_scattered(partial_branch.reshape(halves), "x").astype(jnp.bfloat16)
    kept = lax.dynamic_index_in_dim(chip_branch, core, 0, keepdims=False)
    given = lax.dynamic_index_in_dim(chip_branch, 1 - core, 0, keepdims=False)
    taken = lax.ppermute(given, "c", SWAP)
    branch = jnp.concatenate(
        [jnp.where(core == 0, kept, taken), jnp.where(core == 0, taken, kept)]
    ).astype(jnp.float32)
    initial = activations.reshape(row_count, channels).astype(jnp.float32)
    result = (initial + layer_scale * branch).astype(jnp.bfloat16).reshape(activations.shape)
    grad_totals = jnp.sum(owners[:, :, None, None] * parts[None, :, 6:], axis=1)
    d_gain = grad_totals[:, 0]
    d_bias = grad_totals[:, 1]
    from_mean = per_device[:, 0] / row_count - jnp.sum(
        owners[:, :, None] * group_mean[:, None], axis=0
    )
    rest_parts = parts[:, 4:6] + from_mean[:, None] * parts[:, 2:4]
    scaled_all = norm_gain * group_rstd / counts
    flat_weight = jnp.sum(owners[:, :, None] * (scaled_all * d_bias)[:, None], axis=0)
    rest_weight = jnp.sum(
        owners[:, :, None] * (scaled_all * group_rstd * d_gain)[:, None], axis=0
    )
    piece = jnp.sum(
        parts[:, :2]
        - flat_weight[:, None] * parts[:, 2:4]
        - rest_weight[:, None] * rest_parts,
        axis=0,
    )
    total = sent_to_all(piece, DP).reshape(64, channels)
    d_kernel = total[:TAPS]
    d_b_in = total[TAPS : TAPS + 4].ravel()
    d_scale = total[TAPS + 4]
    own_dgain = jnp.sum(member[:, None] * d_gain, axis=0)
    own_dbias = jnp.sum(member[:, None] * d_bias, axis=0)
    rows = jnp.stack(
        [own_mean, own_rstd, own_scaled, own_dbias / own_count, own_dgain / own_count]
    )
    (d_input,) = kernel_call(
        input_kernel,
        [(image, jnp.bfloat16)],
        (d_normed, filtered, cotangent[0], dw_kernel, rows),
        1 << 29,
        scratch=(pltpu.VMEM(image, jnp.float32), *scratch),
    )
    d_input = d_input[None]
    both_sums = ring_scattered(near.reshape(4, -1, near.shape[1]), "y")
    d_w_in = both_sums[:, :hidden_cols]
    d_w_out = both_sums[:, hidden_cols:].T
    return (result, d_input, d_kernel, d_gain, d_bias, d_w_in, d_b_in, d_w_out, d_scale)


def solution(mesh):
    split = Mesh(mesh.devices.reshape(8, 4, 4, 2), ("z", "y", "x", "c"))
    in_specs = (
        P(DP, None, None, CH),
        P(DP, None, None, CH),
        P(None, CH),
        P(None, CH),
        P(None, CH),
        P(None, CH),
        P(CH),
        P(CH, None),
        P(CH),
        P(),
    )
    out_specs = (
        P(DP, None, None, CH),
        P(DP, None, None, CH),
        P(None, CH),
        P(None, CH),
        P(None, CH),
        P(DP, CH),
        P(CH),
        P(CH, DP),
        P(CH),
    )
    return jax.shard_map(body, mesh=split, in_specs=in_specs, out_specs=out_specs, check_vma=False)
```

time: 164 us -> 153 us (0.933); the launches traced: 163 us -> 151 us
  local copies, waits for them, and re-layouts: 17.4 us -> 6.36 us
  Pallas kernels: 32.9 us -> 27.7 us
  waiting for transfers between devices: 42.8 us -> 47.4 us
    all_to_all x2 -> x1, starting transfers between devices: 15.7 us -> 4.01 us  [sent_to_all(): lax.all_to_all(jnp.broadcast_to(array[None], (size, *array.shape)), axis,...]
    unnamed x54 -> x22, local copies, waits for them, and re-layouts: 9.59 us -> 0.05 us
    pallas_call x6 -> x4, Pallas kernels: 23.4 us -> 14.7 us  [kernel_call(): pl.pallas_call(kernel, out_shape=[jax.ShapeDtypeStruct(s, t) for s, t in...]
    all_to_all x1, starting transfers between devices: 4.33 us -> 11.5 us  [body(): per_device = lax.all_to_all(moments, DP, 0, 0, tiled=True)]
    all_to_all x1, waiting for transfers between devices: 4.7 us -> 11.2 us  [body(): normed_pieces = lax.all_to_all(partial_normed, CH, 0, 0, tiled=True)]
    all_to_all x2 -> x1, waiting for transfers between devices: 10.2 us -> 5.1 us  [sent_to_all(): lax.all_to_all(jnp.broadcast_to(array[None], (size, *array.shape)), axis,...]
    reduce_scatter x1, waiting for transfers between devices: 4.54 us -> 0.02 us  [body(): near = lax.psum_scatter(both_local, 'z', scatter_dimension=0, tiled=True)]
    ppermute x1, waiting for transfers between devices: 0.01 us -> 4.36 us  [body(): from_pair = lax.ppermute(for_pair, 'c', SWAP)]
  transfers between devices with their start and end apart: 18 -> 19, of which waited for: 8 -> 10; matrix products, arithmetic and copies ran while one was open for 7% -> 7% of each run, Pallas kernels for 9% -> 7%
where the time goes in v5:
time: 153 us; the launch traced here: 151 us
  waiting for transfers between devices  47.4 us (31%)
  starting transfers between devices  43.1 us (28%)
  Pallas kernels  27.7 us (18%)
  between operations  15.1 us (10%)
  other arithmetic  10.9 us (7%)
  local copies, waits for them, and re-layouts  6.36 us (4%)
    pallas_call x4, Pallas kernels, kernel_call(): pl.pallas_call(kernel, out_shape=[jax.ShapeDtypeStruct(s, t) for s, t in...  14.7 us
    pallas_call x1, Pallas kernels, pointwise_pass(): pl.pallas_call(lambda *refs: pointwise_kernel(*refs[:15], refs[15:23], re...  13 us
    all_to_all x1, starting transfers between devices, body(): per_device = lax.all_to_all(moments, DP, 0, 0, tiled=True)  11.5 us
    all_to_all x1, waiting for transfers between devices, body(): normed_pieces = lax.all_to_all(partial_normed, CH, 0, 0, tiled=True)  11.2 us
    ppermute x6, starting transfers between devices, ring_scattered(): lax.ppermute(piece(k), axis, [(i, (i + k) % 4) for i in range(4)])  8.82 us
    all_to_all x1, waiting for transfers between devices, rows_of_all(): lax.all_to_all(halves.reshape(8, rows // 2, own), CH, 0, 0, tiled=True)  8.56 us
    all_to_all x1, starting transfers between devices, body(): normed_pieces = lax.all_to_all(partial_normed, CH, 0, 0, tiled=True)  6.63 us
    all_to_all x1, waiting for transfers between devices, body(): per_device = lax.all_to_all(moments, DP, 0, 0, tiled=True)  6.44 us
  transfers between devices with their start and end apart: 19, of which 10 were waited for; matrix products, arithmetic and copies ran while one was open for 7% of the time, Pallas kernels for 7%

profile of v5, /device:TPU:4, one launch (start us, length us, event | category | flops | bytes accessed | tf_op | source)
XLA Modules:
  0.0 150.6 jit_solution(10833921094288690191)
XLA Ops:
  7.3 4.5 %shard_map.169 = (f32[16,64,128]{2,1,0:T(8,128)S(1)}, f32[32,2,128]{2,1,0:T(2,128)}, bf16[16,64,128]{2,1,0:T(8,128)(2,1)}) custom-call(bf16[16,64,128]{2,1,0:T(8,128)(2,1)} %bitcast.83, bf16[16,64,128]{2,1,0:T(8,128)(2,1)} %bitcast.86, f32[1,128]{1,0:T(1,128)} %bitcast.112, f32[49,128]{1,0:T(8,128)} %kernel.1), custom_call_target="tpu_custom_call" | custom-call | flops 536870912 | bytes 8388608 | tf_op jit(solution)/shard_map/pallas_call | solution.py:246
  11.8 11.5 %all-to-all-start = ((f32[32,2,128]{2,1,0:T(2,128)}), f32[32,2,128]{2,1,0:T(2,128)S(1)}, u32[]{:S(2)}, u32[]{:S(2)}) async-start(f32[32,2,128]{2,1,0:T(2,128)} %get-tuple-element.25), calls=%async_computation | async-start | bytes 65536 | tf_op jit(solution)/shard_map/all_to_all | solution.py:459
  24.8 1.2 fusion.16
  26.7 6.4 %all-to-all-done = f32[32,2,128]{2,1,0:T(2,128)S(1)} async-done(((f32[32,2,128]{2,1,0:T(2,128)}), f32[32,2,128]{2,1,0:T(2,128)S(1)}, u32[]{:S(2)}, u32[]{:S(2)}) %all-to-all-start) | async-done | bytes 32800 | tf_op jit(solution)/shard_map/all_to_all | solution.py:459
  34.6 4.8 %all-to-all-start.1 = ((bf16[8,512,128]{2,1,0:T(8,128)(2,1)}), bf16[8,512,128]{2,1,0:T(8,128)(2,1)S(1)}, u32[]{:S(2)}, u32[]{:S(2)}) async-start(bf16[8,512,128]{2,1,0:T(8,128)(2,1)} %bitcast.90), calls=%async_computation.1 | async-start | bytes 2097152 | tf_op jit(solution)/shard_map/all_to_all | solution.py:27
  40.3 3.3 %shard_map.170.base = f32[32,8,128]{2,1,0:T(8,128)S(1)} custom-call(bf16[16,64,128]{2,1,0:T(8,128)(2,1)S(1)} %bitcast.84, f32[16,64,128]{2,1,0:T(8,128)S(1)} %get-tuple-element.24.filtered, f32[1,128]{1,0:T(1,128)S(1)} %multiply_bitcast_fusion.mean), custom_call_target="tpu_custom_call" | custom-call | flops 536870912 | bytes 8388608 | tf_op jit(solution)/shard_map/pallas_call | solution.py:246
  43.7 8.6 %all-to-all-done.1.refs_1_ = bf16[8,512,128]{2,1,0:T(8,128)(2,1)S(1)} async-done(((bf16[8,512,128]{2,1,0:T(8,128)(2,1)}), bf16[8,512,128]{2,1,0:T(8,128)(2,1)S(1)}, u32[]{:S(2)}, u32[]{:S(2)}) %all-to-all-start.1) | async-done | bytes 1048608 | tf_op jit(solution)/shard_map/all_to_all | solution.py:27
  52.3 13.0 %shard_map.171 = (bf16[8,512,128]{2,1,0:T(8,128)(2,1)}, bf16[8,528,128]{2,1,0:T(8,128)(2,1)}, bf16[1024,1024]{1,0:T(8,128)(2,1)}, bf16[1024,1024]{1,0:T(8,128)(2...) custom-call(s32[1]{0:T(128)} %bitcast.refs_0_, bf16[8,512,128]{2,1,0:T(8,128)(2,1)S(1)} %all-to-all-done.1.refs_1_, ...), custom_call_target="tpu_custom_call" | custom-call | flops 4294967296 | bytes 8388608 | tf_op jit(solution)/shard_map/pallas_call | solution.py:373
  65.4 4.4 %collective-permute-done.8 = bf16[1024,1024]{1,0:T(8,128)(2,1)S(1)} collective-permute-done((bf16[1024,1024]{1,0:T(8,128)(2,1)}, bf16[1024,1024]{1,0:T(8,128)(2,1)S(1)}, u32[]{:S(2)}, u32[]{:S(2)}) %collective-permute-start.8) | collective-permute-done | bytes 2097184 | tf_op jit(solution)/shard_map/ppermute | solution.py:488
  69.7 3.9 %add_convert_fusion = bf16[1024,1024]{1,0:T(8,128)(2,1)} fusion(bf16[1024,1024]{1,0:T(8,128)(2,1)S(1)} %collective-permute-done.8, bf16[1024,1024]{1,0:T(8,128)(2,1)} %get-tuple-element.37), kind=kLoop, calls=%fused_computation | loop fusion | flops 4194304 | bytes 6291456 | tf_op jit(solution)/shard_map/convert_element_type | solution.py:490
  73.7 6.6 %all-to-all-start.2 = ((bf16[8,528,128]{2,1,0:T(8,128)(2,1)}), bf16[8,528,128]{2,1,0:T(8,128)(2,1)S(1)}, u32[]{:S(2)}, u32[]{:S(2)}) async-start(bf16[8,528,128]{2,1,0:T(8,128)(2,1)} %get-tuple-element.28), calls=%async_computation.2 | async-start | bytes 2162688 | tf_op jit(solution)/shard_map/all_to_all | solution.py:487
  82.2 11.2 %all-to-all-done.2.pieces = bf16[8,528,128]{2,1,0:T(8,128)(2,1)S(1)} async-done(((bf16[8,528,128]{2,1,0:T(8,128)(2,1)}), bf16[8,528,128]{2,1,0:T(8,128)(2,1)S(1)}, u32[]{:S(2)}, u32[]{:S(2)}) %all-to-all-start.2) | async-done | bytes 1081376 | tf_op jit(solution)/shard_map/all_to_all | solution.py:487
  93.4 3.4 %shard_map.172 = (f32[16,64,128]{2,1,0:T(8,128)S(1)}, f32[32,8,128]{2,1,0:T(8,128)}) custom-call(bf16[8,528,128]{2,1,0:T(8,128)(2,1)S(1)} %all-to-all-done.2.pieces, bf16[16,64,128]{2,1,0:T(8,128)(2,1)S(1)} %bitcast.85, f32[16,64,128]{2,1,0:T(8,128)S(1)} %get-tuple-element.24.filtered, f32[4,128]{1,0:T(4,128)S(1)} %pad_maximum_fusion.1.rows, ...), custom_call_target="tpu_custom_call" | custom-call | flops 536870912 | bytes 8388608 | tf_op jit(solution)/shard_map/pallas_call | solution.py:246
  96.9 6.1 %all-to-all-start.3 = ((f32[32,8,128]{2,1,0:T(8,128)}), f32[32,8,128]{2,1,0:T(8,128)S(1)}, u32[]{:S(2)}, u32[]{:S(2)}) async-start(f32[32,8,128]{2,1,0:T(8,128)} %get-tuple-element.36), calls=%async_computation.3 | async-start | bytes 262144 | tf_op jit(solution)/shard_map/all_to_all | solution.py:514
  103.1 1.2 dynamic-slice_bitcast_fusion.2
  104.2 3.4 %collective-permute-start.4 = (bf16[2,512,128]{2,1,0:T(8,128)(2,1)S(1)}, bf16[2,512,128]{2,1,0:T(8,128)(2,1)S(1)}, u32[]{:S(2)}, u32[]{:S(2)}) collective-permute-start(bf16[2,512,128]{2,1,0:T(8,128)(2,1)S(1)} %get-tuple-element.49), channel_id=1, source_target_pairs={{0,4},{2,6},{4,0},{6,2},{1,5},{3,7},{5,1},{7,3},{8,12},{10,14},{12... | collective-permute-start | bytes 786440 | tf_op jit(solution)/shard_map/ppermute | solution.py:37
  107.6 1.2 collective-permute-start.5
  109.7 5.8 %all-to-all-done.3 = f32[32,8,128]{2,1,0:T(8,128)S(1)} async-done(((f32[32,8,128]{2,1,0:T(8,128)}), f32[32,8,128]{2,1,0:T(8,128)S(1)}, u32[]{:S(2)}, u32[]{:S(2)}) %all-to-all-start.3) | async-done | bytes 131104 | tf_op jit(solution)/shard_map/all_to_all | solution.py:514
  116.5 4.0 %all-to-all-start.4 = ((f32[32,2,128]{2,1,0:T(2,128)}), f32[32,2,128]{2,1,0:T(2,128)S(1)}, u32[]{:S(2)}, u32[]{:S(2)}) async-start(f32[32,2,128]{2,1,0:T(2,128)} %broadcast_in_dim.26), calls=%async_computation.4 | async-start | bytes 65536 | tf_op jit(solution)/shard_map/all_to_all | solution.py:19
  120.6 3.5 %shard_map.173 = bf16[16,64,128]{2,1,0:T(8,128)(2,1)} custom-call(f32[16,64,128]{2,1,0:T(8,128)S(1)} %get-tuple-element.35.d_normed, f32[16,64,128]{2,1,0:T(8,128)S(1)} %get-tuple-element.24.filtered, bf16[16,64,128]{2,1,0:T(8,128)(2,1)S(1)} %bitcast.87, f32[49,128]{1,0:T(8,128)S(1)} %copy-done.3, f32[5,128]{1,0:T(8,128)S(1)} %stack.5.rows), custom_call_target="tpu_custom_call" | custom-call | flops 536870912 | bytes 8388608 | tf_op jit(solution)/shard_map/pallas_call | solution.py:246
  125.3 5.1 %all-to-all-done.4 = f32[32,2,128]{2,1,0:T(2,128)S(1)} async-done(((f32[32,2,128]{2,1,0:T(2,128)}), f32[32,2,128]{2,1,0:T(2,128)S(1)}, u32[]{:S(2)}, u32[]{:S(2)}) %all-to-all-start.4) | async-done | bytes 32800 | tf_op jit(solution)/shard_map/all_to_all | solution.py:19
  133.8 2.7 %collective-permute-start.11 = (bf16[32,1024]{1,0:T(8,128)(2,1)S(1)}, bf16[32,1024]{1,0:T(8,128)(2,1)S(1)}, u32[]{:S(2)}, u32[]{:S(2)}) collective-permute-start(bf16[32,1024]{1,0:T(8,128)(2,1)S(1)} %get-tuple-element.55), channel_id=1, source_target_pairs={{0,24},{8,0},{16,8},{24,16},{1,25},{9,1},{17,9},{25,17},{2,26},{10... | collective-permute-start | bytes 196616 | tf_op jit(solution)/shard_map/ppermute | solution.py:37
  137.3 1.4 collective-permute-done.10
  139.0 3.3 %collective-permute-done.9 = bf16[32,1024]{1,0:T(8,128)(2,1)S(1)} collective-permute-done((bf16[32,1024]{1,0:T(8,128)(2,1)S(1)}, bf16[32,1024]{1,0:T(8,128)(2,1)S(1)}, u32[]{:S(2)}, u32[]{:S(2)}) %collective-permute-start.9) | collective-permute-done | bytes 65568 | tf_op jit(solution)/shard_map/ppermute | solution.py:37
  (84 shorter events, 15.2 us)
Async XLA Ops:
  7.2 16.7 %copy-start.10 = (s32[4]{0:T(128)S(1)}, s32[4]{0:T(128)}, u32[]{:S(2)}) copy-start(s32[4]{0:T(128)} %param.19) | copy-start | bytes 52
  7.2 26.0 %copy-start.5 = (f32[4,128]{1,0:T(4,128)S(1)}, f32[4,128]{1,0:T(4,128)}, u32[]{:S(2)}) copy-start(f32[4,128]{1,0:T(4,128)} %param.13) | copy-start | bytes 6148
  7.2 26.0 %copy-start.8 = (f32[4,128]{1,0:T(4,128)S(1)}, f32[4,128]{1,0:T(4,128)}, u32[]{:S(2)}) copy-start(f32[4,128]{1,0:T(4,128)} %param.14) | copy-start | bytes 6148
  7.2 45.0 %all-gather.2.cloned.1.call-start = ((), (), s32[]{:S(2)}) async-start(), calls=%async_computation.6 | async-start | bytes 2359296 | tf_op jit(solution)/shard_map/all_gather | solution.py:458
  11.8 21.4 %all-to-all-start = ((f32[32,2,128]{2,1,0:T(2,128)}), f32[32,2,128]{2,1,0:T(2,128)S(1)}, u32[]{:S(2)}, u32[]{:S(2)}) async-start(f32[32,2,128]{2,1,0:T(2,128)} %get-tuple-element.25), calls=%async_computation | async-start | bytes 65536 | tf_op jit(solution)/shard_map/all_to_all | solution.py:459
  23.3 29.0 %collective-permute-start = (bf16[1024,512]{1,0:T(8,128)(2,1)S(1)}, bf16[1024,512]{1,0:T(8,128)(2,1)}, u32[]{:S(2)}, u32[]{:S(2)}) collective-permute-start(bf16[1024,512]{1,0:T(8,128)(2,1)S(1)} %copy-done.1), channel_id=1, source_target_pairs={{0,1},{1,0},{2,3},{3,2},{4,5},{5,4},{6,7},{7,6},{8,9},{9,8},{10,11... | collective-permute-start | bytes 3145736 | tf_op jit(solution)/shard_map/ppermute | solution.py:438
  23.4 28.9 %collective-permute-start.2 = (bf16[512,1024]{1,0:T(8,128)(2,1)}, bf16[512,1024]{1,0:T(8,128)(2,1)}, u32[]{:S(2)}, u32[]{:S(2)}) collective-permute-start(bf16[512,1024]{1,0:T(8,128)(2,1)} %refs_7_.1), channel_id=1, source_target_pairs={{0,1},{1,0},{2,3},{3,2},{4,5},{5,4},{6,7},{7,6},{8,9},{9,8},{10,11... | collective-permute-start | bytes 3145736 | tf_op jit(solution)/shard_map/ppermute | solution.py:439
  34.6 17.6 %all-to-all-start.1 = ((bf16[8,512,128]{2,1,0:T(8,128)(2,1)}), bf16[8,512,128]{2,1,0:T(8,128)(2,1)S(1)}, u32[]{:S(2)}, u32[]{:S(2)}) async-start(bf16[8,512,128]{2,1,0:T(8,128)(2,1)} %bitcast.90), calls=%async_computation.1 | async-start | bytes 2097152 | tf_op jit(solution)/shard_map/all_to_all | solution.py:27
  39.4 92.8 %reduce-scatter.2.cloned.1.call-start = ((), (), s32[]{:S(2)}) async-start(), calls=%async_computation.7 | async-start | bytes 2359296 | tf_op jit(solution)/shard_map/reduce_scatter | solution.py:493
  39.4 12.8 %collective-permute-start.1 = (f32[512]{0:T(512)S(1)}, f32[512]{0:T(512)S(1)}, u32[]{:S(2)}, u32[]{:S(2)}) collective-permute-start(f32[512]{0:T(512)S(1)} %copy-done.4), channel_id=1, source_target_pairs={{0,1},{1,0},{2,3},{3,2},{4,5},{5,4},{6,7},{7,6},{8,9},{9,8},{10,11... | collective-permute-start | bytes 6152 | tf_op jit(solution)/shard_map/ppermute | solution.py:440
  65.3 4.5 %collective-permute-start.8 = (bf16[1024,1024]{1,0:T(8,128)(2,1)}, bf16[1024,1024]{1,0:T(8,128)(2,1)S(1)}, u32[]{:S(2)}, u32[]{:S(2)}) collective-permute-start(bf16[1024,1024]{1,0:T(8,128)(2,1)} %get-tuple-element.38), channel_id=1, source_target_pairs={{0,1},{1,0},{2,3},{3,2},{4,5},{5,4},{6,7},{7,6},{8,9},{9,8},{10,11... | collective-permute-start | bytes 6291464 | tf_op jit(solution)/shard_map/ppermute | solution.py:488
  73.7 19.8 %all-to-all-start.2 = ((bf16[8,528,128]{2,1,0:T(8,128)(2,1)}), bf16[8,528,128]{2,1,0:T(8,128)(2,1)S(1)}, u32[]{:S(2)}, u32[]{:S(2)}) async-start(bf16[8,528,128]{2,1,0:T(8,128)(2,1)} %get-tuple-element.28), calls=%async_computation.2 | async-start | bytes 2162688 | tf_op jit(solution)/shard_map/all_to_all | solution.py:487
  81.0 1.3 collective-permute-start.3
  82.2 38.4 %copy-start.2 = (bf16[1,16,64,128]{3,2,1,0:T(8,128)(2,1)S(1)}, bf16[1,16,64,128]{3,2,1,0:T(8,128)(2,1)}, u32[]{:S(2)}) copy-start(bf16[1,16,64,128]{3,2,1,0:T(8,128)(2,1)} %param.11) | copy-start | bytes 786436
  82.2 38.4 %copy-start.3 = (f32[49,128]{1,0:T(8,128)S(1)}, f32[49,128]{1,0:T(8,128)}, u32[]{:S(2)}) copy-start(f32[49,128]{1,0:T(8,128)} %kernel.1) | copy-start | bytes 75268
  96.9 18.6 %all-to-all-start.3 = ((f32[32,8,128]{2,1,0:T(8,128)}), f32[32,8,128]{2,1,0:T(8,128)S(1)}, u32[]{:S(2)}, u32[]{:S(2)}) async-start(f32[32,8,128]{2,1,0:T(8,128)} %get-tuple-element.36), calls=%async_computation.3 | async-start | bytes 262144 | tf_op jit(solution)/shard_map/all_to_all | solution.py:514
  104.2 19.8 %collective-permute-start.4 = (bf16[2,512,128]{2,1,0:T(8,128)(2,1)S(1)}, bf16[2,512,128]{2,1,0:T(8,128)(2,1)S(1)}, u32[]{:S(2)}, u32[]{:S(2)}) collective-permute-start(bf16[2,512,128]{2,1,0:T(8,128)(2,1)S(1)} %get-tuple-element.49), channel_id=1, source_target_pairs={{0,4},{2,6},{4,0},{6,2},{1,5},{3,7},{5,1},{7,3},{8,12},{10,14},{12... | collective-permute-start | bytes 786440 | tf_op jit(solution)/shard_map/ppermute | solution.py:37
  107.6 16.4 %collective-permute-start.5 = (bf16[2,512,128]{2,1,0:T(8,128)(2,1)S(1)}, bf16[2,512,128]{2,1,0:T(8,128)(2,1)S(1)}, u32[]{:S(2)}, u32[]{:S(2)}) collective-permute-start(bf16[2,512,128]{2,1,0:T(8,128)(2,1)S(1)} %get-tuple-element.51), channel_id=1, source_target_pairs={{0,2},{2,4},{4,6},{6,0},{1,3},{3,5},{5,7},{7,1},{8,10},{10,12},{12... | collective-permute-start | bytes 786440 | tf_op jit(solution)/shard_map/ppermute | solution.py:37
  108.8 15.2 %collective-permute-start.6 = (bf16[2,512,128]{2,1,0:T(8,128)(2,1)S(1)}, bf16[2,512,128]{2,1,0:T(8,128)(2,1)S(1)}, u32[]{:S(2)}, u32[]{:S(2)}) collective-permute-start(bf16[2,512,128]{2,1,0:T(8,128)(2,1)S(1)} %get-tuple-element.50), channel_id=1, source_target_pairs={{0,6},{2,0},{4,2},{6,4},{1,7},{3,1},{5,3},{7,5},{8,14},{10,8},{12,... | collective-permute-start | bytes 786440 | tf_op jit(solution)/shard_map/ppermute | solution.py:37
  116.5 13.9 %all-to-all-start.4 = ((f32[32,2,128]{2,1,0:T(2,128)}), f32[32,2,128]{2,1,0:T(2,128)S(1)}, u32[]{:S(2)}, u32[]{:S(2)}) async-start(f32[32,2,128]{2,1,0:T(2,128)} %broadcast_in_dim.26), calls=%async_computation.4 | async-start | bytes 65536 | tf_op jit(solution)/shard_map/all_to_all | solution.py:19
  125.2 6.9 %collective-permute-start.7 = (bf16[512,128]{1,0:T(8,128)(2,1)S(1)}, bf16[512,128]{1,0:T(8,128)(2,1)S(1)}, u32[]{:S(2)}, u32[]{:S(2)}) collective-permute-start(bf16[512,128]{1,0:T(8,128)(2,1)S(1)} %dynamic-slice_bitcast_fusion.3), channel_id=1, source_target_pairs={{0,1},{1,0},{2,3},{3,2},{4,5},{5,4},{6,7},{7,6},{8,9},{9,8},{10,11... | collective-permute-start | bytes 393224 | tf_op jit(solution)/shard_map/ppermute | solution.py:519
  133.1 5.6 %collective-permute-start.10 = (bf16[32,1024]{1,0:T(8,128)(2,1)S(1)}, bf16[32,1024]{1,0:T(8,128)(2,1)S(1)}, u32[]{:S(2)}, u32[]{:S(2)}) collective-permute-start(bf16[32,1024]{1,0:T(8,128)(2,1)S(1)} %get-tuple-element.56), channel_id=1, source_target_pairs={{0,8},{8,16},{16,24},{24,0},{1,9},{9,17},{17,25},{25,1},{2,10},{10... | collective-permute-start | bytes 196616 | tf_op jit(solution)/shard_map/ppermute | solution.py:37
  133.8 5.2 %collective-permute-start.11 = (bf16[32,1024]{1,0:T(8,128)(2,1)S(1)}, bf16[32,1024]{1,0:T(8,128)(2,1)S(1)}, u32[]{:S(2)}, u32[]{:S(2)}) collective-permute-start(bf16[32,1024]{1,0:T(8,128)(2,1)S(1)} %get-tuple-element.55), channel_id=1, source_target_pairs={{0,24},{8,0},{16,8},{24,16},{1,25},{9,1},{17,9},{25,17},{2,26},{10... | collective-permute-start | bytes 196616 | tf_op jit(solution)/shard_map/ppermute | solution.py:37
  136.4 5.8 %collective-permute-start.9 = (bf16[32,1024]{1,0:T(8,128)(2,1)S(1)}, bf16[32,1024]{1,0:T(8,128)(2,1)S(1)}, u32[]{:S(2)}, u32[]{:S(2)}) collective-permute-start(bf16[32,1024]{1,0:T(8,128)(2,1)S(1)} %get-tuple-element.54), channel_id=1, source_target_pairs={{0,16},{8,24},{16,0},{24,8},{1,17},{9,25},{17,1},{25,9},{2,18},{10... | collective-permute-start | bytes 196616 | tf_op jit(solution)/shard_map/ppermute | solution.py:37
  (6 other events, 69.7 us)
Sparse Core Ops, SparseCore 0:
  11.9 29.8 all-gather.1
  73.8 43.5 reduce-scatter.1

commit v6 on v5

--- a/solution.py
+++ b/solution.py
@@ -224,7 +224,7 @@
 
 GELU_A = 0.7978845608028654
 GELU_B = 0.044715
-TILE = 256
+TILE = 512
 DOT_ROWS = (((0,), (0,)), ((), ()))
 DOT_PLAIN = (((1,), (0,)), ((), ()))
 DOT_COLS = (((1,), (1,)), ((), ()))
@@ -521,7 +521,8 @@
         [jnp.where(core == 0, kept, taken), jnp.where(core == 0, taken, kept)]
     ).astype(jnp.float32)
     initial = activations.reshape(row_count, channels).astype(jnp.float32)
-    result = (initial + layer_scale * branch).astype(jnp.bfloat16).reshape(activations.shape)
+    result = (initial + layer_scale * branch).astype(jnp.bfloat16)
+    result = result.reshape(activations.shape)
     grad_totals = jnp.sum(owners[:, :, None, None] * parts[None, :, 6:], axis=1)
     d_gain = grad_totals[:, 0]
     d_bias = grad_totals[:, 1]

time: 153 us -> 151 us (0.987)
  no operation moved by 1% of the time
where the time goes in v6:
time: 151 us; the launch traced here: 149 us
  waiting for transfers between devices  47.4 us (31%)
  starting transfers between devices  43 us (28%)
  Pallas kernels  26.4 us (17%)
  between operations  15.1 us (10%)
  other arithmetic  10.9 us (7%)
  local copies, waits for them, and re-layouts  6.36 us (4%)
    pallas_call x4, Pallas kernels, kernel_call(): pl.pallas_call(kernel, out_shape=[jax.ShapeDtypeStruct(s, t) for s, t in...  14.7 us
    pallas_call x1, Pallas kernels, pointwise_pass(): pl.pallas_call(lambda *refs: pointwise_kernel(*refs[:15], refs[15:23], re...  11.8 us
    all_to_all x1, starting transfers between devices, body(): per_device = lax.all_to_all(moments, DP, 0, 0, tiled=True)  11.5 us
    all_to_all x1, waiting for transfers between devices, body(): normed_pieces = lax.all_to_all(partial_normed, CH, 0, 0, tiled=True)  11 us
    ppermute x6, starting transfers between devices, ring_scattered(): lax.ppermute(piece(k), axis, [(i, (i + k) % 4) for i in range(4)])  8.64 us
    all_to_all x1, waiting for transfers between devices, rows_of_all(): lax.all_to_all(halves.reshape(8, rows // 2, own), CH, 0, 0, tiled=True)  8.56 us
    all_to_all x1, starting transfers between devices, body(): normed_pieces = lax.all_to_all(partial_normed, CH, 0, 0, tiled=True)  6.64 us
    all_to_all x1, waiting for transfers between devices, body(): per_device = lax.all_to_all(moments, DP, 0, 0, tiled=True)  6.44 us
  transfers between devices with their start and end apart: 19, of which 10 were waited for; matrix products, arithmetic and copies ran while one was open for 7% of the time, Pallas kernels for 7%

profile of v6, /device:TPU:4, one launch (start us, length us, event | category | flops | bytes accessed | tf_op | source)
XLA Modules:
  0.0 149.1 jit_solution(11399645158610403443)
XLA Ops:
  7.3 4.5 %shard_map.169 = (f32[16,64,128]{2,1,0:T(8,128)S(1)}, f32[32,2,128]{2,1,0:T(2,128)}, bf16[16,64,128]{2,1,0:T(8,128)(2,1)}) custom-call(bf16[16,64,128]{2,1,0:T(8,128)(2,1)} %bitcast.83, bf16[16,64,128]{2,1,0:T(8,128)(2,1)} %bitcast.86, f32[1,128]{1,0:T(1,128)} %bitcast.112, f32[49,128]{1,0:T(8,128)} %kernel.1), custom_call_target="tpu_custom_call" | custom-call | flops 536870912 | bytes 8388608 | tf_op jit(solution)/shard_map/pallas_call | solution.py:246
  11.8 11.5 %all-to-all-start = ((f32[32,2,128]{2,1,0:T(2,128)}), f32[32,2,128]{2,1,0:T(2,128)S(1)}, u32[]{:S(2)}, u32[]{:S(2)}) async-start(f32[32,2,128]{2,1,0:T(2,128)} %get-tuple-element.25), calls=%async_computation | async-start | bytes 65536 | tf_op jit(solution)/shard_map/all_to_all | solution.py:459
  24.8 1.2 fusion.16
  26.7 6.4 %all-to-all-done = f32[32,2,128]{2,1,0:T(2,128)S(1)} async-done(((f32[32,2,128]{2,1,0:T(2,128)}), f32[32,2,128]{2,1,0:T(2,128)S(1)}, u32[]{:S(2)}, u32[]{:S(2)}) %all-to-all-start) | async-done | bytes 32800 | tf_op jit(solution)/shard_map/all_to_all | solution.py:459
  34.6 4.8 %all-to-all-start.1 = ((bf16[8,512,128]{2,1,0:T(8,128)(2,1)}), bf16[8,512,128]{2,1,0:T(8,128)(2,1)S(1)}, u32[]{:S(2)}, u32[]{:S(2)}) async-start(bf16[8,512,128]{2,1,0:T(8,128)(2,1)} %bitcast.90), calls=%async_computation.1 | async-start | bytes 2097152 | tf_op jit(solution)/shard_map/all_to_all | solution.py:27
  40.3 3.3 %shard_map.170.base = f32[32,8,128]{2,1,0:T(8,128)S(1)} custom-call(bf16[16,64,128]{2,1,0:T(8,128)(2,1)S(1)} %bitcast.84, f32[16,64,128]{2,1,0:T(8,128)S(1)} %get-tuple-element.24.filtered, f32[1,128]{1,0:T(1,128)S(1)} %multiply_bitcast_fusion.mean), custom_call_target="tpu_custom_call" | custom-call | flops 536870912 | bytes 8388608 | tf_op jit(solution)/shard_map/pallas_call | solution.py:246
  43.7 8.6 %all-to-all-done.1.refs_1_ = bf16[8,512,128]{2,1,0:T(8,128)(2,1)S(1)} async-done(((bf16[8,512,128]{2,1,0:T(8,128)(2,1)}), bf16[8,512,128]{2,1,0:T(8,128)(2,1)S(1)}, u32[]{:S(2)}, u32[]{:S(2)}) %all-to-all-start.1) | async-done | bytes 1048608 | tf_op jit(solution)/shard_map/all_to_all | solution.py:27
  52.3 11.8 %shard_map.171 = (bf16[8,512,128]{2,1,0:T(8,128)(2,1)}, bf16[8,528,128]{2,1,0:T(8,128)(2,1)}, bf16[1024,1024]{1,0:T(8,128)(2,1)}, bf16[1024,1024]{1,0:T(8,128)(2...) custom-call(s32[1]{0:T(128)} %bitcast.refs_0_, bf16[8,512,128]{2,1,0:T(8,128)(2,1)S(1)} %all-to-all-done.1.refs_1_, ...), custom_call_target="tpu_custom_call" | custom-call | flops 4294967296 | bytes 8388608 | tf_op jit(solution)/shard_map/pallas_call | solution.py:373
  64.1 4.4 %collective-permute-done.8 = bf16[1024,1024]{1,0:T(8,128)(2,1)S(1)} collective-permute-done((bf16[1024,1024]{1,0:T(8,128)(2,1)}, bf16[1024,1024]{1,0:T(8,128)(2,1)S(1)}, u32[]{:S(2)}, u32[]{:S(2)}) %collective-permute-start.8) | collective-permute-done | bytes 2097184 | tf_op jit(solution)/shard_map/ppermute | solution.py:488
  68.5 3.9 %add_convert_fusion = bf16[1024,1024]{1,0:T(8,128)(2,1)} fusion(bf16[1024,1024]{1,0:T(8,128)(2,1)S(1)} %collective-permute-done.8, bf16[1024,1024]{1,0:T(8,128)(2,1)} %get-tuple-element.37), kind=kLoop, calls=%fused_computation | loop fusion | flops 4194304 | bytes 6291456 | tf_op jit(solution)/shard_map/convert_element_type | solution.py:490
  72.4 6.6 %all-to-all-start.2 = ((bf16[8,528,128]{2,1,0:T(8,128)(2,1)}), bf16[8,528,128]{2,1,0:T(8,128)(2,1)S(1)}, u32[]{:S(2)}, u32[]{:S(2)}) async-start(bf16[8,528,128]{2,1,0:T(8,128)(2,1)} %get-tuple-element.28), calls=%async_computation.2 | async-start | bytes 2162688 | tf_op jit(solution)/shard_map/all_to_all | solution.py:487
  81.2 11.0 %all-to-all-done.2.pieces = bf16[8,528,128]{2,1,0:T(8,128)(2,1)S(1)} async-done(((bf16[8,528,128]{2,1,0:T(8,128)(2,1)}), bf16[8,528,128]{2,1,0:T(8,128)(2,1)S(1)}, u32[]{:S(2)}, u32[]{:S(2)}) %all-to-all-start.2) | async-done | bytes 1081376 | tf_op jit(solution)/shard_map/all_to_all | solution.py:487
  92.2 3.4 %shard_map.172 = (f32[16,64,128]{2,1,0:T(8,128)S(1)}, f32[32,8,128]{2,1,0:T(8,128)}) custom-call(bf16[8,528,128]{2,1,0:T(8,128)(2,1)S(1)} %all-to-all-done.2.pieces, bf16[16,64,128]{2,1,0:T(8,128)(2,1)S(1)} %bitcast.85, f32[16,64,128]{2,1,0:T(8,128)S(1)} %get-tuple-element.24.filtered, f32[4,128]{1,0:T(4,128)S(1)} %pad_maximum_fusion.1.rows, ...), custom_call_target="tpu_custom_call" | custom-call | flops 536870912 | bytes 8388608 | tf_op jit(solution)/shard_map/pallas_call | solution.py:246
  95.6 6.1 %all-to-all-start.3 = ((f32[32,8,128]{2,1,0:T(8,128)}), f32[32,8,128]{2,1,0:T(8,128)S(1)}, u32[]{:S(2)}, u32[]{:S(2)}) async-start(f32[32,8,128]{2,1,0:T(8,128)} %get-tuple-element.36), calls=%async_computation.3 | async-start | bytes 262144 | tf_op jit(solution)/shard_map/all_to_all | solution.py:514
  101.8 1.2 dynamic-slice_bitcast_fusion.2
  103.0 3.2 %collective-permute-start.4 = (bf16[2,512,128]{2,1,0:T(8,128)(2,1)S(1)}, bf16[2,512,128]{2,1,0:T(8,128)(2,1)S(1)}, u32[]{:S(2)}, u32[]{:S(2)}) collective-permute-start(bf16[2,512,128]{2,1,0:T(8,128)(2,1)S(1)} %get-tuple-element.49), channel_id=1, source_target_pairs={{0,4},{2,6},{4,0},{6,2},{1,5},{3,7},{5,1},{7,3},{8,12},{10,14},{12... | collective-permute-start | bytes 786440 | tf_op jit(solution)/shard_map/ppermute | solution.py:37
  106.2 1.2 collective-permute-start.5
  108.2 5.9 %all-to-all-done.3 = f32[32,8,128]{2,1,0:T(8,128)S(1)} async-done(((f32[32,8,128]{2,1,0:T(8,128)}), f32[32,8,128]{2,1,0:T(8,128)S(1)}, u32[]{:S(2)}, u32[]{:S(2)}) %all-to-all-start.3) | async-done | bytes 131104 | tf_op jit(solution)/shard_map/all_to_all | solution.py:514
  115.2 3.9 %all-to-all-start.4 = ((f32[32,2,128]{2,1,0:T(2,128)}), f32[32,2,128]{2,1,0:T(2,128)S(1)}, u32[]{:S(2)}, u32[]{:S(2)}) async-start(f32[32,2,128]{2,1,0:T(2,128)} %broadcast_in_dim.26), calls=%async_computation.4 | async-start | bytes 65536 | tf_op jit(solution)/shard_map/all_to_all | solution.py:19
  119.2 3.5 %shard_map.173 = bf16[16,64,128]{2,1,0:T(8,128)(2,1)} custom-call(f32[16,64,128]{2,1,0:T(8,128)S(1)} %get-tuple-element.35.d_normed, f32[16,64,128]{2,1,0:T(8,128)S(1)} %get-tuple-element.24.filtered, bf16[16,64,128]{2,1,0:T(8,128)(2,1)S(1)} %bitcast.87, f32[49,128]{1,0:T(8,128)S(1)} %copy-done.3, f32[5,128]{1,0:T(8,128)S(1)} %stack.5.rows), custom_call_target="tpu_custom_call" | custom-call | flops 536870912 | bytes 8388608 | tf_op jit(solution)/shard_map/pallas_call | solution.py:246
  123.9 5.1 %all-to-all-done.4 = f32[32,2,128]{2,1,0:T(2,128)S(1)} async-done(((f32[32,2,128]{2,1,0:T(2,128)}), f32[32,2,128]{2,1,0:T(2,128)S(1)}, u32[]{:S(2)}, u32[]{:S(2)}) %all-to-all-start.4) | async-done | bytes 32800 | tf_op jit(solution)/shard_map/all_to_all | solution.py:19
  132.3 2.7 %collective-permute-start.11 = (bf16[32,1024]{1,0:T(8,128)(2,1)S(1)}, bf16[32,1024]{1,0:T(8,128)(2,1)S(1)}, u32[]{:S(2)}, u32[]{:S(2)}) collective-permute-start(bf16[32,1024]{1,0:T(8,128)(2,1)S(1)} %get-tuple-element.55), channel_id=1, source_target_pairs={{0,24},{8,0},{16,8},{24,16},{1,25},{9,1},{17,9},{25,17},{2,26},{10... | collective-permute-start | bytes 196616 | tf_op jit(solution)/shard_map/ppermute | solution.py:37
  135.9 1.4 collective-permute-done.10
  137.5 3.3 %collective-permute-done.9 = bf16[32,1024]{1,0:T(8,128)(2,1)S(1)} collective-permute-done((bf16[32,1024]{1,0:T(8,128)(2,1)S(1)}, bf16[32,1024]{1,0:T(8,128)(2,1)S(1)}, u32[]{:S(2)}, u32[]{:S(2)}) %collective-permute-start.9) | collective-permute-done | bytes 65568 | tf_op jit(solution)/shard_map/ppermute | solution.py:37
  (84 shorter events, 15.4 us)
Async XLA Ops:
  7.2 16.7 %copy-start.10 = (s32[4]{0:T(128)S(1)}, s32[4]{0:T(128)}, u32[]{:S(2)}) copy-start(s32[4]{0:T(128)} %param.19) | copy-start | bytes 52
  7.2 26.0 %copy-start.5 = (f32[4,128]{1,0:T(4,128)S(1)}, f32[4,128]{1,0:T(4,128)}, u32[]{:S(2)}) copy-start(f32[4,128]{1,0:T(4,128)} %param.13) | copy-start | bytes 6148
  7.2 26.0 %copy-start.8 = (f32[4,128]{1,0:T(4,128)S(1)}, f32[4,128]{1,0:T(4,128)}, u32[]{:S(2)}) copy-start(f32[4,128]{1,0:T(4,128)} %param.14) | copy-start | bytes 6148
  7.2 45.0 %all-gather.2.cloned.1.call-start = ((), (), s32[]{:S(2)}) async-start(), calls=%async_computation.6 | async-start | bytes 2359296 | tf_op jit(solution)/shard_map/all_gather | solution.py:458
  11.8 21.4 %all-to-all-start = ((f32[32,2,128]{2,1,0:T(2,128)}), f32[32,2,128]{2,1,0:T(2,128)S(1)}, u32[]{:S(2)}, u32[]{:S(2)}) async-start(f32[32,2,128]{2,1,0:T(2,128)} %get-tuple-element.25), calls=%async_computation | async-start | bytes 65536 | tf_op jit(solution)/shard_map/all_to_all | solution.py:459
  23.3 29.0 %collective-permute-start = (bf16[1024,512]{1,0:T(8,128)(2,1)S(1)}, bf16[1024,512]{1,0:T(8,128)(2,1)}, u32[]{:S(2)}, u32[]{:S(2)}) collective-permute-start(bf16[1024,512]{1,0:T(8,128)(2,1)S(1)} %copy-done.1), channel_id=1, source_target_pairs={{0,1},{1,0},{2,3},{3,2},{4,5},{5,4},{6,7},{7,6},{8,9},{9,8},{10,11... | collective-permute-start | bytes 3145736 | tf_op jit(solution)/shard_map/ppermute | solution.py:438
  23.4 28.9 %collective-permute-start.2 = (bf16[512,1024]{1,0:T(8,128)(2,1)}, bf16[512,1024]{1,0:T(8,128)(2,1)}, u32[]{:S(2)}, u32[]{:S(2)}) collective-permute-start(bf16[512,1024]{1,0:T(8,128)(2,1)} %refs_7_.1), channel_id=1, source_target_pairs={{0,1},{1,0},{2,3},{3,2},{4,5},{5,4},{6,7},{7,6},{8,9},{9,8},{10,11... | collective-permute-start | bytes 3145736 | tf_op jit(solution)/shard_map/ppermute | solution.py:439
  34.6 17.6 %all-to-all-start.1 = ((bf16[8,512,128]{2,1,0:T(8,128)(2,1)}), bf16[8,512,128]{2,1,0:T(8,128)(2,1)S(1)}, u32[]{:S(2)}, u32[]{:S(2)}) async-start(bf16[8,512,128]{2,1,0:T(8,128)(2,1)} %bitcast.90), calls=%async_computation.1 | async-start | bytes 2097152 | tf_op jit(solution)/shard_map/all_to_all | solution.py:27
  39.4 91.3 %reduce-scatter.2.cloned.1.call-start = ((), (), s32[]{:S(2)}) async-start(), calls=%async_computation.7 | async-start | bytes 2359296 | tf_op jit(solution)/shard_map/reduce_scatter | solution.py:493
  39.4 12.8 %collective-permute-start.1 = (f32[512]{0:T(512)S(1)}, f32[512]{0:T(512)S(1)}, u32[]{:S(2)}, u32[]{:S(2)}) collective-permute-start(f32[512]{0:T(512)S(1)} %copy-done.4), channel_id=1, source_target_pairs={{0,1},{1,0},{2,3},{3,2},{4,5},{5,4},{6,7},{7,6},{8,9},{9,8},{10,11... | collective-permute-start | bytes 6152 | tf_op jit(solution)/shard_map/ppermute | solution.py:440
  64.0 4.5 %collective-permute-start.8 = (bf16[1024,1024]{1,0:T(8,128)(2,1)}, bf16[1024,1024]{1,0:T(8,128)(2,1)S(1)}, u32[]{:S(2)}, u32[]{:S(2)}) collective-permute-start(bf16[1024,1024]{1,0:T(8,128)(2,1)} %get-tuple-element.38), channel_id=1, source_target_pairs={{0,1},{1,0},{2,3},{3,2},{4,5},{5,4},{6,7},{7,6},{8,9},{9,8},{10,11... | collective-permute-start | bytes 6291464 | tf_op jit(solution)/shard_map/ppermute | solution.py:488
  72.4 19.8 %all-to-all-start.2 = ((bf16[8,528,128]{2,1,0:T(8,128)(2,1)}), bf16[8,528,128]{2,1,0:T(8,128)(2,1)S(1)}, u32[]{:S(2)}, u32[]{:S(2)}) async-start(bf16[8,528,128]{2,1,0:T(8,128)(2,1)} %get-tuple-element.28), calls=%async_computation.2 | async-start | bytes 2162688 | tf_op jit(solution)/shard_map/all_to_all | solution.py:487
  79.7 1.4 collective-permute-start.3
  81.1 38.0 %copy-start.2 = (bf16[1,16,64,128]{3,2,1,0:T(8,128)(2,1)S(1)}, bf16[1,16,64,128]{3,2,1,0:T(8,128)(2,1)}, u32[]{:S(2)}) copy-start(bf16[1,16,64,128]{3,2,1,0:T(8,128)(2,1)} %param.11) | copy-start | bytes 786436
  81.2 38.0 %copy-start.3 = (f32[49,128]{1,0:T(8,128)S(1)}, f32[49,128]{1,0:T(8,128)}, u32[]{:S(2)}) copy-start(f32[49,128]{1,0:T(8,128)} %kernel.1) | copy-start | bytes 75268
  95.6 18.6 %all-to-all-start.3 = ((f32[32,8,128]{2,1,0:T(8,128)}), f32[32,8,128]{2,1,0:T(8,128)S(1)}, u32[]{:S(2)}, u32[]{:S(2)}) async-start(f32[32,8,128]{2,1,0:T(8,128)} %get-tuple-element.36), calls=%async_computation.3 | async-start | bytes 262144 | tf_op jit(solution)/shard_map/all_to_all | solution.py:514
  103.0 19.6 %collective-permute-start.4 = (bf16[2,512,128]{2,1,0:T(8,128)(2,1)S(1)}, bf16[2,512,128]{2,1,0:T(8,128)(2,1)S(1)}, u32[]{:S(2)}, u32[]{:S(2)}) collective-permute-start(bf16[2,512,128]{2,1,0:T(8,128)(2,1)S(1)} %get-tuple-element.49), channel_id=1, source_target_pairs={{0,4},{2,6},{4,0},{6,2},{1,5},{3,7},{5,1},{7,3},{8,12},{10,14},{12... | collective-permute-start | bytes 786440 | tf_op jit(solution)/shard_map/ppermute | solution.py:37
  106.2 16.4 %collective-permute-start.5 = (bf16[2,512,128]{2,1,0:T(8,128)(2,1)S(1)}, bf16[2,512,128]{2,1,0:T(8,128)(2,1)S(1)}, u32[]{:S(2)}, u32[]{:S(2)}) collective-permute-start(bf16[2,512,128]{2,1,0:T(8,128)(2,1)S(1)} %get-tuple-element.51), channel_id=1, source_target_pairs={{0,2},{2,4},{4,6},{6,0},{1,3},{3,5},{5,7},{7,1},{8,10},{10,12},{12... | collective-permute-start | bytes 786440 | tf_op jit(solution)/shard_map/ppermute | solution.py:37
  107.4 15.3 %collective-permute-start.6 = (bf16[2,512,128]{2,1,0:T(8,128)(2,1)S(1)}, bf16[2,512,128]{2,1,0:T(8,128)(2,1)S(1)}, u32[]{:S(2)}, u32[]{:S(2)}) collective-permute-start(bf16[2,512,128]{2,1,0:T(8,128)(2,1)S(1)} %get-tuple-element.50), channel_id=1, source_target_pairs={{0,6},{2,0},{4,2},{6,4},{1,7},{3,1},{5,3},{7,5},{8,14},{10,8},{12,... | collective-permute-start | bytes 786440 | tf_op jit(solution)/shard_map/ppermute | solution.py:37
  115.2 13.7 %all-to-all-start.4 = ((f32[32,2,128]{2,1,0:T(2,128)}), f32[32,2,128]{2,1,0:T(2,128)S(1)}, u32[]{:S(2)}, u32[]{:S(2)}) async-start(f32[32,2,128]{2,1,0:T(2,128)} %broadcast_in_dim.26), calls=%async_computation.4 | async-start | bytes 65536 | tf_op jit(solution)/shard_map/all_to_all | solution.py:19
  123.8 6.9 %collective-permute-start.7 = (bf16[512,128]{1,0:T(8,128)(2,1)S(1)}, bf16[512,128]{1,0:T(8,128)(2,1)S(1)}, u32[]{:S(2)}, u32[]{:S(2)}) collective-permute-start(bf16[512,128]{1,0:T(8,128)(2,1)S(1)} %dynamic-slice_bitcast_fusion.3), channel_id=1, source_target_pairs={{0,1},{1,0},{2,3},{3,2},{4,5},{5,4},{6,7},{7,6},{8,9},{9,8},{10,11... | collective-permute-start | bytes 393224 | tf_op jit(solution)/shard_map/ppermute | solution.py:519
  131.7 5.6 %collective-permute-start.10 = (bf16[32,1024]{1,0:T(8,128)(2,1)S(1)}, bf16[32,1024]{1,0:T(8,128)(2,1)S(1)}, u32[]{:S(2)}, u32[]{:S(2)}) collective-permute-start(bf16[32,1024]{1,0:T(8,128)(2,1)S(1)} %get-tuple-element.56), channel_id=1, source_target_pairs={{0,8},{8,16},{16,24},{24,0},{1,9},{9,17},{17,25},{25,1},{2,10},{10... | collective-permute-start | bytes 196616 | tf_op jit(solution)/shard_map/ppermute | solution.py:37
  132.3 5.2 %collective-permute-start.11 = (bf16[32,1024]{1,0:T(8,128)(2,1)S(1)}, bf16[32,1024]{1,0:T(8,128)(2,1)S(1)}, u32[]{:S(2)}, u32[]{:S(2)}) collective-permute-start(bf16[32,1024]{1,0:T(8,128)(2,1)S(1)} %get-tuple-element.55), channel_id=1, source_target_pairs={{0,24},{8,0},{16,8},{24,16},{1,25},{9,1},{17,9},{25,17},{2,26},{10... | collective-permute-start | bytes 196616 | tf_op jit(solution)/shard_map/ppermute | solution.py:37
  135.0 5.8 %collective-permute-start.9 = (bf16[32,1024]{1,0:T(8,128)(2,1)S(1)}, bf16[32,1024]{1,0:T(8,128)(2,1)S(1)}, u32[]{:S(2)}, u32[]{:S(2)}) collective-permute-start(bf16[32,1024]{1,0:T(8,128)(2,1)S(1)} %get-tuple-element.54), channel_id=1, source_target_pairs={{0,16},{8,24},{16,0},{24,8},{1,17},{9,25},{17,1},{25,9},{2,18},{10... | collective-permute-start | bytes 196616 | tf_op jit(solution)/shard_map/ppermute | solution.py:37
  (6 other events, 69.6 us)
Sparse Core Ops, SparseCore 0:
  11.9 29.8 all-gather.1
  72.5 43.4 reduce-scatter.1
